TPU v7x, 32 devices: a whole 2x2x4 slice. The times are simulated.
32 devices in a mesh: dp: 4 (over x, core), graph: 8 (over z, y).
Axes of the slice: x: 2, y: 2, z: 4, core: 2. Of those that a mesh axis runs over, the one named last changes fastest.
Arguments:
- node_feats: bfloat16 [4, 128, 3712], P('dp', 'graph'), may hold values from -6 to 6
- node_cotan: bfloat16 [4, 128, 3712], P('dp', 'graph'), may hold values from -6 to 6
- source: int32 [4, 2560], P('dp', 'graph'), may hold values from 0 to 127, as said below
- target: int32 [4, 2560], P('dp', 'graph'), may hold values from 0 to 127, as said below
- angle: float32 [4, 2560], P('dp', 'graph'), may hold values from -3.140625 to 3.140625
- w_zero: bfloat16 [896, 896], replicated, may hold values from -0.1875 to 0.1875
- w_one: bfloat16 [768, 1536], replicated, may hold values from -0.21875 to 0.21875
- w_two: bfloat16 [640, 1280], replicated, may hold values from -0.25 to 0.25
Outputs:
- grad_nodes: bfloat16 [4, 128, 3712], P('dp', 'graph')
- grad_zero: float32 [896, 896], P('graph')
- grad_one: float32 [768, 1536], P('graph')
- grad_two: float32 [640, 1280], P('graph')
Inputs may be any that keep to these rules, and one draw needn't show every extreme that they name: `source`: the edges at positions d * 320 to (d + 1) * 320 - 1 of a batch have both ends among atoms d * 16 - 8 to (d + 1) * 16 + 7; the first and the last of these atoms that lie in the batch are named on every device; no edge joins an atom to itself. `target`: as for source, with the same ranges per device.
All inputs are finite; a program needn't handle non-finite values.
Results may differ from a plain program's by a relative error of at most 0.0015.
The roundings to bfloat16 on the way count: a program that leaves them out, or rounds other values in their place, can miss the bound.
Values may be sent and summed in bfloat16 or wider, within the bound.
No kernel may reach another device: no remote copies, remote signals or barrier semaphores. Data moves between devices by JAX's collectives and lax.ppermute only.
A program may use at most 128 MiB of HBM per device.

v0:
```python
import jax
import jax.numpy as jnp
from jax import lax
from jax.sharding import PartitionSpec as P

HEADS = 8


def padded_2(cells, sides, width):
    for axis, dim in sides:
        count = lax.axis_size(axis)
        ends = count - 1
        head = lax.slice_in_dim(cells, 0, width, axis=dim)
        tail = lax.slice_in_dim(cells, cells.shape[dim] - width, cells.shape[dim], axis=dim)
        cells = jnp.concatenate(
            [
                lax.ppermute(tail, axis, [(i, (i + 1) % count) for i in range(ends)]),
                cells,
                lax.ppermute(head, axis, [((i + 1) % count, i) for i in range(ends)]),
            ],
            axis=dim,
        )
    return cells


def shifted(block, axis, distance):
    devices = range(lax.axis_size(axis))
    route = [(i - distance, i) for i in devices if i - distance in devices]
    return lax.ppermute(block, axis, route)


def contract_rows(first, second):
    return lax.dot_general(
        first, second, (((0,), (0,)), ((), ())), preferred_element_type=jnp.float32
    )


def contract_cols(first, weight):
    return lax.dot_general(
        first, weight, (((1,), (1,)), ((), ())), preferred_element_type=jnp.float32
    )


def rotate(first, second, cosine, sine):
    return (cosine * first - sine * second, sine * first + cosine * second)


def per_head(block, channels, heads):
    return block.reshape(block.shape[0], -1, heads, channels // heads)


def edge_terms(feats, cotan, phases, w_zero, w_one, w_two, channels, heads):
    count = feats.shape[0]
    bounds = [0, 7 * channels, 13 * channels, 19 * channels, 24 * channels, 29 * channels]
    cos_one = jnp.cos(phases)[:, None]
    sin_one = jnp.sin(phases)[:, None]
    cos_two = jnp.cos(2.0 * phases)[:, None]
    sin_two = jnp.sin(2.0 * phases)[:, None]
    zero_in = feats[:, : bounds[1]]
    pieces = [feats[:, bounds[k] : bounds[k + 1]].astype(jnp.float32) for k in range(1, 5)]
    rot_p1, rot_n1 = rotate(pieces[0], pieces[1], cos_one, sin_one)
    rot_p2, rot_n2 = rotate(pieces[2], pieces[3], cos_two, sin_two)
    stack_one = jnp.concatenate([rot_p1.astype(jnp.bfloat16), rot_n1.astype(jnp.bfloat16)], 0)
    stack_two = jnp.concatenate([rot_p2.astype(jnp.bfloat16), rot_n2.astype(jnp.bfloat16)], 0)
    zero_out = jnp.dot(zero_in, w_zero, preferred_element_type=jnp.float32)
    prod_one = jnp.dot(stack_one, w_one, preferred_element_type=jnp.float32)
    prod_two = jnp.dot(stack_two, w_two, preferred_element_type=jnp.float32)
    half_one = 6 * channels
    half_two = 5 * channels
    out_p1 = prod_one[:count, :half_one] - prod_one[count:, half_one:]
    out_n1 = prod_one[:count, half_one:] + prod_one[count:, :half_one]
    out_p2 = prod_two[:count, :half_two] - prod_two[count:, half_two:]
    out_n2 = prod_two[:count, half_two:] + prod_two[count:, :half_two]
    scale = 1.0 / jnp.sqrt(jnp.float32(channels // heads))
    logits = per_head(zero_out[:, :channels], channels, heads).sum(axis=(1, 3)) * scale
    gate = jax.nn.sigmoid(logits)
    grads_in = [cotan[:, bounds[k] : bounds[k + 1]].astype(jnp.float32) for k in range(5)]
    du_zero = grads_in[0]
    du_p1, du_n1 = rotate(grads_in[1], grads_in[2], cos_one, sin_one)
    du_p2, du_n2 = rotate(grads_in[3], grads_in[4], cos_two, sin_two)
    dgate = jnp.zeros((count, heads), jnp.float32)
    for upstream, forward in (
        (du_zero, zero_out),
        (du_p1, out_p1),
        (du_n1, out_n1),
        (du_p2, out_p2),
        (du_n2, out_n2),
    ):
        dgate = dgate + per_head(upstream * forward, channels, heads).sum(axis=(1, 3))
    dlogit = dgate * gate * (1.0 - gate) * scale

    def gated(block):
        shaped = per_head(block, channels, heads) * gate[:, None, :, None]
        return shaped.reshape(count, -1)

    dz_zero = gated(du_zero)
    dz_zero = jnp.concatenate(
        [
            dz_zero[:, :channels] + jnp.repeat(dlogit, channels // heads, axis=1),
            dz_zero[:, channels:],
        ],
        1,
    )
    dz_zero = dz_zero.astype(jnp.bfloat16)
    dz_p1, dz_n1, dz_p2, dz_n2 = (gated(du_p1), gated(du_n1), gated(du_p2), gated(du_n2))
    grad_one = jnp.concatenate(
        [jnp.concatenate([dz_p1, dz_n1], 1), jnp.concatenate([dz_n1, -dz_p1], 1)], 0
    ).astype(jnp.bfloat16)
    grad_two = jnp.concatenate(
        [jnp.concatenate([dz_p2, dz_n2], 1), jnp.concatenate([dz_n2, -dz_p2], 1)], 0
    ).astype(jnp.bfloat16)
    back_zero = contract_cols(dz_zero, w_zero)
    back_one = contract_cols(grad_one, w_one)
    back_two = contract_cols(grad_two, w_two)
    dp_one, dn_one = rotate(back_one[:count], back_one[count:], cos_one, -sin_one)
    dp_two, dn_two = rotate(back_two[:count], back_two[count:], cos_two, -sin_two)
    node_terms = jnp.concatenate([back_zero, dp_one, dn_one, dp_two, dn_two], 1)
    return (node_terms, (zero_in, dz_zero), (stack_one, grad_one), (stack_two, grad_two))


def weight_term(operands):
    inputs, upstream = operands
    return contract_rows(inputs, upstream)


def shards(node_feats, node_cotan, source, target, angle, w_zero, w_one, w_two):
    atom_count = node_feats.shape[1]
    row_width = node_feats.shape[2]
    channels = row_width // 29
    position = lax.axis_index("graph")
    reach = atom_count // 2
    stacked = jnp.stack([node_feats[0], node_cotan[0]], 0)
    padded = padded_2(stacked, (("graph", 1),), reach)
    feat_table = padded[0]
    cotan_table = padded[1]
    first_atom = position * atom_count - reach
    src_local = source[0] - first_atom
    dst_local = target[0] - first_atom
    node_terms, pair_zero, pair_one, pair_two = edge_terms(
        feat_table[src_local],
        cotan_table[dst_local],
        angle[0],
        w_zero,
        w_one,
        w_two,
        channels,
        HEADS,
    )
    collected = (
        jnp.zeros((atom_count + 2 * reach, row_width), jnp.float32).at[src_local].add(node_terms)
    )
    from_next = shifted(collected[:reach], "graph", -1)
    from_prev = shifted(collected[atom_count + reach :], "graph", 1)
    own_rows = collected[reach : reach + atom_count]
    own_rows = own_rows + jnp.pad(from_prev, ((0, atom_count - reach), (0, 0)))
    own_rows = own_rows + jnp.pad(from_next, ((atom_count - reach, 0), (0, 0)))
    grad_nodes = own_rows.astype(jnp.bfloat16)[None]
    part_zero = lax.psum_scatter(weight_term(pair_zero), "graph", scatter_dimension=0, tiled=True)
    part_one = lax.psum_scatter(weight_term(pair_one), "graph", scatter_dimension=0, tiled=True)
    part_two = lax.psum_scatter(weight_term(pair_two), "graph", scatter_dimension=0, tiled=True)
    totals = lax.psum((part_zero, part_one, part_two), "dp")
    batches = lax.axis_size("dp")
    return (grad_nodes, totals[0] / batches, totals[1] / batches, totals[2] / batches)


def solution(mesh):
    return jax.shard_map(
        shards,
        mesh=mesh,
        in_specs=(
            P("dp", "graph", None),
            P("dp", "graph", None),
            P("dp", "graph"),
            P("dp", "graph"),
            P("dp", "graph"),
            P(),
            P(),
            P(),
        ),
        out_specs=(P("dp", "graph", None), P("graph", None), P("graph", None), P("graph", None)),
        check_vma=False,
    )
```

profile of v0, /device:TPU:0, one launch (start us, length us, event | category | flops | bytes accessed | tf_op | source)
XLA Modules:
  0.0 395.5 jit_solution(7562235290491583224)
XLA Ops:
  9.2 4.9 %collective-permute-start = (bf16[2,8,3712]{2,1,0:T(8,128)(2,1)S(1)}, bf16[2,8,3712]{2,1,0:T(8,128)(2,1)S(1)}, u32[]{:S(2)}, u32[]{:S(2)}) collective-permute-start(bf16[2,8,3712]{2,1,0:T(8,128)(2,1)S(1)} %get-tuple-element.35), channel_id=1, source_target_pairs={{0,1},{1,2},{2,3},{3,4},{4,5},{5,6},{6,7},{8,9},{9,10},{10,11},{11... | collective-permute-start | bytes 356360 | tf_op jit(solution)/shard_map/ppermute | solution.py:17
  17.0 3.8 collective-permute-done.1
  21.0 3.9 gather_fusion.1
  24.8 2.4 fusion.25
  29.5 2.5 copy.22
  33.1 2.6 copy.20
  36.9 2.8 copy.13
  39.7 3.8 gather_fusion
  43.5 3.0 convert_multiply_fusion
  46.5 1.6 copy.14
  48.1 2.2 slice.248
  54.1 3.3 fusion.44
  58.8 2.0 reduce_sum.55
  63.7 1.6 fusion.3
  66.2 1.7 fusion.19
  67.9 3.6 fusion.45
  71.6 1.6 copy.16
  73.8 1.6 copy.15
  78.0 4.0 %fusion.23 = f32[896,896]{1,0:T(8,128)} fusion(bf16[320,3712]{1,0:T(8,128)(2,1)} %gather_fusion.1, bf16[320,768]{1,0:T(8,128)(2,1)} %slice.248, bf16[320,128]{1,0:T(8,128)(2,1)S(1)} %fusion.32), kind=kOutput, calls=%fused_computation.63 | convolution fusion | flops 514949120 | bytes 4358144 | tf_op jit(solution)/shard_map/dot_general | solution.py:33
  83.1 4.5 %fusion.21 = f32[640,1280]{1,0:T(8,128)} fusion(bf16[320,640]{1,0:T(8,128)(2,1)S(1)} %copy-done.14, bf16[320,640]{1,0:T(8,128)(2,1)S(1)} %copy-done.12, bf16[320,640]{1,0:T(8,128)(2,1)} %get-tuple-element.19, bf16[320,640]{1,0:T(8,128)(2,1)} %get-tuple-element.20, bf16[320,640]{1,0:T(8,128)(2,1)} %get-tuple-element.18), kind=kOutput, calls=%fused_computation.61 | convolution fusion | flops 1056768000 | bytes 5324800 | tf_op jit(solution)/shard_map/dot_general | solution.py:33
  88.8 5.7 %fusion.18 = f32[768,1536]{1,0:T(8,128)} fusion(bf16[320,768]{1,0:T(8,128)(2,1)} %copy-done.10, bf16[320,768]{1,0:T(8,128)(2,1)} %copy-done.9, bf16[320,768]{1,0:T(8,128)(2,1)S(1)} %copy-done.6, bf16[320,768]{1,0:T(8,128)(2,1)} %get-tuple-element.17, bf16[320,768]{1,0:T(8,128)(2,1)S(1)} %copy-done.5), kind=kOutput, calls=%fused_computation.57 | convolution fusion | flops 1519779840 | bytes 7176192 | tf_op jit(solution)/shard_map/dot_general | solution.py:33
  95.5 3.3 convolution_dynamic-update-slice_fusion
  98.8 1.7 fusion.20
  106.7 8.7 %scatter_custom_fusion = f32[32,3712]{1,0:T(8,128)S(1)} fusion(s32[320]{0:T(512)} %copy-done.24, f32[320,3712]{1,0:T(8,128)} %add_dynamic-update-slice_fusion.1, f32[]{:T(128)} %constant.9.clone.1), kind=kCustom, calls=%fused_computation.75 | custom fusion | flops 1187840 | bytes 475648 | tf_op jit(solution)/shard_map/scatter-add | solution.py:150
  115.4 4.4 %collective-permute-start.2 = (f32[8,3712]{1,0:T(8,128)S(1)}, f32[8,3712]{1,0:T(8,128)S(1)}, u32[]{:S(2)}, u32[]{:S(2)}) collective-permute-start(f32[8,3712]{1,0:T(8,128)S(1)} %get-tuple-element.31), channel_id=1, source_target_pairs={{0,1},{1,2},{2,3},{3,4},{4,5},{5,6},{6,7},{8,9},{9,10},{10,11},{11... | collective-permute-start | bytes 356360 | tf_op jit(solution)/shard_map/ppermute | solution.py:29
  121.2 42.4 %reduce-scatter.4.cloned.1.call-done = f32[112,896]{1,0:T(8,128)} async-done(((f32[896,896]{1,0:T(8,128)}), f32[112,896]{1,0:T(8,128)}) %reduce-scatter.4.cloned.1.call-update) | async-done | bytes 401424 | tf_op jit(solution)/shard_map/reduce_scatter | solution.py:158
  163.6 78.9 %reduce-scatter.8.cloned.1.call-done = f32[80,1280]{1,0:T(8,128)} async-done(((f32[640,1280]{1,0:T(8,128)}), f32[80,1280]{1,0:T(8,128)}) %reduce-scatter.8.cloned.1.call-update) | async-done | bytes 409616 | tf_op jit(solution)/shard_map/reduce_scatter | solution.py:160
  242.6 98.3 %reduce-scatter.6.cloned.1.call-done = f32[96,1536]{1,0:T(8,128)} async-done(((f32[768,1536]{1,0:T(8,128)}), f32[96,1536]{1,0:T(8,128)}) %reduce-scatter.6.cloned.1.call-update) | async-done | bytes 589840 | tf_op jit(solution)/shard_map/reduce_scatter | solution.py:159
  341.6 41.9 %all-reduce.5.cloned.1.call-done = (f32[112,896]{1,0:T(8,128)}, f32[96,1536]{1,0:T(8,128)}, f32[80,1280]{1,0:T(8,128)}) async-done(((f32[112,896]{1,0:T(8,128)}, f32[96,1536]{1,0:T(8,128)}, f32[80,1280]{1,0:T(8,128)}), (f32[112,896]{1,0:T(8,128)}, f32[96,1536]{1,0:T(8,128)}, f32[80,1280]{1,0:T(8,128)})) %all-reduce.5.cloned.1.call-update) | async-done | bytes 1400848 | tf_op jit(solution)/shard_map/psum | solution.py:161
  383.5 1.8 broadcast_multiply_fusion.2
  385.3 1.8 broadcast_multiply_fusion.1
  387.1 1.9 broadcast_multiply_fusion
  (104 shorter events, 33.2 us)
Async XLA Ops:
  7.2 59.1 %copy-start = (bf16[768,1536]{1,0:T(8,128)(2,1)S(1)}, bf16[768,1536]{1,0:T(8,128)(2,1)}, u32[]{:S(2)}) copy-start(bf16[768,1536]{1,0:T(8,128)(2,1)} %param.14) | copy-start | bytes 7077892
  7.2 156.5 %reduce-scatter.4.cloned.1.call-start = ((), (), s32[]{:S(2)}) async-start(), calls=%async_computation.3 | async-start | bytes 3612672 | tf_op jit(solution)/shard_map/reduce_scatter | solution.py:158
  9.2 7.8 %collective-permute-start = (bf16[2,8,3712]{2,1,0:T(8,128)(2,1)S(1)}, bf16[2,8,3712]{2,1,0:T(8,128)(2,1)S(1)}, u32[]{:S(2)}, u32[]{:S(2)}) collective-permute-start(bf16[2,8,3712]{2,1,0:T(8,128)(2,1)S(1)} %get-tuple-element.35), channel_id=1, source_target_pairs={{0,1},{1,2},{2,3},{3,4},{4,5},{5,6},{6,7},{8,9},{9,10},{10,11},{11... | collective-permute-start | bytes 356360 | tf_op jit(solution)/shard_map/ppermute | solution.py:17
  14.1 6.7 %collective-permute-start.1 = (bf16[2,8,3712]{2,1,0:T(8,128)(2,1)S(1)}, bf16[2,8,3712]{2,1,0:T(8,128)(2,1)S(1)}, u32[]{:S(2)}, u32[]{:S(2)}) collective-permute-start(bf16[2,8,3712]{2,1,0:T(8,128)(2,1)S(1)} %get-tuple-element.36), channel_id=1, source_target_pairs={{1,0},{2,1},{3,2},{4,3},{5,4},{6,5},{7,6},{9,8},{10,9},{11,10},{12... | collective-permute-start | bytes 356360 | tf_op jit(solution)/shard_map/ppermute | solution.py:19
  16.2 8.7 %copy-start.24 = (s32[320]{0:T(512)}, s32[320]{0:T(512)S(1)}, u32[]{:S(2)}) copy-start(s32[320]{0:T(512)S(1)} %get-tuple-element.37) | copy-start | bytes 3844
  17.0 37.0 %copy-start.20 = (f32[320]{0:T(512)}, f32[320]{0:T(512)S(1)}, u32[]{:S(2)}) copy-start(f32[320]{0:T(512)S(1)} %get-tuple-element.5) | copy-start | bytes 3844
  17.0 50.9 %copy-start.18 = (f32[320]{0:T(512)}, f32[320]{0:T(512)S(1)}, u32[]{:S(2)}) copy-start(f32[320]{0:T(512)S(1)} %get-tuple-element.4) | copy-start | bytes 3844
  17.0 50.9 %copy-start.22 = (f32[320]{0:T(512)}, f32[320]{0:T(512)S(1)}, u32[]{:S(2)}) copy-start(f32[320]{0:T(512)S(1)} %get-tuple-element.7) | copy-start | bytes 3844
  27.2 1.0 copy-start.4
  48.1 4.5 %copy-start.25 = (bf16[640,1280]{1,0:T(8,128)(2,1)S(1)}, bf16[640,1280]{1,0:T(8,128)(2,1)}, u32[]{:S(2)}) copy-start(bf16[640,1280]{1,0:T(8,128)(2,1)} %param.15) | copy-start | bytes 4915204
  51.7 0.9 copy-start.13
  52.6 1.5 copy-start.2
  65.2 0.8 copy-start.9
  65.3 1.0 copy-start.10
  66.2 1.7 copy-start.1
  81.9 1.0 copy-start.12
  81.9 1.1 copy-start.14
  82.0 160.6 %reduce-scatter.8.cloned.1.call-start = ((), (), s32[]{:S(2)}) async-start(), calls=%async_computation.5 | async-start | bytes 3686400 | tf_op jit(solution)/shard_map/reduce_scatter | solution.py:160
  87.6 1.0 copy-start.5
  87.6 1.2 copy-start.6
  87.6 253.3 %reduce-scatter.6.cloned.1.call-start = ((), (), s32[]{:S(2)}) async-start(), calls=%async_computation.4 | async-start | bytes 5308416 | tf_op jit(solution)/shard_map/reduce_scatter | solution.py:159
  94.5 1.0 copy-start.3
  94.5 289.0 %all-reduce.5.cloned.1.call-start = ((), (), s32[]{:S(2)}) async-start(), calls=%async_computation.6 | async-start | bytes 2801664 | tf_op jit(solution)/shard_map/psum | solution.py:161
  95.1 3.7 copy-start.7
  95.1 3.7 copy-start.8
  98.8 1.7 copy-start.19
  100.5 2.4 copy-start.15
  100.6 2.4 copy-start.16
  100.6 2.4 copy-start.17
  100.6 2.3 copy-start.26
  115.4 225.5 %collective-permute-start.2 = (f32[8,3712]{1,0:T(8,128)S(1)}, f32[8,3712]{1,0:T(8,128)S(1)}, u32[]{:S(2)}, u32[]{:S(2)}) collective-permute-start(f32[8,3712]{1,0:T(8,128)S(1)} %get-tuple-element.31), channel_id=1, source_target_pairs={{0,1},{1,2},{2,3},{3,4},{4,5},{5,6},{6,7},{8,9},{9,10},{10,11},{11... | collective-permute-start | bytes 356360 | tf_op jit(solution)/shard_map/ppermute | solution.py:29
  119.9 221.0 %collective-permute-start.3 = (f32[8,3712]{1,0:T(8,128)S(1)}, f32[8,3712]{1,0:T(8,128)S(1)}, u32[]{:S(2)}, u32[]{:S(2)}) collective-permute-start(f32[8,3712]{1,0:T(8,128)S(1)} %get-tuple-element.32), channel_id=1, source_target_pairs={{1,0},{2,1},{3,2},{4,3},{5,4},{6,5},{7,6},{9,8},{10,9},{11,10},{12... | collective-permute-start | bytes 356360 | tf_op jit(solution)/shard_map/ppermute | solution.py:29
  (3 other events, 2.2 us)
Sparse Core Ops, SparseCore 0:
  82.1 81.5 reduce-scatter.3
  167.2 75.2 reduce-scatter.7
  246.2 94.6 reduce-scatter.5
  343.3 40.1 all-reduce.4
where the time goes:
time: 397 us; the launch traced here: 396 us
  waiting for transfers between devices  265 us (67%)
  other arithmetic  40.5 us (10%)
  local copies, waits for them, and re-layouts  36.8 us (9%)
  matrix products  26.2 us (7%)
  between operations  14.2 us (4%)
  starting transfers between devices  12.3 us (3%)
    reduce_scatter x1, waiting for transfers between devices, shards(): lax.psum_scatter(weight_term(pair_one), 'graph', scatter_dimension=0, til...  98.3 us
    reduce_scatter x1, waiting for transfers between devices, shards(): lax.psum_scatter(weight_term(pair_two), 'graph', scatter_dimension=0, til...  78.9 us
    reduce_scatter x1, waiting for transfers between devices, shards(): lax.psum_scatter(weight_term(pair_zero), 'graph', scatter_dimension=0, ti...  42.4 us
    psum x1, waiting for transfers between devices, shards(): totals = lax.psum((part_zero, part_one, part_two), 'dp')  41.9 us
    dot_general x3, matrix products, contract_rows(): lax.dot_general(first, second, (((0,), (0,)), ((), ())), preferred_elemen...  14.2 us
    mul x6, local copies, waits for them, and re-layouts, gated(): shaped = per_head(block, channels, heads) * gate[:, None, :, None]  11.2 us
    scatter-add x1, other arithmetic, shards(): jnp.zeros((atom_count + 2 * reach, row_width), jnp.float32).at[src_local]  8.74 us
  transfers between devices with their start and end apart: 8, of which 5 were waited for; matrix products, arithmetic and copies ran while one was open for 8% of the time, Pallas kernels for 0%

commit v1 on v0

v1 whole, which is shorter than its diff:
```python
import jax
import jax.numpy as jnp
from jax import lax
from jax.experimental import pallas as pl
from jax.experimental.pallas import tpu as pltpu
from jax.sharding import PartitionSpec as P

HEADS = 8
LEVELS = 7
ROWS = 16
LANES = 128
F32 = jnp.float32
BF16 = jnp.bfloat16


def mm(first, second):
    return lax.dot_general(first, second, (((1,), (0,)), ((), ())), preferred_element_type=F32)


def mm_t(first, second):
    return lax.dot_general(first, second, (((1,), (1,)), ((), ())), preferred_element_type=F32)


def pieces(value, count):
    out = []
    rest = value
    for _ in range(count):
        part = rest.astype(BF16)
        out.append(part)
        rest = rest - part.astype(F32)
    return out


def one_hot(index, shape, dim):
    return jnp.where(lax.broadcasted_iota(jnp.int32, shape, dim) == index, 1.0, 0.0).astype(F32)


def chunks(width, step=256):
    return [(lo, min(lo + step, width)) for lo in range(0, width, step)]


def head_mask(channels, heads):
    size = channels // heads
    row = lax.broadcasted_iota(jnp.int32, (channels, channels), 0) // size
    col = lax.broadcasted_iota(jnp.int32, (channels, channels), 1) // size
    return jnp.where(row == col, 1.0, 0.0).astype(BF16)


def head_sum(value, channels, heads):
    mask = head_mask(channels, heads)
    total = None
    for part in pieces(value, 3):
        term = mm(part, mask)
        total = term if total is None else total + term
    return total


class Tiles:
    def __init__(self, rows, cols, graph, parts):
        self.rows = rows // graph
        self.cols = cols
        self.graph = graph
        self.down = -(-self.rows // ROWS)
        self.across = cols // LANES
        self.count = self.down * self.across
        self.parts = parts
        self.each = -(-self.count // parts)
        self.shape = (parts, graph, self.each + 1, ROWS, LANES)

    def store(self, ref, block, lo):
        for g in range(self.graph):
            for i in range(self.down):
                r0 = i * ROWS
                r1 = min(r0 + ROWS, self.rows)
                for j in range(block.shape[1] // LANES):
                    tile = i * self.across + lo // LANES + j
                    ref[tile // self.each, g, tile % self.each, : r1 - r0, :] = block[
                        g * self.rows + r0 : g * self.rows + r1, j * LANES : (j + 1) * LANES
                    ]

    def finish(self, ref, exponent):
        level = jnp.broadcast_to(exponent, (ROWS, LANES))
        for q in range(self.parts):
            for g in range(self.graph):
                ref[q, g, self.each] = level
        for tile in range(self.count, self.parts * self.each):
            for g in range(self.graph):
                ref[tile // self.each, g, tile % self.each] = jnp.zeros((ROWS, LANES), F32)

    def rebuild(self, tiles):
        flat = tiles.reshape(self.parts * self.each, ROWS, LANES)[: self.count]
        grid = flat.reshape(self.down, self.across, ROWS, LANES).transpose(0, 2, 1, 3)
        return grid.reshape(self.down * ROWS, self.cols)[: self.rows]


def level_of(bound):
    return jnp.floor(jnp.log2(jnp.maximum(bound, 1e-30))) + 2.0


def top(value):
    return jnp.max(jnp.max(jnp.abs(value), axis=1, keepdims=True), axis=0, keepdims=True)


def wgrad_pair(tiles, ref, xst, dref, width, count):
    turned = xst.T
    for lo, hi in chunks(2 * width):
        if hi <= width:
            upper = dref[:, lo:hi]
            lower = dref[:, width + lo : width + hi]
        elif lo >= width:
            upper = dref[:, lo:hi]
            lower = -dref[:, lo - width : hi - width]
        else:
            upper = dref[:, lo:hi]
            lower = jnp.concatenate([dref[:, width + lo :], -dref[:, : hi - width]], 1)
        tiles.store(ref, mm(turned, jnp.concatenate([upper, lower], 0)), lo)


def make_first(channels, heads, tiles):
    z, w1, w2 = LEVELS * channels, (LEVELS - 1) * channels, (LEVELS - 2) * channels
    b1, b2 = z + 2 * w1, z + 2 * w1 + 2 * w2

    def body(table, src, dst, trig, wz, x1, d1, x2, d2, gate_out, cot_out, level_out, grad):
        count = src.shape[0]
        atoms = table.shape[1]
        pick = one_hot(src[...], (count, atoms), 1).astype(BF16)
        aim = one_hot(dst[...], (count, atoms), 1).astype(BF16)
        feat = table.at[0]
        cot = table.at[1]
        scale = 1.0 / (channels // heads) ** 0.5
        logits = mm(feat[:, :z], wz[...])
        gate_node = jax.nn.sigmoid(head_sum(logits, channels, heads) * scale)
        gate = sum(mm(pick, part) for part in pieces(gate_node, 3))
        gate_out[...] = gate
        cot_out[...] = mm(aim, cot[...]).astype(BF16)

        def turn(lo, width, cosine, sine, x, d):
            for j in range(width // channels):
                at = slice(lo + j * channels, lo + (j + 1) * channels)
                bt = slice(lo + width + j * channels, lo + width + (j + 1) * channels)
                p = mm(pick, feat[:, at])
                n = mm(pick, feat[:, bt])
                to = slice(j * channels, (j + 1) * channels)
                x[:count, to] = (cosine * p - sine * n).astype(BF16)
                x[count:, to] = (sine * p + cosine * n).astype(BF16)
                p = cot_out[:, at].astype(F32)
                n = cot_out[:, bt].astype(F32)
                d[:, to] = (gate * (cosine * p - sine * n)).astype(BF16)
                d[:, width + j * channels : width + (j + 1) * channels] = (
                    gate * (sine * p + cosine * n)
                ).astype(BF16)

        turn(z, w1, trig[:, 0:1], trig[:, 1:2], x1, d1)
        turn(b1, w2, trig[:, 2:3], trig[:, 3:4], x2, d2)
        wgrad_pair(tiles, grad, x1[...], d1, w1, count)
        bound = top(feat[...].astype(F32)) * top(cot[...].astype(F32)) * (4.1 * count)
        level = level_of(bound)
        level_out[...] = jnp.broadcast_to(level, level_out.shape)
        tiles.finish(grad, level)

    return body


def make_second(channels, tiles):
    w2 = (LEVELS - 2) * channels

    def body(x2, d2, level_in, grad):
        wgrad_pair(tiles, grad, x2[...], d2, w2, d2.shape[0])
        tiles.finish(grad, level_in[0:1, 0:1])

    return body


def make_third(channels, heads, tiles):
    z, w1, w2 = LEVELS * channels, (LEVELS - 1) * channels, (LEVELS - 2) * channels
    b1 = z + 2 * w1

    def body(table, src, trig, src_row, trig_row, x1, d1, x2, d2, gate_in, cot, wz, wo, wt, grad, nodes):
        count = src.shape[0]
        atoms = table.shape[1]
        feat = table.at[0]
        gate = gate_in[...]
        pick = one_hot(src[...], (count, atoms), 1).astype(BF16)
        place = one_hot(src_row[...], (atoms, count), 0)
        scale = 1.0 / (channels // heads) ** 0.5

        dgate = jnp.zeros((count, channels), F32)
        node_zero = mm(feat[:, :z], wz[...])
        wide = jnp.concatenate(pieces(node_zero, 3), 0)
        pick_wide = jnp.concatenate([pick, pick, pick], 1)
        for lo, hi in chunks(z):
            out = mm(pick_wide, wide[:, lo:hi])
            term = cot[:, lo:hi].astype(F32) * out
            for k in range((hi - lo) // channels):
                dgate = dgate + term[:, k * channels : (k + 1) * channels]

        def forward(dgate, lo0, width, cosine, sine, x, w):
            rp = x[:count, :]
            rn = x[count:, :]
            for lo, hi in chunks(width):
                wa = w[:, lo:hi]
                wb = w[:, width + lo : width + hi]
                out_p = mm(rp, wa) - mm(rn, wb)
                out_n = mm(rp, wb) + mm(rn, wa)
                p = cot[:, lo0 + lo : lo0 + hi].astype(F32)
                n = cot[:, lo0 + width + lo : lo0 + width + hi].astype(F32)
                term = (cosine * p - sine * n) * out_p + (sine * p + cosine * n) * out_n
                for k in range((hi - lo) // channels):
                    dgate = dgate + term[:, k * channels : (k + 1) * channels]
            return dgate

        dgate = forward(dgate, z, w1, trig[:, 0:1], trig[:, 1:2], x1, wo)
        dgate = forward(dgate, b1, w2, trig[:, 2:3], trig[:, 3:4], x2, wt)
        dlogit = head_sum(dgate, channels, heads) * gate * (1.0 - gate) * scale
        dz = []
        for j in range(LEVELS):
            block = gate * cot[:, j * channels : (j + 1) * channels].astype(F32)
            if j == 0:
                block = block + dlogit
            dz.append(block.astype(BF16))
        dz = jnp.concatenate(dz, 1)

        node_dz = mm(place.astype(BF16), dz)
        parts = pieces(node_dz, 3)
        turned = feat[:, :z].astype(F32).T.astype(BF16)
        turned = jnp.concatenate([turned, turned, turned], 1)
        stack = jnp.concatenate(parts, 0)
        for lo, hi in chunks(z):
            tiles.store(grad, mm(turned, stack[:, lo:hi]), lo)
        bound = top(feat[:, :z].astype(F32)) * top(dz.astype(F32)) * (1.01 * count)
        tiles.finish(grad, level_of(bound))

        back = mm_t(stack, wz[...])
        nodes[:, :z] = back[:atoms] + back[atoms : 2 * atoms] + back[2 * atoms :]

        def backward(lo0, width, cosine, sine, d, w):
            terms = pieces(place * cosine, 2) + pieces(place * sine, 2)
            spread = mm(jnp.concatenate(terms, 0), d[...])
            by_c = spread[:atoms] + spread[atoms : 2 * atoms]
            by_s = spread[2 * atoms : 3 * atoms] + spread[3 * atoms :]
            t1 = by_c[:, :width] + by_s[:, width:]
            t2 = by_c[:, width:] - by_s[:, :width]
            plus = pieces(jnp.concatenate([t1, t2], 1), 2)
            minus = pieces(jnp.concatenate([t2, -t1], 1), 2)
            back = mm_t(jnp.concatenate(plus + minus, 0), w[...])
            nodes[:, lo0 : lo0 + width] = back[:atoms] + back[atoms : 2 * atoms]
            nodes[:, lo0 + width : lo0 + 2 * width] = (
                back[2 * atoms : 3 * atoms] + back[3 * atoms :]
            )

        backward(z, w1, trig_row[0:1, :], trig_row[1:2, :], d1, wo)
        backward(b1, w2, trig_row[2:3, :], trig_row[3:4, :], d2, wt)

    return body


def bits_of(size):
    return [k for k in range(size.bit_length() - 1)]


def main_mask(ndim, each):
    shape = [1] * ndim
    shape[-3] = each + 1
    return lax.broadcasted_iota(jnp.int32, tuple(shape), ndim - 3) < each


def level_in(value):
    for _ in range(value.ndim - 3):
        value = value[0]
    return value[-1, 0, 0]


def encode(value, each):
    level = level_in(value)
    factor = jnp.where(main_mask(value.ndim, each), jnp.exp2(15.0 - level), 1.0)
    return (value * factor).astype(jnp.float16)


def decode(message, each):
    value = message.astype(F32)
    factor = jnp.where(main_mask(value.ndim, each), jnp.exp2(level_in(value) - 15.0), 1.0)
    return value * factor


def combine(first, second, each):
    both = jnp.where(
        main_mask(first.ndim, each), first + second, jnp.maximum(first, second) + 1.0
    )
    return both


def exchange(parts, bit, me):
    size = lax.axis_size("dp")
    mine = (me >> bit) & 1
    sends = [
        encode(lax.dynamic_index_in_dim(value, 1 - mine, 0, False), tiles.each)
        for value, tiles in parts
    ]
    return mine, sends, [(i, i ^ (1 << bit)) for i in range(size)]


def halve(parts, bit, me):
    mine, sends, route = exchange(parts, bit, me)
    got = join(sends)
    got = lax.ppermute(got, "dp", route)
    out = []
    for (value, tiles), message in zip(parts, split(got, parts)):
        keep = lax.dynamic_index_in_dim(value, mine, 0, False)
        out.append((combine(keep, decode(message, tiles.each), tiles.each), tiles))
    return out


def join(values):
    return values[0] if len(values) == 1 else jnp.concatenate(values, axis=values[0].ndim - 3)


def split(value, parts):
    out = []
    at = 0
    for _, tiles in parts:
        out.append(lax.slice_in_dim(value, at, at + tiles.each + 1, axis=value.ndim - 3))
        at += tiles.each + 1
    return out


def over_graph(parts):
    sent = join([encode(value, tiles.each) for value, tiles in parts])
    got = lax.all_to_all(sent, "graph", 0, 0, tiled=True)
    out = []
    for (_, tiles), message in zip(parts, split(got, parts)):
        value = message.astype(F32)
        factor = jnp.exp2(value[:, -1:, :1, :1] - 15.0)
        out.append(((value[:, : tiles.each] * factor).sum(0), tiles))
    return out


def regather(parts, me):
    size = lax.axis_size("dp")
    whole = join([value for value, _ in parts])[None]
    for bit in reversed(bits_of(size)):
        other = lax.ppermute(whole, "dp", [(i, i ^ (1 << bit)) for i in range(size)])
        low = ((me >> bit) & 1) == 0
        whole = jnp.concatenate([jnp.where(low, whole, other), jnp.where(low, other, whole)], 0)
    out = []
    at = 0
    for _, tiles in parts:
        out.append(tiles.rebuild(whole[:, at : at + tiles.each]) / size)
        at += tiles.each
    return out


def call(body, outs, flops, *args):
    return pl.pallas_call(
        body,
        out_shape=outs,
        in_specs=[pl.BlockSpec(memory_space=pltpu.VMEM)] * len(args),
        out_specs=jax.tree.map(lambda _: pl.BlockSpec(memory_space=pltpu.VMEM), outs),
        compiler_params=pltpu.CompilerParams(vmem_limit_bytes=60 * 1024 * 1024),
        cost_estimate=pl.CostEstimate(flops=flops, bytes_accessed=1 << 24, transcendentals=0),
    )(*args)


def shards(node_feats, node_cotan, source, target, angle, w_zero, w_one, w_two):
    atom_count = node_feats.shape[1]
    row_width = node_feats.shape[2]
    channels = row_width // 29
    edges = source.shape[1]
    graph = lax.axis_size("graph")
    size = lax.axis_size("dp")
    position = lax.axis_index("graph")
    me = lax.axis_index("dp")
    reach = atom_count // 2
    w1, w2 = (LEVELS - 1) * channels, (LEVELS - 2) * channels

    up = [(i, i + 1) for i in range(graph - 1)]
    down = [(i + 1, i) for i in range(graph - 1)]
    own = jnp.stack([node_feats[0], node_cotan[0]], 0)
    before = lax.ppermute(own[:, atom_count - reach :], "graph", up)
    after = lax.ppermute(own[:, :reach], "graph", down)
    table = jnp.concatenate([before, own, after], 1)
    first_atom = position * atom_count - reach
    src = source[0] - first_atom
    dst = target[0] - first_atom
    phases = angle[0]
    trig_row = jnp.stack(
        [jnp.cos(phases), jnp.sin(phases), jnp.cos(2.0 * phases), jnp.sin(2.0 * phases)], 0
    )
    trig = trig_row.T

    t_one = Tiles(*w_one.shape, graph, size)
    t_two = Tiles(*w_two.shape, graph, size)
    t_zero = Tiles(*w_zero.shape, graph, size)
    shape = jax.ShapeDtypeStruct
    x1, d1, x2, d2, gate, cot, level, grad_one = call(
        make_first(channels, HEADS, t_one),
        (
            shape((2 * edges, w1), BF16),
            shape((edges, 2 * w1), BF16),
            shape((2 * edges, w2), BF16),
            shape((edges, 2 * w2), BF16),
            shape((edges, channels), F32),
            shape((edges, row_width), BF16),
            shape((8, LANES), F32),
            shape(t_one.shape, F32),
        ),
        3_000_000_000,
        table,
        src[:, None],
        dst[:, None],
        trig,
        w_zero[:, :channels],
    )
    grad_two = call(
        make_second(channels, t_two), shape(t_two.shape, F32), 1_200_000_000, x2, d2, level
    )
    grad_zero, nodes = call(
        make_third(channels, HEADS, t_zero),
        (shape(t_zero.shape, F32), shape((atom_count + 2 * reach, row_width), F32)),
        4_000_000_000,
        table,
        src[:, None],
        trig,
        src[None, :],
        trig_row,
        x1,
        d1,
        x2,
        d2,
        gate,
        cot,
        w_zero,
        w_one,
        w_two,
    )

    from_next = lax.ppermute(nodes[:reach], "graph", down)
    from_prev = lax.ppermute(nodes[atom_count + reach :], "graph", up)
    rows = nodes[reach : reach + atom_count]
    rows = rows + jnp.concatenate([from_prev, from_next], 0)
    grad_nodes = rows.astype(BF16)[None]

    def paired(value):
        return value.reshape((2,) * len(bits_of(size)) + value.shape[1:])

    one = [(paired(grad_one), t_one)]
    rest = [(paired(grad_two), t_two), (paired(grad_zero), t_zero)]
    groups = [one, rest]
    for bit in bits_of(size):
        groups = [halve(parts, bit, me) for parts in groups]
    groups = [over_graph(parts) for parts in groups]
    (one,), (two, zero) = [regather(parts, me) for parts in groups]
    return (grad_nodes, zero, one, two)


def solution(mesh):
    return jax.shard_map(
        shards,
        mesh=mesh,
        in_specs=(
            P("dp", "graph", None),
            P("dp", "graph", None),
            P("dp", "graph"),
            P("dp", "graph"),
            P("dp", "graph"),
            P(),
            P(),
            P(),
        ),
        out_specs=(P("dp", "graph", None), P("graph", None), P("graph", None), P("graph", None)),
        check_vma=False,
    )
```

time: 397 us -> 148 us (0.37)
  waiting for transfers between devices: 265 us -> 33.2 us
  matrix products: 26.2 us -> 0 us
  Pallas kernels: 0 us -> 26.1 us
  starting transfers between devices: 12.3 us -> 31.4 us
  other arithmetic: 40.5 us -> 24.2 us
  local copies, waits for them, and re-layouts: 36.8 us -> 20.8 us
    reduce_scatter x3 -> x0, waiting for transfers between devices: 220 us -> none  [the longest x1 98.3 us: shards(): lax.psum_scatter(weight_term(pair_one), 'graph', scatter_dimension=0, til...]
    psum x1 -> x0, waiting for transfers between devices: 41.9 us -> none  [shards(): totals = lax.psum((part_zero, part_one, part_two), 'dp')]
    dot_general x9 -> x0, matrix products: 26.2 us -> none  [the longest x3 14.2 us: contract_rows(): lax.dot_general(first, second, (((0,), (0,)), ((), ())), preferred_elemen...]
    pallas_call x0 -> x3, Pallas kernels: none -> 26.1 us  [call(): pl.pallas_call(body, out_shape=outs, in_specs=[pl.BlockSpec(memory_space=...]
    mul x11 -> x0, local copies, waits for them, and re-layouts: 18.8 us -> none  [the longest x6 11.2 us: gated(): shaped = per_head(block, channels, heads) * gate[:, None, :, None]]
    all_to_all x0 -> x2, waiting for transfers between devices: none -> 16.5 us  [over_graph(): got = lax.all_to_all(sent, 'graph', 0, 0, tiled=True)]
    all_to_all x0 -> x2, starting transfers between devices: none -> 13.9 us  [over_graph(): got = lax.all_to_all(sent, 'graph', 0, 0, tiled=True)]
    ppermute x4 -> x12, waiting for transfers between devices: 3.84 us -> 16.6 us  [the longest x4 12.4 us: halve(): got = lax.ppermute(got, 'dp', route)]
  transfers between devices with their start and end apart: 8 -> 14, of which waited for: 5 -> 4; matrix products, arithmetic and copies ran while one was open for 8% -> 23% of each run, Pallas kernels for 0% -> 13%
where the time goes in v1:
time: 148 us; the launch traced here: 147 us
  waiting for transfers between devices  33.2 us (22%)
  starting transfers between devices  31.4 us (21%)
  Pallas kernels  26.1 us (18%)
  other arithmetic  24.2 us (16%)
  local copies, waits for them, and re-layouts  20.8 us (14%)
  between operations  11.7 us (8%)
    pallas_call x3, Pallas kernels, call(): pl.pallas_call(body, out_shape=outs, in_specs=[pl.BlockSpec(memory_space=...  26.1 us
    all_to_all x2, waiting for transfers between devices, over_graph(): got = lax.all_to_all(sent, 'graph', 0, 0, tiled=True)  16.5 us
    all_to_all x2, starting transfers between devices, over_graph(): got = lax.all_to_all(sent, 'graph', 0, 0, tiled=True)  13.9 us
    ppermute x4, waiting for transfers between devices, halve(): got = lax.ppermute(got, 'dp', route)  12.4 us
    convert_element_type x9, other arithmetic, encode(): return (value * factor).astype(jnp.float16)  8.43 us
    slice x15, local copies, waits for them, and re-layouts, level_in(): return value[-1, 0, 0]  7.76 us
    select_n x4, other arithmetic, combine(): jnp.where(main_mask(first.ndim, each), first + second, jnp.maximum(first,...  5.42 us
    ppermute x1, starting transfers between devices, shards(): before = lax.ppermute(own[:, atom_count - reach:], 'graph', up)  4.91 us
  transfers between devices with their start and end apart: 14, of which 4 were waited for; matrix products, arithmetic and copies ran while one was open for 23% of the time, Pallas kernels for 13%

profile of v1, /device:TPU:0, one launch (start us, length us, event | category | flops | bytes accessed | tf_op | source)
XLA Modules:
  0.0 147.3 jit_solution(17674853947185709900)
XLA Ops:
  0.6 0.9 constant_dynamic-update-slice_fusion.1
  1.5 0.9 constant_dynamic-update-slice_fusion
  2.5 4.9 %collective-permute-start = (bf16[2,8,3712]{2,1,0:T(8,128)(2,1)S(1)}, bf16[2,8,3712]{2,1,0:T(8,128)(2,1)S(1)}, u32[]{:S(2)}, u32[]{:S(2)}) collective-permute-start(bf16[2,8,3712]{2,1,0:T(8,128)(2,1)S(1)} %get-tuple-element.46), channel_id=1, source_target_pairs={{0,1},{1,2},{2,3},{3,4},{4,5},{5,6},{6,7},{8,9},{9,10},{10,11},{11... | collective-permute-start | bytes 356360 | tf_op jit(solution)/shard_map/ppermute | solution.py:378
  7.4 1.3 collective-permute-start.1
  13.2 1.6 %slice.182.wz = bf16[896,128]{1,0:T(8,128)(2,1)} slice(bf16[896,896]{1,0:T(8,128)(2,1)} %wz.1), slice={[0:896], [0:128]} | slice | bytes 458752 | tf_op jit(solution)/shard_map/slice | solution.py:411
  15.7 7.7 %shard_map.111 = (bf16[640,768]{1,0:T(8,128)(2,1)}, bf16[320,1536]{1,0:T(8,128)(2,1)}, bf16[640,640]{1,0:T(8,128)(2,1)}, bf16[320,1280]{1,0:T(8,128)(2,1)}, f32[...) custom-call(bf16[2,32,3712]{2,1,0:T(8,128)(2,1)} %pad_maximum_fusion.3.table, ...), custom_call_target="tpu_custom_call" | custom-call | flops 3000000000 | bytes 16777216 | tf_op jit(solution)/shard_map/pallas_call | solution.py:353
  23.4 0.9 dynamic-slice_bitcast_fusion.1
  25.5 3.1 %fusion = f16[2,8,19,16,128]{4,3,2,1,0:T(8,128)(2,1)} fusion(f32[2,2,8,19,16,128]{5,4,3,2,1,0:T(8,128)} %bitcast.172, s32[]{:T(128)S(6)} %select_n.221, f32[19]{0:T(128)S(1)} %fusion.47), kind=kLoop, calls=%fused_computation.1 | loop fusion | flops 1245184 | bytes 3735632 | tf_op jit(solution)/shard_map/convert_element_type | solution.py:276
  28.6 13.7 %shard_map.112 = (f32[4,8,14,16,128]{4,3,2,1,0:T(8,128)}, f32[32,3712]{1,0:T(8,128)}) custom-call(bf16[2,32,3712]{2,1,0:T(8,128)(2,1)} %pad_maximum_fusion.3.table, s32[320,1]{1,0:T(8,128)} %copy.30.src, f32[320,4]{1,0:T(8,128)} %copy.31.trig, s32[1,320]{1,0:T(1,128)} %copy-done.6, f32[4,320]{1,0:T(4,128)} %get-tuple-element.48.trig_row, ...), custom_call_target="tpu_custom_call" | custom-call | flops 4000000000 | bytes 16777216 | tf_op jit(solution)/shard_map/pallas_call | solution.py:353
  42.3 0.9 dynamic-slice_bitcast_fusion.4
  44.5 1.8 %fusion.5 = f16[2,8,14,16,128]{4,3,2,1,0:T(8,128)(2,1)S(1)} fusion(f32[2,2,8,14,16,128]{5,4,3,2,1,0:T(8,128)} %bitcast.175, s32[]{:T(128)S(6)} %select_n.221, f32[14]{0:T(128)S(1)} %fusion.41), kind=kLoop, calls=%fused_computation.12 | loop fusion | flops 917504 | bytes 2752572 | tf_op jit(solution)/shard_map/convert_element_type | solution.py:276
  46.2 4.7 %shard_map.113 = f32[4,8,14,16,128]{4,3,2,1,0:T(8,128)} custom-call(bf16[640,640]{1,0:T(8,128)(2,1)} %get-tuple-element.16.x2, bf16[320,1280]{1,0:T(8,128)(2,1)} %get-tuple-element.17.d2, f32[8,128]{1,0:T(8,128)} %get-tuple-element.21.level_in), custom_call_target="tpu_custom_call" | custom-call | flops 1200000000 | bytes 16777216 | tf_op jit(solution)/shard_map/pallas_call | solution.py:353
  53.0 1.8 %fusion.6 = f16[2,8,14,16,128]{4,3,2,1,0:T(8,128)(2,1)S(1)} fusion(f32[2,2,8,14,16,128]{5,4,3,2,1,0:T(8,128)} %bitcast.169, s32[]{:T(128)S(6)} %select_n.221, f32[14]{0:T(128)S(1)} %fusion.42), kind=kLoop, calls=%fused_computation.14 | loop fusion | flops 917504 | bytes 2752572 | tf_op jit(solution)/shard_map/convert_element_type | solution.py:276
  54.8 2.1 %pad_maximum_fusion = f16[2,8,28,16,128]{4,3,2,1,0:T(8,128)(2,1)} fusion(f16[2,8,14,16,128]{4,3,2,1,0:T(8,128)(2,1)S(1)} %fusion.5, f16[2,8,14,16,128]{4,3,2,1,0:T(8,128)(2,1)S(1)} %fusion.6), kind=kLoop, calls=%fused_computation.6 | loop fusion | flops 917504 | bytes 3670016 | tf_op jit(solution)/shard_map/concatenate | solution.py:314
  58.8 2.3 %fusion.1 = f32[2,8,19,16,128]{4,3,2,1,0:T(8,128)S(1)} fusion(f32[2,2,8,19,16,128]{5,4,3,2,1,0:T(8,128)} %bitcast.173, s32[]{:T(128)S(6)} %select_n.220, f32[19]{0:T(128)S(1)} %fusion.46, pred[19]{0:T(512)(128)(4,1)S(1)} %iota_compare_fusion, f16[2,8,19,16,128]{4,3,2,1,0:T(8,128)(2,1)S(1)} %collective-permute-done.8), kind=kLoop, calls=%fused_computation.4 | loop fusion | flops 3735552 | bytes 6226019 | tf_op jit(solution)/shard_map/jit(_where)/select_n | solution.py:286
  62.6 1.6 %collective-permute-start.9 = (f16[8,19,16,128]{3,2,1,0:T(8,128)(2,1)S(1)}, f16[8,19,16,128]{3,2,1,0:T(8,128)(2,1)S(1)}, u32[]{:S(2)}, u32[]{:S(2)}) collective-permute-start(f16[8,19,16,128]{3,2,1,0:T(8,128)(2,1)S(1)} %fusion.9), channel_id=1, source_target_pairs={{0,16},{8,24},{16,0},{24,8},{1,17},{9,25},{17,1},{25,9},{2,18},{10... | collective-permute-start | bytes 1867784 | tf_op jit(solution)/shard_map/ppermute | solution.py:305
  64.4 1.0 copy-done.3
  67.9 2.3 %fusion.7 = (f32[2,8,14,16,128]{4,3,2,1,0:T(8,128)S(1)}, f32[2,8,14,16,128]{4,3,2,1,0:T(8,128)S(1)}) fusion(f32[2,2,8,14,16,128]{5,4,3,2,1,0:T(8,128)S(1)} %bitcast.170, s32[]{:T(128)S(6)} %select_n.220, f32[14]{0:T(128)S(1)} %fusion.40, pred[14]{0:T(512)(128)(4,1)S(1)} %iota_compare_fusion.1, f16[2,8,28,16,128]{4,3,2,1,0:T(8,128)(2,1)} %copy-done.3, ...), kind=kLoop, calls=%fused_computation.17 | loop fusion | flops 5505024 | bytes 9175170 | tf_op jit(solution)/shard_map/jit(_where)/select_n | solution.py:286
  73.1 1.2 pad_maximum_fusion.1
  75.0 4.5 %collective-permute-done.9 = f16[8,19,16,128]{3,2,1,0:T(8,128)(2,1)S(1)} collective-permute-done((f16[8,19,16,128]{3,2,1,0:T(8,128)(2,1)S(1)}, f16[8,19,16,128]{3,2,1,0:T(8,128)(2,1)S(1)}, u32[]{:S(2)}, u32[]{:S(2)}) %collective-permute-start.9) | collective-permute-done | bytes 622624 | tf_op jit(solution)/shard_map/ppermute | solution.py:305
  82.4 1.0 multiply_convert_fusion
  83.4 7.0 %all-to-all-start.1 = ((f16[8,19,16,128]{3,2,1,0:T(8,128)(2,1)}), f16[8,19,16,128]{3,2,1,0:T(8,128)(2,1)S(1)}, u32[]{:S(2)}, u32[]{:S(2)}) async-start(f16[8,19,16,128]{3,2,1,0:T(8,128)(2,1)} %multiply_convert_fusion), calls=%async_computation.1 | async-start | bytes 1245184 | tf_op jit(solution)/shard_map/all_to_all | solution.py:328
  90.4 7.8 %collective-permute-done.5 = f16[8,28,16,128]{3,2,1,0:T(8,128)(2,1)S(1)} collective-permute-done((f16[8,28,16,128]{3,2,1,0:T(8,128)(2,1)}, f16[8,28,16,128]{3,2,1,0:T(8,128)(2,1)S(1)}, u32[]{:S(2)}, u32[]{:S(2)}) %collective-permute-start.5) | collective-permute-done | bytes 917536 | tf_op jit(solution)/shard_map/ppermute | solution.py:305
  104.3 1.2 pad_maximum_fusion.2
  105.5 7.0 %all-to-all-start = ((f16[8,28,16,128]{3,2,1,0:T(8,128)(2,1)}), f16[8,28,16,128]{3,2,1,0:T(8,128)(2,1)S(1)}, u32[]{:S(2)}, u32[]{:S(2)}) async-start(f16[8,28,16,128]{3,2,1,0:T(8,128)(2,1)} %pad_maximum_fusion.2), calls=%async_computation | async-start | bytes 1835008 | tf_op jit(solution)/shard_map/all_to_all | solution.py:328
  112.5 3.9 %collective-permute-start.2 = (f32[8,3712]{1,0:T(8,128)S(1)}, f32[8,3712]{1,0:T(8,128)S(1)}, u32[]{:S(2)}, u32[]{:S(2)}) collective-permute-start(f32[8,3712]{1,0:T(8,128)S(1)} %get-tuple-element.40), channel_id=1, source_target_pairs={{0,1},{1,2},{2,3},{3,4},{4,5},{5,6},{6,7},{8,9},{9,10},{10,11},{11... | collective-permute-start | bytes 356360 | tf_op jit(solution)/shard_map/ppermute | solution.py:437
  116.4 1.3 collective-permute-start.3
  118.1 1.6 %collective-permute-start.10 = (f32[1,18,16,128]{3,2,1,0:T(8,128)S(1)}, f32[1,18,16,128]{3,2,1,0:T(8,128)S(1)}, u32[]{:S(2)}, u32[]{:S(2)}) collective-permute-start(f32[1,18,16,128]{3,2,1,0:T(8,128)S(1)} %bitcast.185), channel_id=1, source_target_pairs={{0,16},{8,24},{16,0},{24,8},{1,17},{9,25},{17,1},{25,9},{2,18},{10... | collective-permute-start | bytes 442376 | tf_op jit(solution)/shard_map/ppermute | solution.py:341
  119.7 16.5 %all-to-all-done = f16[8,28,16,128]{3,2,1,0:T(8,128)(2,1)S(1)} async-done(((f16[8,28,16,128]{3,2,1,0:T(8,128)(2,1)}), f16[8,28,16,128]{3,2,1,0:T(8,128)(2,1)S(1)}, u32[]{:S(2)}, u32[]{:S(2)}) %all-to-all-start) | async-done | bytes 917536 | tf_op jit(solution)/shard_map/all_to_all | solution.py:328
  137.0 1.6 %collective-permute-start.6 = (f32[1,26,16,128]{3,2,1,0:T(8,128)S(1)}, f32[1,26,16,128]{3,2,1,0:T(8,128)S(1)}, u32[]{:S(2)}, u32[]{:S(2)}) collective-permute-start(f32[1,26,16,128]{3,2,1,0:T(8,128)S(1)} %maximum_bitcast_fusion), channel_id=1, source_target_pairs={{0,16},{8,24},{16,0},{24,8},{1,17},{9,25},{17,1},{25,9},{2,18},{10... | collective-permute-start | bytes 638984 | tf_op jit(solution)/shard_map/ppermute | solution.py:341
  138.7 4.2 %collective-permute-done.6 = f32[1,26,16,128]{3,2,1,0:T(8,128)S(1)} collective-permute-done((f32[1,26,16,128]{3,2,1,0:T(8,128)S(1)}, f32[1,26,16,128]{3,2,1,0:T(8,128)S(1)}, u32[]{:S(2)}, u32[]{:S(2)}) %collective-permute-start.6) | collective-permute-done | bytes 213024 | tf_op jit(solution)/shard_map/ppermute | solution.py:341
  144.1 1.0 copy.41
  (118 shorter events, 22.5 us)
Async XLA Ops:
  2.5 12.4 %collective-permute-start = (bf16[2,8,3712]{2,1,0:T(8,128)(2,1)S(1)}, bf16[2,8,3712]{2,1,0:T(8,128)(2,1)S(1)}, u32[]{:S(2)}, u32[]{:S(2)}) collective-permute-start(bf16[2,8,3712]{2,1,0:T(8,128)(2,1)S(1)} %get-tuple-element.46), channel_id=1, source_target_pairs={{0,1},{1,2},{2,3},{3,4},{4,5},{5,6},{6,7},{8,9},{9,10},{10,11},{11... | collective-permute-start | bytes 356360 | tf_op jit(solution)/shard_map/ppermute | solution.py:378
  7.4 7.5 %collective-permute-start.1 = (bf16[2,8,3712]{2,1,0:T(8,128)(2,1)S(1)}, bf16[2,8,3712]{2,1,0:T(8,128)(2,1)S(1)}, u32[]{:S(2)}, u32[]{:S(2)}) collective-permute-start(bf16[2,8,3712]{2,1,0:T(8,128)(2,1)S(1)} %get-tuple-element.47), channel_id=1, source_target_pairs={{1,0},{2,1},{3,2},{4,3},{5,4},{6,5},{7,6},{9,8},{10,9},{11,10},{12... | collective-permute-start | bytes 356360 | tf_op jit(solution)/shard_map/ppermute | solution.py:379
  11.6 11.8 %copy-start.6 = (s32[1,320]{1,0:T(1,128)}, s32[1,320]{1,0:T(1,128)S(1)}, u32[]{:S(2)}) copy-start(s32[1,320]{1,0:T(1,128)S(1)} %get-tuple-element.55.src_row) | copy-start | bytes 3844
  28.6 28.8 %collective-permute-start.8 = (f16[2,8,19,16,128]{4,3,2,1,0:T(8,128)(2,1)}, f16[2,8,19,16,128]{4,3,2,1,0:T(8,128)(2,1)S(1)}, u32[]{:S(2)}, u32[]{:S(2)}) collective-permute-start(f16[2,8,19,16,128]{4,3,2,1,0:T(8,128)(2,1)} %fusion), channel_id=1, source_target_pairs={{0,8},{8,0},{16,24},{24,16},{1,9},{9,1},{17,25},{25,17},{2,10},{10... | collective-permute-start | bytes 3735560 | tf_op jit(solution)/shard_map/ppermute | solution.py:305
  56.8 7.3 %collective-permute-start.4 = (f16[2,8,28,16,128]{4,3,2,1,0:T(8,128)(2,1)}, f16[2,8,28,16,128]{4,3,2,1,0:T(8,128)(2,1)S(1)}, u32[]{:S(2)}, u32[]{:S(2)}) collective-permute-start(f16[2,8,28,16,128]{4,3,2,1,0:T(8,128)(2,1)} %pad_maximum_fusion), channel_id=1, source_target_pairs={{0,8},{8,0},{16,24},{24,16},{1,9},{9,1},{17,25},{25,17},{2,10},{10... | collective-permute-start | bytes 5505032 | tf_op jit(solution)/shard_map/ppermute | solution.py:305
  62.3 5.5 %copy-start.4 = (f32[4,8,14,16,128]{4,3,2,1,0:T(8,128)S(1)}, f32[4,8,14,16,128]{4,3,2,1,0:T(8,128)}, u32[]{:S(2)}) copy-start(f32[4,8,14,16,128]{4,3,2,1,0:T(8,128)} %get-tuple-element.22) | copy-start | bytes 11010052
  62.5 5.3 %copy-start = (f32[4,8,14,16,128]{4,3,2,1,0:T(8,128)S(1)}, f32[4,8,14,16,128]{4,3,2,1,0:T(8,128)}, u32[]{:S(2)}) copy-start(f32[4,8,14,16,128]{4,3,2,1,0:T(8,128)} %shard_map.113) | copy-start | bytes 11010052
  62.6 17.0 %collective-permute-start.9 = (f16[8,19,16,128]{3,2,1,0:T(8,128)(2,1)S(1)}, f16[8,19,16,128]{3,2,1,0:T(8,128)(2,1)S(1)}, u32[]{:S(2)}, u32[]{:S(2)}) collective-permute-start(f16[8,19,16,128]{3,2,1,0:T(8,128)(2,1)S(1)} %fusion.9), channel_id=1, source_target_pairs={{0,16},{8,24},{16,0},{24,8},{1,17},{9,25},{17,1},{25,9},{2,18},{10... | collective-permute-start | bytes 1867784 | tf_op jit(solution)/shard_map/ppermute | solution.py:305
  64.1 1.3 copy-start.3
  70.1 4.1 %copy-start.1 = (f32[2,8,14,16,128]{4,3,2,1,0:T(8,128)}, f32[2,8,14,16,128]{4,3,2,1,0:T(8,128)S(1)}, u32[]{:S(2)}) copy-start(f32[2,8,14,16,128]{4,3,2,1,0:T(8,128)S(1)} %get-tuple-element.25) | copy-start | bytes 5505028
  74.3 24.0 %collective-permute-start.5 = (f16[8,28,16,128]{3,2,1,0:T(8,128)(2,1)}, f16[8,28,16,128]{3,2,1,0:T(8,128)(2,1)S(1)}, u32[]{:S(2)}, u32[]{:S(2)}) collective-permute-start(f16[8,28,16,128]{3,2,1,0:T(8,128)(2,1)} %pad_maximum_fusion.1), channel_id=1, source_target_pairs={{0,16},{8,24},{16,0},{24,8},{1,17},{9,25},{17,1},{25,9},{2,18},{10... | collective-permute-start | bytes 2752520 | tf_op jit(solution)/shard_map/ppermute | solution.py:305
  83.4 22.1 %all-to-all-start.1 = ((f16[8,19,16,128]{3,2,1,0:T(8,128)(2,1)}), f16[8,19,16,128]{3,2,1,0:T(8,128)(2,1)S(1)}, u32[]{:S(2)}, u32[]{:S(2)}) async-start(f16[8,19,16,128]{3,2,1,0:T(8,128)(2,1)} %multiply_convert_fusion), calls=%async_computation.1 | async-start | bytes 1245184 | tf_op jit(solution)/shard_map/all_to_all | solution.py:328
  90.4 10.5 %copy-start.2 = (f32[2,8,14,16,128]{4,3,2,1,0:T(8,128)S(1)}, f32[2,8,14,16,128]{4,3,2,1,0:T(8,128)}, u32[]{:S(2)}) copy-start(f32[2,8,14,16,128]{4,3,2,1,0:T(8,128)} %copy-done.1) | copy-start | bytes 5505028
  104.3 8.2 %copy-start.5 = (f32[32,3712]{1,0:T(8,128)S(1)}, f32[32,3712]{1,0:T(8,128)}, u32[]{:S(2)}) copy-start(f32[32,3712]{1,0:T(8,128)} %get-tuple-element.20) | copy-start | bytes 1425412
  105.5 30.7 %all-to-all-start = ((f16[8,28,16,128]{3,2,1,0:T(8,128)(2,1)}), f16[8,28,16,128]{3,2,1,0:T(8,128)(2,1)S(1)}, u32[]{:S(2)}, u32[]{:S(2)}) async-start(f16[8,28,16,128]{3,2,1,0:T(8,128)(2,1)} %pad_maximum_fusion.2), calls=%async_computation | async-start | bytes 1835008 | tf_op jit(solution)/shard_map/all_to_all | solution.py:328
  112.5 30.6 %collective-permute-start.2 = (f32[8,3712]{1,0:T(8,128)S(1)}, f32[8,3712]{1,0:T(8,128)S(1)}, u32[]{:S(2)}, u32[]{:S(2)}) collective-permute-start(f32[8,3712]{1,0:T(8,128)S(1)} %get-tuple-element.40), channel_id=1, source_target_pairs={{0,1},{1,2},{2,3},{3,4},{4,5},{5,6},{6,7},{8,9},{9,10},{10,11},{11... | collective-permute-start | bytes 356360 | tf_op jit(solution)/shard_map/ppermute | solution.py:437
  116.4 26.7 %collective-permute-start.3 = (f32[8,3712]{1,0:T(8,128)S(1)}, f32[8,3712]{1,0:T(8,128)S(1)}, u32[]{:S(2)}, u32[]{:S(2)}) collective-permute-start(f32[8,3712]{1,0:T(8,128)S(1)} %get-tuple-element.41), channel_id=1, source_target_pairs={{1,0},{2,1},{3,2},{4,3},{5,4},{6,5},{7,6},{9,8},{10,9},{11,10},{12... | collective-permute-start | bytes 356360 | tf_op jit(solution)/shard_map/ppermute | solution.py:436
  118.1 20.4 %collective-permute-start.10 = (f32[1,18,16,128]{3,2,1,0:T(8,128)S(1)}, f32[1,18,16,128]{3,2,1,0:T(8,128)S(1)}, u32[]{:S(2)}, u32[]{:S(2)}) collective-permute-start(f32[1,18,16,128]{3,2,1,0:T(8,128)S(1)} %bitcast.185), channel_id=1, source_target_pairs={{0,16},{8,24},{16,0},{24,8},{1,17},{9,25},{17,1},{25,9},{2,18},{10... | collective-permute-start | bytes 442376 | tf_op jit(solution)/shard_map/ppermute | solution.py:341
  137.0 5.9 %collective-permute-start.6 = (f32[1,26,16,128]{3,2,1,0:T(8,128)S(1)}, f32[1,26,16,128]{3,2,1,0:T(8,128)S(1)}, u32[]{:S(2)}, u32[]{:S(2)}) collective-permute-start(f32[1,26,16,128]{3,2,1,0:T(8,128)S(1)} %maximum_bitcast_fusion), channel_id=1, source_target_pairs={{0,16},{8,24},{16,0},{24,8},{1,17},{9,25},{17,1},{25,9},{2,18},{10... | collective-permute-start | bytes 638984 | tf_op jit(solution)/shard_map/ppermute | solution.py:341
  138.6 5.1 %collective-permute-start.11 = (f32[2,18,16,128]{3,2,1,0:T(8,128)S(1)}, f32[2,18,16,128]{3,2,1,0:T(8,128)S(1)}, u32[]{:S(2)}, u32[]{:S(2)}) collective-permute-start(f32[2,18,16,128]{3,2,1,0:T(8,128)S(1)} %pad_maximum_fusion.6), channel_id=1, source_target_pairs={{0,8},{8,0},{16,24},{24,16},{1,9},{9,1},{17,25},{25,17},{2,10},{10... | collective-permute-start | bytes 884744 | tf_op jit(solution)/shard_map/ppermute | solution.py:341
  143.0 2.1 %collective-permute-start.7 = (f32[2,26,16,128]{3,2,1,0:T(8,128)S(1)}, f32[2,26,16,128]{3,2,1,0:T(8,128)S(1)}, u32[]{:S(2)}, u32[]{:S(2)}) collective-permute-start(f32[2,26,16,128]{3,2,1,0:T(8,128)S(1)} %pad_maximum_fusion.5), channel_id=1, source_target_pairs={{0,8},{8,0},{16,24},{24,16},{1,9},{9,1},{17,25},{25,17},{2,10},{10... | collective-permute-start | bytes 1277960 | tf_op jit(solution)/shard_map/ppermute | solution.py:341

commit v2 on v1

v2 whole, which is shorter than its diff:
```python
import jax
import jax.numpy as jnp
from jax import lax
from jax.experimental import pallas as pl
from jax.experimental.pallas import tpu as pltpu
from jax.sharding import PartitionSpec as P


HEADS = 8
LEVELS = 7
ROWS = 16
LANES = 128
F32 = jnp.float32
BF16 = jnp.bfloat16
F16 = jnp.float16


def mm(first, second):
    return lax.dot_general(first, second, (((1,), (0,)), ((), ())), preferred_element_type=F32)


def mm_t(first, second):
    return lax.dot_general(first, second, (((1,), (1,)), ((), ())), preferred_element_type=F32)


def pieces(value, count):
    out = []
    rest = value
    for _ in range(count):
        part = rest.astype(BF16)
        out.append(part)
        rest = rest - part.astype(F32)
    return out


def one_hot(index, shape, dim):
    count = lax.broadcasted_iota(jnp.int32, shape, dim).astype(F32)
    return jnp.where(count == index, 1.0, 0.0).astype(F32)


def chunks(width, step=256):
    return [(lo, min(lo + step, width)) for lo in range(0, width, step)]


def head_mask(channels, heads):
    size = channels // heads
    row = lax.broadcasted_iota(jnp.int32, (channels, channels), 0) // size
    col = lax.broadcasted_iota(jnp.int32, (channels, channels), 1) // size
    return jnp.where(row == col, 1.0, 0.0).astype(BF16)


def head_sum(value, channels, heads):
    mask = head_mask(channels, heads)
    total = None
    for part in pieces(value, 3):
        term = mm(part, mask)
        total = term if total is None else total + term
    return total


class Tiles:
    def __init__(self, rows, cols, graph, parts, spare=0):
        self.rows = rows // graph
        self.cols = cols
        self.graph = graph
        self.down = -(-self.rows // ROWS)
        self.across = cols // LANES
        self.count = self.down * self.across
        self.parts = parts
        self.each = -(-self.count // parts) + spare
        self.block = (graph, self.each + 1, ROWS, LANES)

    def scratch(self):
        return pltpu.VMEM((2, self.parts // 2) + self.block, F32)

    def store(self, ref, flip, block, lo):
        half = self.parts // 2
        for g in range(self.graph):
            for i in range(self.down):
                r0 = i * ROWS
                r1 = min(r0 + ROWS, self.rows)
                for j in range(block.shape[1] // LANES):
                    tile = i * self.across + lo // LANES + j
                    q = tile // self.each
                    ref[flip ^ (q // half), q % half, g, tile % self.each, : r1 - r0, :] = block[
                        g * self.rows + r0 : g * self.rows + r1, j * LANES : (j + 1) * LANES
                    ]

    def blank(self, ref, flip):
        half = self.parts // 2
        for tile in range(self.count, self.parts * self.each):
            q = tile // self.each
            for g in range(self.graph):
                ref[flip ^ (q // half), q % half, g, tile % self.each] = jnp.zeros(
                    (ROWS, LANES), F32
                )


def is_level(value):
    axis = value.ndim - 3
    return lax.broadcasted_iota(jnp.int32, value.shape, axis) == value.shape[axis] - 1


def unit_of(value, rows):
    tile = value[..., -1:, :rows, :].astype(F32)
    tile = tile * tile
    tile = tile * tile
    return jnp.broadcast_to(tile * tile, value.shape)


def encode(value, rows):
    return jnp.where(is_level(value), value, value * (32768.0 / unit_of(value, rows))).astype(F16)


def decode(message, rows):
    value = message.astype(F32)
    return jnp.where(is_level(value), value, value * (unit_of(message, rows) * (1.0 / 32768.0)))


def combine(first, second):
    return jnp.where(is_level(first), jnp.maximum(first, second), first + second)


def level_of(bound):
    level = jnp.full(bound.shape, 2.0**-12, F32)
    for k in range(-11, 9):
        level = jnp.where(bound > 2.0 ** (8 * (k - 1)), 2.0**k, level)
    return level


def top(value):
    return jnp.max(jnp.max(jnp.abs(value), axis=1, keepdims=True), axis=0, keepdims=True)


def wgrad_pair(tiles, ref, flip, xst, dref, width):
    turned = xst.T
    for lo, hi in chunks(2 * width):
        if hi <= width:
            upper = dref[:, lo:hi]
            lower = dref[:, width + lo : width + hi]
        elif lo >= width:
            upper = dref[:, lo:hi]
            lower = -dref[:, lo - width : hi - width]
        else:
            upper = dref[:, lo:hi]
            lower = jnp.concatenate([dref[:, width + lo :], -dref[:, : hi - width]], 1)
        tiles.store(ref, flip, mm(turned, jnp.concatenate([upper, lower], 0)), lo)
    tiles.blank(ref, flip)


def hand_out(tiles, full, level, keep, send):
    tail = jnp.broadcast_to(level, (ROWS, LANES))
    for k, out in enumerate((keep, send)):
        for q in range(tiles.parts // 2):

            def step(g, carry):
                out[q, g, : tiles.each] = full[k, q, g, : tiles.each]
                out[q, g, tiles.each] = tail
                return carry

            lax.fori_loop(0, tiles.graph, step, 0)


def make_first(channels, heads, tiles, size, marks):
    z, w1, w2 = LEVELS * channels, (LEVELS - 1) * channels, (LEVELS - 2) * channels
    b1 = z + 2 * w1

    def body(
        me, table, cols, wz,
        x1, d1, x2, d2, gate_out, cot_out, feat_zero, level_out, keep, send, *rest,
    ):
        flags, full = rest[:-1], rest[-1]
        for flag, (axis, bit) in zip(flags, marks):
            value = (me[0 if axis == "dp" else 1] >> bit) & 1
            flag[...] = jnp.full((ROWS, LANES), value, jnp.int32).astype(F32)
        count = cols.shape[0]
        atoms = table.shape[1]
        flip = me[0] & 1
        feat = table.at[0]
        cot = table.at[1]
        feat_zero[...] = feat[:, :z]
        pick = one_hot(cols[:, 4:5], (count, atoms), 1).astype(BF16)
        aim = one_hot(cols[:, 5:6], (count, atoms), 1).astype(BF16)
        scale = 1.0 / (channels // heads) ** 0.5
        logits = mm(feat[:, :z], wz[...])
        gate_node = jax.nn.sigmoid(head_sum(logits, channels, heads) * scale)
        gate = sum(mm(pick, part) for part in pieces(gate_node, 3))
        gate_out[...] = gate
        cot_out[...] = mm(aim, cot[...]).astype(BF16)

        def turn(lo, width, cosine, sine, x, d):
            for j in range(width // channels):
                at = slice(lo + j * channels, lo + (j + 1) * channels)
                bt = slice(lo + width + j * channels, lo + width + (j + 1) * channels)
                p = mm(pick, feat[:, at])
                n = mm(pick, feat[:, bt])
                to = slice(j * channels, (j + 1) * channels)
                x[:count, to] = (cosine * p - sine * n).astype(BF16)
                x[count:, to] = (sine * p + cosine * n).astype(BF16)
                p = cot_out[:, at].astype(F32)
                n = cot_out[:, bt].astype(F32)
                d[:, to] = (gate * (cosine * p - sine * n)).astype(BF16)
                d[:, width + j * channels : width + (j + 1) * channels] = (
                    gate * (sine * p + cosine * n)
                ).astype(BF16)

        turn(z, w1, cols[:, 0:1], cols[:, 1:2], x1, d1)
        turn(b1, w2, cols[:, 2:3], cols[:, 3:4], x2, d2)
        wgrad_pair(tiles, full, flip, x1[...], d1, w1)
        bound = top(feat[...].astype(F32)) * top(cot[...].astype(F32)) * (4.1 * count * size * tiles.graph)
        level = level_of(bound)
        level_out[...] = jnp.broadcast_to(level, level_out.shape)
        hand_out(tiles, full, level, keep, send)

    return body


def make_second(channels, tiles):
    w2 = (LEVELS - 2) * channels

    def body(me, x2, d2, level_in, keep, send, full):
        wgrad_pair(tiles, full, me[0] & 1, x2[...], d2, w2)
        hand_out(tiles, full, level_in[0:1, 0:1], keep, send)

    return body


def make_forward(channels, heads):
    z, w1, w2 = LEVELS * channels, (LEVELS - 1) * channels, (LEVELS - 2) * channels
    b1 = z + 2 * w1

    def body(
        feat, cols, rows, x1, x2, gate_in, cot, wz, wo, wt, sums
    ):
        count = cols.shape[0]
        atoms = feat.shape[0]
        gate = gate_in[...]
        pick = one_hot(cols[:, 4:5], (count, atoms), 1).astype(BF16)
        place = one_hot(rows[4:5, :], (atoms, count), 0)
        scale = 1.0 / (channels // heads) ** 0.5

        dgate = jnp.zeros((count, channels), F32)
        node_zero = mm(feat[:, :z], wz[...])
        wide = jnp.concatenate(pieces(node_zero, 3), 0)
        pick_wide = jnp.concatenate([pick, pick, pick], 1)
        for lo, hi in chunks(z):
            out = mm(pick_wide, wide[:, lo:hi])
            term = cot[:, lo:hi].astype(F32) * out
            for k in range((hi - lo) // channels):
                dgate = dgate + term[:, k * channels : (k + 1) * channels]

        def forward(dgate, lo0, width, cosine, sine, x, w):
            rp = x[:count, :]
            rn = x[count:, :]
            for lo, hi in chunks(width):
                wa = w[:, lo:hi]
                wb = w[:, width + lo : width + hi]
                out_p = mm(rp, wa) - mm(rn, wb)
                out_n = mm(rp, wb) + mm(rn, wa)
                p = cot[:, lo0 + lo : lo0 + hi].astype(F32)
                n = cot[:, lo0 + width + lo : lo0 + width + hi].astype(F32)
                term = (cosine * p - sine * n) * out_p + (sine * p + cosine * n) * out_n
                for k in range((hi - lo) // channels):
                    dgate = dgate + term[:, k * channels : (k + 1) * channels]
            return dgate

        dgate = forward(dgate, z, w1, cols[:, 0:1], cols[:, 1:2], x1, wo)
        dgate = forward(dgate, b1, w2, cols[:, 2:3], cols[:, 3:4], x2, wt)
        dlogit = head_sum(dgate, channels, heads) * gate * (1.0 - gate) * scale
        dz = []
        for j in range(LEVELS):
            block = gate * cot[:, j * channels : (j + 1) * channels].astype(F32)
            if j == 0:
                block = block + dlogit
            dz.append(block.astype(BF16))
        dz = jnp.concatenate(dz, 1)

        node_dz = mm(place.astype(BF16), dz)
        parts = pieces(node_dz, 3)
        sums[0] = feat[...]
        for k in range(3):
            sums[k + 1] = parts[k]

    return body


def make_backward(channels):
    z, w1, w2 = LEVELS * channels, (LEVELS - 1) * channels, (LEVELS - 2) * channels
    b1 = z + 2 * w1

    def body(sums, rows, d1, d2, wz, wo, wt, nodes):
        count = rows.shape[1]
        atoms = sums.shape[1]
        place = one_hot(rows[4:5, :], (atoms, count), 0)
        stack = jnp.concatenate([sums[k] for k in (1, 2, 3)], 0)
        back = mm_t(stack, wz[...])
        nodes[:, :z] = back[:atoms] + back[atoms : 2 * atoms] + back[2 * atoms :]

        def backward(lo0, width, cosine, sine, d, w):
            terms = pieces(place * cosine, 2) + pieces(place * sine, 2)
            spread = mm(jnp.concatenate(terms, 0), d[...])
            by_c = spread[:atoms] + spread[atoms : 2 * atoms]
            by_s = spread[2 * atoms : 3 * atoms] + spread[3 * atoms :]
            t1 = by_c[:, :width] + by_s[:, width:]
            t2 = by_c[:, width:] - by_s[:, :width]
            plus = pieces(jnp.concatenate([t1, t2], 1), 2)
            minus = pieces(jnp.concatenate([t2, -t1], 1), 2)
            back = mm_t(jnp.concatenate(plus + minus, 0), w[...])
            nodes[:, lo0 : lo0 + width] = back[:atoms] + back[atoms : 2 * atoms]
            nodes[:, lo0 + width : lo0 + 2 * width] = (
                back[2 * atoms : 3 * atoms] + back[3 * atoms :]
            )

        backward(z, w1, rows[0:1, :], rows[1:2, :], d1, wo)
        backward(b1, w2, rows[2:3, :], rows[3:4, :], d2, wt)

    return body


def slot_of(me, size):
    bits = size.bit_length() - 1
    return sum(((me >> k) & 1) << (bits - 1 - k) for k in range(bits))


def make_zero(tiles, size):
    def body(me, *refs):
        sums, out, full = refs[:size], refs[size], refs[size + 1]
        left = [ref[0].astype(F32).T.astype(BF16) for ref in sums]
        left = jnp.concatenate([part for part in left for _ in range(3)], 1)
        right = jnp.concatenate([ref[k] for ref in sums for k in (1, 2, 3)], 0)
        for lo, hi in chunks(tiles.cols):
            tiles.store(full, 0, mm(left, right[:, lo:hi]), lo)
        tiles.blank(full, 0)
        rows = size * sums[0].shape[1]
        high = jnp.concatenate([ref[1].astype(F32) for ref in sums], 0)
        feats = jnp.concatenate([ref[0].astype(F32) for ref in sums], 0)
        level = level_of(top(feats) * top(high) * (1.02 * rows * tiles.graph))
        slot = slot_of(me[0], size)
        half = size // 2

        def step(g, carry):
            out[g, : tiles.each] = full[slot // half, slot % half, g, : tiles.each]
            out[g, tiles.each] = jnp.broadcast_to(level, (ROWS, LANES))
            return carry

        lax.fori_loop(0, tiles.graph, step, 0)

    return body


def make_output(tiles, size):
    def body(me, *refs):
        parts, out, flat = refs[:size], refs[size], refs[size + 1]
        for mask in range(size):
            flat[slot_of(me[0] ^ mask, size)] = parts[mask][...] * (1.0 / size)
        for tile in range(tiles.count):
            i, j = tile // tiles.across, tile % tiles.across
            r0, r1 = i * ROWS, min((i + 1) * ROWS, tiles.rows)
            out[r0:r1, j * LANES : (j + 1) * LANES] = flat[
                tile // tiles.each, tile % tiles.each, : r1 - r0
            ]

    return body


def call(body, outs, flops, mib, *args, scratch=(), scalars=1):
    vmem = pl.BlockSpec(memory_space=pltpu.VMEM)
    smem = pl.BlockSpec(memory_space=pltpu.SMEM)
    return pl.pallas_call(
        body,
        out_shape=outs,
        in_specs=[smem] * scalars + [vmem] * (len(args) - scalars),
        out_specs=jax.tree.map(lambda _: vmem, outs),
        scratch_shapes=scratch,
        compiler_params=pltpu.CompilerParams(vmem_limit_bytes=(mib << 20) + sum(ref.get_array_aval().size * 4 for ref in scratch)),
        cost_estimate=pl.CostEstimate(flops=flops, bytes_accessed=1 << 22, transcendentals=0),
    )(*args)


def swap(value, bit, axis="dp"):
    size = lax.axis_size(axis)
    return lax.ppermute(value, axis, [(i, i ^ (1 << bit)) for i in range(size)])


def shards(node_feats, node_cotan, source, target, angle, w_zero, w_one, w_two):
    atom_count = node_feats.shape[1]
    row_width = node_feats.shape[2]
    channels = row_width // 29
    edges = source.shape[1]
    graph = lax.axis_size("graph")
    size = lax.axis_size("dp")
    bits = size.bit_length() - 1
    position = lax.axis_index("graph")
    me = jnp.stack([lax.axis_index("dp"), position])
    reach = atom_count // 2
    atoms = atom_count + 2 * reach
    z, w1, w2 = LEVELS * channels, (LEVELS - 1) * channels, (LEVELS - 2) * channels
    shape = jax.ShapeDtypeStruct

    up = [(i, i + 1) for i in range(graph - 1)]
    down = [(i + 1, i) for i in range(graph - 1)]
    feats, cots = node_feats[0], node_cotan[0]
    before = lax.ppermute(
        jnp.stack([feats[atom_count - reach :], cots[atom_count - reach :]], 0), "graph", up
    )
    after = lax.ppermute(jnp.stack([feats[:reach], cots[:reach]], 0), "graph", down)
    first_atom = position * atom_count - reach
    src = (source[0] - first_atom).astype(F32)
    dst = (target[0] - first_atom).astype(F32)
    phases = angle[0]
    twice = 2.0 * phases
    trig = [jnp.cos(phases), jnp.sin(phases), jnp.cos(twice), jnp.sin(twice)]
    rows = jnp.stack(trig + [src, dst, src, dst], 0)
    cols = rows.T
    table = jnp.concatenate([before, jnp.stack([feats, cots], 0), after], 1)

    t_one = Tiles(*w_one.shape, graph, size)
    t_two = Tiles(*w_two.shape, graph, size)
    t_zero = Tiles(*w_zero.shape, graph, size, spare=1)

    def halves(tiles, parts):
        return (shape((parts,) + tiles.block, F32), shape((parts,) + tiles.block, F32))

    marks = [("dp", k) for k in range(bits)]
    marks += [("graph", k) for k in reversed(range(graph.bit_length() - 1))]
    x1, d1, x2, d2, gate, cot, feat_zero, level, keep_one, send_one, *flags = call(
        make_first(channels, HEADS, t_one, size, marks),
        (
            shape((2 * edges, w1), BF16),
            shape((edges, 2 * w1), BF16),
            shape((2 * edges, w2), BF16),
            shape((edges, 2 * w2), BF16),
            shape((edges, channels), F32),
            shape((edges, row_width), BF16),
            shape((atoms, z), BF16),
            shape((8, LANES), F32),
        )
        + halves(t_one, size // 2)
        + tuple(shape((ROWS, LANES), F32) for _ in marks),
        3_000_000_000,
        14,
        me,
        table,
        cols,
        w_zero[:, :channels],
        scratch=(t_one.scratch(),),
    )

    flags = dict(zip(marks, flags))

    def halving(value, left, steps, rows=ROWS):
        left = list(left)
        value = value.reshape((2,) * len(left) + value.shape[-3:])
        for axis, bit in steps:
            high = flags[axis, bit] > 0.5
            at = left.index((axis, bit))
            left.pop(at)
            low_half = lax.index_in_dim(value, 0, at, False)
            high_half = lax.index_in_dim(value, 1, at, False)
            send = encode(jnp.where(high, low_half, high_half), rows)
            got = swap(send, bit, axis)
            value = combine(jnp.where(high, high_half, low_half), decode(got, rows))
        return value

    def spread(tiles, value):
        parts = {0: value[: tiles.each]}
        for bit in reversed(range(bits)):
            parts.update({m | (1 << bit): swap(v, bit) for m, v in list(parts.items())})
        return call(
            make_output(tiles, size),
            shape((tiles.rows, tiles.cols), F32),
            50_000_000,
            4,
            me,
            *[parts[m] for m in range(size)],
            scratch=(pltpu.VMEM((size, tiles.each, ROWS, LANES), F32),),
        )

    keep_two, send_two = call(
        make_second(channels, t_two),
        halves(t_two, size // 2),
        1_200_000_000,
        6,
        me,
        x2,
        d2,
        level,
        scratch=(t_two.scratch(),),
    )
    one = combine(keep_one, swap(send_one, 0))
    two = combine(keep_two, swap(send_two, 0))
    over_dp = marks[1:bits]
    over_graph = list(reversed(marks[bits:]))
    one = halving(one, marks[1:], over_graph[:-1] + over_dp + over_graph[-1:])
    two = halving(two, marks[1:], over_dp + over_graph, rows=1)

    sums = call(
        make_forward(channels, HEADS),
        shape((4, atoms, z), BF16),
        4_000_000_000,
        8,
        feat_zero,
        cols,
        rows,
        x1,
        x2,
        gate,
        cot,
        w_zero,
        w_one,
        w_two,
        scalars=0,
    )
    nodes = call(
        make_backward(channels),
        shape((atoms, row_width), F32),
        2_000_000_000,
        8,
        sums,
        rows,
        d1,
        d2,
        w_zero,
        w_one,
        w_two,
        scalars=0,
    )

    from_next = lax.ppermute(nodes[:reach], "graph", down)
    from_prev = lax.ppermute(nodes[atom_count + reach :], "graph", up)
    owned = nodes[reach : reach + atom_count]
    owned = owned + jnp.concatenate([from_prev, from_next], 0)
    grad_nodes = owned.astype(BF16)[None]

    parts = {0: sums}
    for bit in reversed(range(bits)):
        parts.update({m | (1 << bit): swap(v, bit) for m, v in list(parts.items())})
    zero = call(
        make_zero(t_zero, size),
        shape(t_zero.block, F32),
        1_000_000_000,
        8,
        me,
        *[parts[m] for m in range(size)],
        scratch=(t_zero.scratch(),),
    )
    zero = halving(zero, marks[bits:], over_graph[1::-1] + over_graph[2:])
    grad_one = spread(t_one, one)
    grad_two = spread(t_two, two)
    grad_zero = spread(t_zero, zero)
    return (grad_nodes, grad_zero, grad_one, grad_two)


def solution(mesh):
    return jax.shard_map(
        shards,
        mesh=mesh,
        in_specs=(
            P("dp", "graph", None),
            P("dp", "graph", None),
            P("dp", "graph"),
            P("dp", "graph"),
            P("dp", "graph"),
            P(),
            P(),
            P(),
        ),
        out_specs=(P("dp", "graph", None), P("graph", None), P("graph", None), P("graph", None)),
        check_vma=False,
    )
```

time: 148 us -> 123 us (0.83)
  waiting for transfers between devices: 33.2 us -> 52.3 us
  local copies, waits for them, and re-layouts: 20.8 us -> 2.58 us
  other arithmetic: 24.2 us -> 7.51 us
  between operations: 11.7 us -> 1.21 us
  starting transfers between devices: 31.4 us -> 37.4 us
  Pallas kernels: 26.1 us -> 21.9 us
    ppermute x10 -> x27, waiting for transfers between devices: 16.6 us -> 52.3 us  [the longest x25 51.1 us: swap(): return lax.ppermute(value, axis, [(i, i ^ 1 << bit) for i in range(size)])]
    ppermute x10 -> x27, starting transfers between devices: 12.2 us -> 30.9 us  [the longest x25 24.1 us: swap(): return lax.ppermute(value, axis, [(i, i ^ 1 << bit) for i in range(size)])]
    all_to_all x2 -> x0, waiting for transfers between devices: 16.5 us -> none  [over_graph(): got = lax.all_to_all(sent, 'graph', 0, 0, tiled=True)]
    all_to_all x2 -> x0, starting transfers between devices: 13.9 us -> none  [over_graph(): got = lax.all_to_all(sent, 'graph', 0, 0, tiled=True)]
    convert_element_type x15 -> x12, other arithmetic: 9.42 us -> 2.09 us  [the longest x11 1.39 us: encode(): jnp.where(is_level(value), value, value * (32768.0 / unit_of(value, rows)))]
    slice x16 -> x3, local copies, waits for them, and re-layouts: 7.77 us -> 1.34 us  [the longest x1 0.97 us: shards(): feats[atom_count - reach:]]
    concatenate x7 -> x1, other arithmetic: 5.37 us -> 0.05 us  [shards(): table = jnp.concatenate([before, jnp.stack([feats, cots], 0), after], 1)]
    unnamed x18 -> x10, local copies, waits for them, and re-layouts: 4.66 us -> 0.03 us
  transfers between devices with their start and end apart: 14 -> 29, of which waited for: 4 -> 14; matrix products, arithmetic and copies ran while one was open for 23% -> 7% of each run, Pallas kernels for 13% -> 8%
where the time goes in v2:
time: 123 us
  waiting for transfers between devices  52.3 us (43%)
  starting transfers between devices  37.4 us (30%)
  Pallas kernels  21.9 us (18%)
  other arithmetic  7.51 us (6%)
  local copies, waits for them, and re-layouts  2.58 us (2%)
    ppermute x25, waiting for transfers between devices, swap(): return lax.ppermute(value, axis, [(i, i ^ 1 << bit) for i in range(size)])  51.1 us
    ppermute x25, starting transfers between devices, swap(): return lax.ppermute(value, axis, [(i, i ^ 1 << bit) for i in range(size)])  24.1 us
    pallas_call x8, Pallas kernels, call(): pl.pallas_call(body, out_shape=outs, in_specs=[smem] * scalars + [vmem] *...  21.9 us
    ppermute x1, starting transfers between devices, shards(): lax.ppermute(jnp.stack([feats[atom_count - reach:], cots[atom_count - rea...  5.53 us
    ppermute x1, starting transfers between devices, shards(): from_prev = lax.ppermute(nodes[atom_count + reach:], 'graph', up)  5.2 us
    select_n x12, other arithmetic, combine(): jnp.where(is_level(first), jnp.maximum(first, second), first + second)  2.81 us
  transfers between devices with their start and end apart: 29, of which 14 were waited for; matrix products, arithmetic and copies ran while one was open for 7% of the time, Pallas kernels for 8%

profile of v2, /device:TPU:0, one launch (start us, length us, event | category | flops | bytes accessed | tf_op | source)
XLA Modules:
  0.0 122.9 jit_solution(8733148759179613736)
XLA Ops:
  1.6 1.3 %collective-permute-start.1 = (bf16[2,8,3712]{2,1,0:T(8,128)(2,1)S(1)}, bf16[2,8,3712]{2,1,0:T(8,128)(2,1)S(1)}, u32[]{:S(2)}, u32[]{:S(2)}) collective-permute-start(bf16[2,8,3712]{2,1,0:T(8,128)(2,1)S(1)} %pad_maximum_fusion.2), channel_id=1, source_target_pairs={{1,0},{2,1},{3,2},{4,3},{5,4},{6,5},{7,6},{9,8},{10,9},{11,10},{12... | collective-permute-start | bytes 356360 | tf_op jit(solution)/shard_map/ppermute | solution.py:406
  3.0 5.5 %collective-permute-start = (bf16[2,8,3712]{2,1,0:T(8,128)(2,1)S(1)}, bf16[2,8,3712]{2,1,0:T(8,128)(2,1)S(1)}, u32[]{:S(2)}, u32[]{:S(2)}) collective-permute-start(bf16[2,8,3712]{2,1,0:T(8,128)(2,1)S(1)} %pad_maximum_fusion.1), channel_id=1, source_target_pairs={{0,1},{1,2},{2,3},{3,4},{4,5},{5,6},{6,7},{8,9},{9,10},{10,11},{11... | collective-permute-start | bytes 356360 | tf_op jit(solution)/shard_map/ppermute | solution.py:403
  12.6 5.8 %shard_map.111 = (bf16[640,768]{1,0:T(8,128)(2,1)S(1)}, bf16[320,1536]{1,0:T(8,128)(2,1)S(1)}, bf16[640,640]{1,0:T(8,128)(2,1)S(1)}, bf16[320,1280]{1,0:T(8,128)...) custom-call(s32[2]{0:T(128)S(1)} %pad_add_fusion.me, ...), custom_call_target="tpu_custom_call" | custom-call | flops 3000000000 | bytes 4194304 | tf_op jit(solution)/shard_map/pallas_call | solution.py:369
  18.4 4.7 %shard_map.112.sums.refs_0_ = bf16[4,32,896]{2,1,0:T(8,128)(2,1)S(1)} custom-call(bf16[32,896]{1,0:T(8,128)(2,1)S(1)} %get-tuple-element.20.feat, f32[320,8]{1,0:T(8,128)S(1)} %copy.14.cols, f32[8,320]{1,0:T(8,128)S(1)} %stack.39.rows, bf16[640,768]{1,0:T(8,128)(2,1)S(1)} %get-tuple-element.21.x1, bf16[640,640]{1,0:T(8,128)(2,1)S(1)} %get-tuple-element.22.x2, ...), custom_call_target="tpu_custom_call" | custom-call | flops 4000000000 | bytes 4194304 | tf_op jit(solution)/shard_map/pallas_call | solution.py:369
  23.2 1.6 %collective-permute-start.5 = (bf16[4,32,896]{2,1,0:T(8,128)(2,1)S(1)}, bf16[4,32,896]{2,1,0:T(8,128)(2,1)S(1)}, u32[]{:S(2)}, u32[]{:S(2)}) collective-permute-start(bf16[4,32,896]{2,1,0:T(8,128)(2,1)S(1)} %shard_map.112.sums.refs_0_), channel_id=1, source_target_pairs={{0,16},{8,24},{16,0},{24,8},{1,17},{9,25},{17,1},{25,9},{2,18},{10... | collective-permute-start | bytes 688136 | tf_op jit(solution)/shard_map/ppermute | solution.py:382
  24.7 2.2 %shard_map.113 = f32[32,3712]{1,0:T(8,128)S(1)} custom-call(bf16[4,32,896]{2,1,0:T(8,128)(2,1)S(1)} %shard_map.112.sums.refs_0_, f32[8,320]{1,0:T(8,128)S(1)} %stack.39.rows, bf16[320,1536]{1,0:T(8,128)(2,1)S(1)} %get-tuple-element.25.d1, bf16[320,1280]{1,0:T(8,128)(2,1)S(1)} %get-tuple-element.26.d2, bf16[896,896]{1,0:T(8,128)(2,1)S(1)} %copy-done.1, ...), custom_call_target="tpu_custom_call" | custom-call | flops 2000000000 | bytes 4194304 | tf_op jit(solution)/shard_map/pallas_call | solution.py:369
  28.3 5.2 %collective-permute-start.2 = (f32[8,3712]{1,0:T(8,128)S(1)}, f32[8,3712]{1,0:T(8,128)S(1)}, u32[]{:S(2)}, u32[]{:S(2)}) collective-permute-start(f32[8,3712]{1,0:T(8,128)S(1)} %get-tuple-element.40), channel_id=1, source_target_pairs={{0,1},{1,2},{2,3},{3,4},{4,5},{5,6},{6,7},{8,9},{9,10},{10,11},{11... | collective-permute-start | bytes 356360 | tf_op jit(solution)/shard_map/ppermute | solution.py:530
  33.6 1.4 %collective-permute-done.6.refs_3_ = bf16[4,32,896]{2,1,0:T(8,128)(2,1)S(1)} collective-permute-done((bf16[4,32,896]{2,1,0:T(8,128)(2,1)S(1)}, bf16[4,32,896]{2,1,0:T(8,128)(2,1)S(1)}, u32[]{:S(2)}, u32[]{:S(2)}) %collective-permute-start.6) | collective-permute-done | bytes 229408 | tf_op jit(solution)/shard_map/ppermute | solution.py:382
  35.1 2.4 %shard_map.114 = f32[8,15,16,128]{3,2,1,0:T(8,128)S(1)} custom-call(s32[2]{0:T(128)S(1)} %pad_add_fusion.me, bf16[4,32,896]{2,1,0:T(8,128)(2,1)S(1)} %shard_map.112.sums.refs_0_, bf16[4,32,896]{2,1,0:T(8,128)(2,1)S(1)} %collective-permute-done.4.refs_1_, bf16[4,32,896]{2,1,0:T(8,128)(2,1)S(1)} %collective-permute-done.5.refs_2_, ...), custom_call_target="tpu_custom_call" | custom-call | flops 1000000000 | bytes 4194304 | tf_op jit(solution)/shard_map/pallas_call | solution.py:369
  37.7 2.8 %collective-permute-start.7 = (f16[2,2,15,16,128]{4,3,2,1,0:T(8,128)(2,1)S(1)}, f16[2,2,15,16,128]{4,3,2,1,0:T(8,128)(2,1)S(1)}, u32[]{:S(2)}, u32[]{:S(2)}) collective-permute-start(f16[2,2,15,16,128]{4,3,2,1,0:T(8,128)(2,1)S(1)} %fusion.5), channel_id=1, source_target_pairs={{0,2},{1,3},{2,0},{3,1},{4,6},{5,7},{6,4},{7,5},{8,10},{9,11},{10,... | collective-permute-start | bytes 737288 | tf_op jit(solution)/shard_map/ppermute | solution.py:382
  40.5 2.6 %shard_map.117 = (f32[2,8,14,16,128]{4,3,2,1,0:T(8,128)S(1)}, f32[2,8,14,16,128]{4,3,2,1,0:T(8,128)S(1)}) custom-call(s32[2]{0:T(128)S(1)} %pad_add_fusion.me, bf16[640,640]{1,0:T(8,128)(2,1)S(1)} %get-tuple-element.22.x2, bf16[320,1280]{1,0:T(8,128)(2,1)S(1)} %get-tuple-element.26.d2, f32[8,128]{1,0:T(8,128)S(1)} %get-tuple-element.33.level_in), custom_call_target="tpu_custom_call" | custom-call | flops 1200000000 | bytes 4194304 | tf_op jit(solution)/shard_map/pallas_call | solution.py:369
  43.7 3.0 %collective-permute-done.7 = f16[2,2,15,16,128]{4,3,2,1,0:T(8,128)(2,1)S(1)} collective-permute-done((f16[2,2,15,16,128]{4,3,2,1,0:T(8,128)(2,1)S(1)}, f16[2,2,15,16,128]{4,3,2,1,0:T(8,128)(2,1)S(1)}, u32[]{:S(2)}, u32[]{:S(2)}) %collective-permute-start.7) | collective-permute-done | bytes 245792 | tf_op jit(solution)/shard_map/ppermute | solution.py:382
  47.1 2.0 %collective-permute-start.8 = (f16[2,15,16,128]{3,2,1,0:T(8,128)(2,1)S(1)}, f16[2,15,16,128]{3,2,1,0:T(8,128)(2,1)S(1)}, u32[]{:S(2)}, u32[]{:S(2)}) collective-permute-start(f16[2,15,16,128]{3,2,1,0:T(8,128)(2,1)S(1)} %fusion.11), channel_id=1, source_target_pairs={{0,1},{1,0},{2,3},{3,2},{4,5},{5,4},{6,7},{7,6},{8,9},{9,8},{10,11... | collective-permute-start | bytes 368648 | tf_op jit(solution)/shard_map/ppermute | solution.py:382
  49.1 3.0 %collective-permute-done.8 = f16[2,15,16,128]{3,2,1,0:T(8,128)(2,1)S(1)} collective-permute-done((f16[2,15,16,128]{3,2,1,0:T(8,128)(2,1)S(1)}, f16[2,15,16,128]{3,2,1,0:T(8,128)(2,1)S(1)}, u32[]{:S(2)}, u32[]{:S(2)}) %collective-permute-start.8) | collective-permute-done | bytes 122912 | tf_op jit(solution)/shard_map/ppermute | solution.py:382
  53.8 2.8 %collective-permute-start.9 = (f16[15,16,128]{2,1,0:T(8,128)(2,1)S(1)}, f16[15,16,128]{2,1,0:T(8,128)(2,1)S(1)}, u32[]{:S(2)}, u32[]{:S(2)}) collective-permute-start(f16[15,16,128]{2,1,0:T(8,128)(2,1)S(1)} %fusion.17), channel_id=1, source_target_pairs={{0,4},{1,5},{2,6},{3,7},{4,0},{5,1},{6,2},{7,3},{8,12},{9,13},{10,... | collective-permute-start | bytes 184328 | tf_op jit(solution)/shard_map/ppermute | solution.py:382
  56.7 2.3 %collective-permute-done.9 = f16[15,16,128]{2,1,0:T(8,128)(2,1)S(1)} collective-permute-done((f16[15,16,128]{2,1,0:T(8,128)(2,1)S(1)}, f16[15,16,128]{2,1,0:T(8,128)(2,1)S(1)}, u32[]{:S(2)}, u32[]{:S(2)}) %collective-permute-start.9) | collective-permute-done | bytes 61472 | tf_op jit(solution)/shard_map/ppermute | solution.py:382
  59.0 5.0 %collective-permute-done.22 = f16[2,2,2,14,16,128]{5,4,3,0,1,2:T(8,128)(2,1)S(1)} collective-permute-done((f16[2,2,2,14,16,128]{5,4,3,0,1,2:T(8,128)(2,1)S(1)}, f16[2,2,2,14,16,128]{5,4,3,0,1,2:T(8,128)(2,1)S(1)}, u32[]{:S(2)}, u32[]{:S(2)}) %collective-permute-start.22) | collective-permute-done | bytes 458784 | tf_op jit(solution)/shard_map/ppermute | solution.py:382
  64.6 1.7 %collective-permute-start.23 = (f16[2,2,14,16,128]{4,3,2,0,1:T(8,128)(2,1)S(1)}, f16[2,2,14,16,128]{4,3,2,0,1:T(8,128)(2,1)S(1)}, u32[]{:S(2)}, u32[]{:S(2)}) collective-permute-start(f16[2,2,14,16,128]{4,3,2,0,1:T(8,128)(2,1)S(1)} %fusion.7), channel_id=1, source_target_pairs={{0,1},{1,0},{2,3},{3,2},{4,5},{5,4},{6,7},{7,6},{8,9},{9,8},{10,11... | collective-permute-start | bytes 688136 | tf_op jit(solution)/shard_map/ppermute | solution.py:382
  67.3 3.4 %collective-permute-done.23 = f16[2,2,14,16,128]{4,3,2,0,1:T(8,128)(2,1)S(1)} collective-permute-done((f16[2,2,14,16,128]{4,3,2,0,1:T(8,128)(2,1)S(1)}, f16[2,2,14,16,128]{4,3,2,0,1:T(8,128)(2,1)S(1)}, u32[]{:S(2)}, u32[]{:S(2)}) %collective-permute-start.23) | collective-permute-done | bytes 229408 | tf_op jit(solution)/shard_map/ppermute | solution.py:382
  71.1 1.6 %collective-permute-start.24 = (f16[2,14,16,128]{3,2,1,0:T(8,128)(2,1)S(1)}, f16[2,14,16,128]{3,2,1,0:T(8,128)(2,1)S(1)}, u32[]{:S(2)}, u32[]{:S(2)}) collective-permute-start(f16[2,14,16,128]{3,2,1,0:T(8,128)(2,1)S(1)} %fusion.14), channel_id=1, source_target_pairs={{0,2},{1,3},{2,0},{3,1},{4,6},{5,7},{6,4},{7,5},{8,10},{9,11},{10,... | collective-permute-start | bytes 344072 | tf_op jit(solution)/shard_map/ppermute | solution.py:382
  72.8 2.2 %collective-permute-start.14 = (f16[2,2,2,19,16,128]{5,4,3,1,0,2:T(8,128)(2,1)S(1)}, f16[2,2,2,19,16,128]{5,4,3,1,0,2:T(8,128)(2,1)S(1)}, u32[]{:S(2)}, u32[]{:S(2)}) collective-permute-start(f16[2,2,2,19,16,128]{5,4,3,1,0,2:T(8,128)(2,1)S(1)} %fusion), channel_id=1, source_target_pairs={{0,1},{1,0},{2,3},{3,2},{4,5},{5,4},{6,7},{7,6},{8,9},{9,8},{10,11... | collective-permute-start | bytes 1867784 | tf_op jit(solution)/shard_map/ppermute | solution.py:382
  76.8 7.9 %collective-permute-done.14 = f16[2,2,2,19,16,128]{5,4,3,1,0,2:T(8,128)(2,1)S(1)} collective-permute-done((f16[2,2,2,19,16,128]{5,4,3,1,0,2:T(8,128)(2,1)S(1)}, f16[2,2,2,19,16,128]{5,4,3,1,0,2:T(8,128)(2,1)S(1)}, u32[]{:S(2)}, u32[]{:S(2)}) %collective-permute-start.14) | collective-permute-done | bytes 622624 | tf_op jit(solution)/shard_map/ppermute | solution.py:382
  86.4 6.6 %collective-permute-done.15 = f16[2,2,19,16,128]{4,3,2,1,0:T(8,128)(2,1)S(1)} collective-permute-done((f16[2,2,19,16,128]{4,3,2,1,0:T(8,128)(2,1)S(1)}, f16[2,2,19,16,128]{4,3,2,1,0:T(8,128)(2,1)S(1)}, u32[]{:S(2)}, u32[]{:S(2)}) %collective-permute-start.15) | collective-permute-done | bytes 311328 | tf_op jit(solution)/shard_map/ppermute | solution.py:382
  92.9 1.9 %collective-permute-start.25 = (f16[14,16,128]{2,1,0:T(8,128)(2,1)S(1)}, f16[14,16,128]{2,1,0:T(8,128)(2,1)S(1)}, u32[]{:S(2)}, u32[]{:S(2)}) collective-permute-start(f16[14,16,128]{2,1,0:T(8,128)(2,1)S(1)} %fusion.19), channel_id=1, source_target_pairs={{0,4},{1,5},{2,6},{3,7},{4,0},{5,1},{6,2},{7,3},{8,12},{9,13},{10,... | collective-permute-start | bytes 172040 | tf_op jit(solution)/shard_map/ppermute | solution.py:382
  95.3 3.6 %collective-permute-done.25 = f16[14,16,128]{2,1,0:T(8,128)(2,1)S(1)} collective-permute-done((f16[14,16,128]{2,1,0:T(8,128)(2,1)S(1)}, f16[14,16,128]{2,1,0:T(8,128)(2,1)S(1)}, u32[]{:S(2)}, u32[]{:S(2)}) %collective-permute-start.25) | collective-permute-done | bytes 57376 | tf_op jit(solution)/shard_map/ppermute | solution.py:382
  99.4 6.0 %collective-permute-done.16 = f16[2,19,16,128]{3,2,1,0:T(8,128)(2,1)S(1)} collective-permute-done((f16[2,19,16,128]{3,2,1,0:T(8,128)(2,1)S(1)}, f16[2,19,16,128]{3,2,1,0:T(8,128)(2,1)S(1)}, u32[]{:S(2)}, u32[]{:S(2)}) %collective-permute-start.16) | collective-permute-done | bytes 155680 | tf_op jit(solution)/shard_map/ppermute | solution.py:382
  106.6 4.4 %collective-permute-done.17 = f16[19,16,128]{2,1,0:T(8,128)(2,1)S(1)} collective-permute-done((f16[19,16,128]{2,1,0:T(8,128)(2,1)S(1)}, f16[19,16,128]{2,1,0:T(8,128)(2,1)S(1)}, u32[]{:S(2)}, u32[]{:S(2)}) %collective-permute-start.17) | collective-permute-done | bytes 77856 | tf_op jit(solution)/shard_map/ppermute | solution.py:382
  111.8 1.6 %collective-permute-start.27 = (f32[13,16,128]{2,1,0:T(8,128)S(1)}, f32[13,16,128]{2,1,0:T(8,128)S(1)}, u32[]{:S(2)}, u32[]{:S(2)}) collective-permute-start(f32[13,16,128]{2,1,0:T(8,128)S(1)} %add_select_fusion.12.refs_0_), channel_id=1, source_target_pairs={{0,16},{8,24},{16,0},{24,8},{1,17},{9,25},{17,1},{25,9},{2,18},{10... | collective-permute-start | bytes 319496 | tf_op jit(solution)/shard_map/ppermute | solution.py:382
  113.9 3.6 %collective-permute-done.27.refs_2_ = f32[13,16,128]{2,1,0:T(8,128)S(1)} collective-permute-done((f32[13,16,128]{2,1,0:T(8,128)S(1)}, f32[13,16,128]{2,1,0:T(8,128)S(1)}, u32[]{:S(2)}, u32[]{:S(2)}) %collective-permute-start.27) | collective-permute-done | bytes 106528 | tf_op jit(solution)/shard_map/ppermute | solution.py:382
  118.8 1.4 %shard_map.115 = f32[112,896]{1,0:T(8,128)} custom-call(s32[2]{0:T(128)S(1)} %pad_add_fusion.me, f32[14,16,128]{2,1,0:T(8,128)S(1)} %get-tuple-element.53.refs_0_, f32[14,16,128]{2,1,0:T(8,128)S(1)} %collective-permute-done.10.refs_1_, f32[14,16,128]{2,1,0:T(8,128)S(1)} %collective-permute-done.11.refs_2_, f32[14,16,128]{2,1,0:T(8,128)S(1)} %collective-permute-done.12.refs_3_), custom_call_target="tpu_custom_call" | custom-call | flops 50000000 | bytes 4194304 | tf_op jit(solution)/shard_map/pallas_call | solution.py:369
  120.1 1.4 %shard_map.118 = f32[80,1280]{1,0:T(8,128)} custom-call(s32[2]{0:T(128)S(1)} %pad_add_fusion.me, f32[13,16,128]{2,1,0:T(8,128)S(1)} %add_select_fusion.12.refs_0_, f32[13,16,128]{2,1,0:T(8,128)S(1)} %collective-permute-done.26.refs_1_, f32[13,16,128]{2,1,0:T(8,128)S(1)} %collective-permute-done.27.refs_2_, f32[13,16,128]{2,1,0:T(8,128)S(1)} %collective-permute-done.28.refs_3_), custom_call_target="tpu_custom_call" | custom-call | flops 50000000 | bytes 4194304 | tf_op jit(solution)/shard_map/pallas_call | solution.py:369
  121.5 1.4 %shard_map.116 = f32[96,1536]{1,0:T(8,128)} custom-call(s32[2]{0:T(128)S(1)} %pad_add_fusion.me, f32[18,16,128]{2,1,0:T(8,128)S(1)} %add_select_fusion.10.refs_0_, f32[18,16,128]{2,1,0:T(8,128)S(1)} %collective-permute-done.18.refs_1_, f32[18,16,128]{2,1,0:T(8,128)S(1)} %collective-permute-done.19.refs_2_, f32[18,16,128]{2,1,0:T(8,128)S(1)} %collective-permute-done.20.refs_3_), custom_call_target="tpu_custom_call" | custom-call | flops 50000000 | bytes 4194304 | tf_op jit(solution)/shard_map/pallas_call | solution.py:369
  (124 shorter events, 19.5 us)
Async XLA Ops:
  0.6 11.8 %copy-start.3 = (bf16[1,16,3712]{2,1,0:T(8,128)(2,1)S(1)}, bf16[1,16,3712]{2,1,0:T(8,128)(2,1)}, u32[]{:S(2)}) copy-start(bf16[1,16,3712]{2,1,0:T(8,128)(2,1)} %param.8) | copy-start | bytes 356356
  0.6 11.8 %copy-start.4 = (bf16[1,16,3712]{2,1,0:T(8,128)(2,1)S(1)}, bf16[1,16,3712]{2,1,0:T(8,128)(2,1)}, u32[]{:S(2)}) copy-start(bf16[1,16,3712]{2,1,0:T(8,128)(2,1)} %param.9) | copy-start | bytes 356356
  1.6 9.6 %collective-permute-start.1 = (bf16[2,8,3712]{2,1,0:T(8,128)(2,1)S(1)}, bf16[2,8,3712]{2,1,0:T(8,128)(2,1)S(1)}, u32[]{:S(2)}, u32[]{:S(2)}) collective-permute-start(bf16[2,8,3712]{2,1,0:T(8,128)(2,1)S(1)} %pad_maximum_fusion.2), channel_id=1, source_target_pairs={{1,0},{2,1},{3,2},{4,3},{5,4},{6,5},{7,6},{9,8},{10,9},{11,10},{12... | collective-permute-start | bytes 356360 | tf_op jit(solution)/shard_map/ppermute | solution.py:406
  3.0 9.5 %collective-permute-start = (bf16[2,8,3712]{2,1,0:T(8,128)(2,1)S(1)}, bf16[2,8,3712]{2,1,0:T(8,128)(2,1)S(1)}, u32[]{:S(2)}, u32[]{:S(2)}) collective-permute-start(bf16[2,8,3712]{2,1,0:T(8,128)(2,1)S(1)} %pad_maximum_fusion.1), channel_id=1, source_target_pairs={{0,1},{1,2},{2,3},{3,4},{4,5},{5,6},{6,7},{8,9},{9,10},{10,11},{11... | collective-permute-start | bytes 356360 | tf_op jit(solution)/shard_map/ppermute | solution.py:403
  12.5 5.9 %copy-start = (bf16[768,1536]{1,0:T(8,128)(2,1)S(1)}, bf16[768,1536]{1,0:T(8,128)(2,1)}, u32[]{:S(2)}) copy-start(bf16[768,1536]{1,0:T(8,128)(2,1)} %wo.3) | copy-start | bytes 7077892
  23.1 10.5 %collective-permute-start.4 = (bf16[4,32,896]{2,1,0:T(8,128)(2,1)S(1)}, bf16[4,32,896]{2,1,0:T(8,128)(2,1)S(1)}, u32[]{:S(2)}, u32[]{:S(2)}) collective-permute-start(bf16[4,32,896]{2,1,0:T(8,128)(2,1)S(1)} %shard_map.112.sums.refs_0_), channel_id=1, source_target_pairs={{0,8},{8,0},{16,24},{24,16},{1,9},{9,1},{17,25},{25,17},{2,10},{10... | collective-permute-start | bytes 688136 | tf_op jit(solution)/shard_map/ppermute | solution.py:382
  23.2 10.3 %collective-permute-start.5 = (bf16[4,32,896]{2,1,0:T(8,128)(2,1)S(1)}, bf16[4,32,896]{2,1,0:T(8,128)(2,1)S(1)}, u32[]{:S(2)}, u32[]{:S(2)}) collective-permute-start(bf16[4,32,896]{2,1,0:T(8,128)(2,1)S(1)} %shard_map.112.sums.refs_0_), channel_id=1, source_target_pairs={{0,16},{8,24},{16,0},{24,8},{1,17},{9,25},{17,1},{25,9},{2,18},{10... | collective-permute-start | bytes 688136 | tf_op jit(solution)/shard_map/ppermute | solution.py:382
  27.0 84.8 %collective-permute-start.3 = (f32[8,3712]{1,0:T(8,128)S(1)}, f32[8,3712]{1,0:T(8,128)S(1)}, u32[]{:S(2)}, u32[]{:S(2)}) collective-permute-start(f32[8,3712]{1,0:T(8,128)S(1)} %get-tuple-element.41), channel_id=1, source_target_pairs={{1,0},{2,1},{3,2},{4,3},{5,4},{6,5},{7,6},{9,8},{10,9},{11,10},{12... | collective-permute-start | bytes 356360 | tf_op jit(solution)/shard_map/ppermute | solution.py:529
  28.3 85.1 %collective-permute-start.2 = (f32[8,3712]{1,0:T(8,128)S(1)}, f32[8,3712]{1,0:T(8,128)S(1)}, u32[]{:S(2)}, u32[]{:S(2)}) collective-permute-start(f32[8,3712]{1,0:T(8,128)S(1)} %get-tuple-element.40), channel_id=1, source_target_pairs={{0,1},{1,2},{2,3},{3,4},{4,5},{5,6},{6,7},{8,9},{9,10},{10,11},{11... | collective-permute-start | bytes 356360 | tf_op jit(solution)/shard_map/ppermute | solution.py:530
  33.5 1.6 %collective-permute-start.6 = (bf16[4,32,896]{2,1,0:T(8,128)(2,1)S(1)}, bf16[4,32,896]{2,1,0:T(8,128)(2,1)S(1)}, u32[]{:S(2)}, u32[]{:S(2)}) collective-permute-start(bf16[4,32,896]{2,1,0:T(8,128)(2,1)S(1)} %collective-permute-done.5.refs_2_), channel_id=1, source_target_pairs={{0,8},{8,0},{16,24},{24,16},{1,9},{9,1},{17,25},{25,17},{2,10},{10... | collective-permute-start | bytes 688136 | tf_op jit(solution)/shard_map/ppermute | solution.py:382
  37.7 9.1 %collective-permute-start.7 = (f16[2,2,15,16,128]{4,3,2,1,0:T(8,128)(2,1)S(1)}, f16[2,2,15,16,128]{4,3,2,1,0:T(8,128)(2,1)S(1)}, u32[]{:S(2)}, u32[]{:S(2)}) collective-permute-start(f16[2,2,15,16,128]{4,3,2,1,0:T(8,128)(2,1)S(1)} %fusion.5), channel_id=1, source_target_pairs={{0,2},{1,3},{2,0},{3,1},{4,6},{5,7},{6,4},{7,5},{8,10},{9,11},{10,... | collective-permute-start | bytes 737288 | tf_op jit(solution)/shard_map/ppermute | solution.py:382
  43.1 9.1 %collective-permute-start.21 = (f32[2,8,14,16,128]{4,3,2,1,0:T(8,128)S(1)}, f32[2,8,14,16,128]{4,3,2,1,0:T(8,128)S(1)}, u32[]{:S(2)}, u32[]{:S(2)}) collective-permute-start(f32[2,8,14,16,128]{4,3,2,1,0:T(8,128)S(1)} %get-tuple-element.35), channel_id=1, source_target_pairs={{0,8},{8,0},{16,24},{24,16},{1,9},{9,1},{17,25},{25,17},{2,10},{10... | collective-permute-start | bytes 5505032 | tf_op jit(solution)/shard_map/ppermute | solution.py:382
  43.2 23.1 %collective-permute-start.13 = (f32[2,8,19,16,128]{4,3,2,1,0:T(8,128)S(1)}, f32[2,8,19,16,128]{4,3,2,1,0:T(8,128)S(1)}, u32[]{:S(2)}, u32[]{:S(2)}) collective-permute-start(f32[2,8,19,16,128]{4,3,2,1,0:T(8,128)S(1)} %get-tuple-element.32), channel_id=1, source_target_pairs={{0,8},{8,0},{16,24},{24,16},{1,9},{9,1},{17,25},{25,17},{2,10},{10... | collective-permute-start | bytes 7471112 | tf_op jit(solution)/shard_map/ppermute | solution.py:382
  47.1 4.9 %collective-permute-start.8 = (f16[2,15,16,128]{3,2,1,0:T(8,128)(2,1)S(1)}, f16[2,15,16,128]{3,2,1,0:T(8,128)(2,1)S(1)}, u32[]{:S(2)}, u32[]{:S(2)}) collective-permute-start(f16[2,15,16,128]{3,2,1,0:T(8,128)(2,1)S(1)} %fusion.11), channel_id=1, source_target_pairs={{0,1},{1,0},{2,3},{3,2},{4,5},{5,4},{6,7},{7,6},{8,9},{9,8},{10,11... | collective-permute-start | bytes 368648 | tf_op jit(solution)/shard_map/ppermute | solution.py:382
  53.2 10.9 %collective-permute-start.22 = (f16[2,2,2,14,16,128]{5,4,3,0,1,2:T(8,128)(2,1)S(1)}, f16[2,2,2,14,16,128]{5,4,3,0,1,2:T(8,128)(2,1)S(1)}, u32[]{:S(2)}, u32[]{:S(2)}) collective-permute-start(f16[2,2,2,14,16,128]{5,4,3,0,1,2:T(8,128)(2,1)S(1)} %fusion.2), channel_id=1, source_target_pairs={{0,16},{8,24},{16,0},{24,8},{1,17},{9,25},{17,1},{25,9},{2,18},{10... | collective-permute-start | bytes 1376264 | tf_op jit(solution)/shard_map/ppermute | solution.py:382
  53.8 5.2 %collective-permute-start.9 = (f16[15,16,128]{2,1,0:T(8,128)(2,1)S(1)}, f16[15,16,128]{2,1,0:T(8,128)(2,1)S(1)}, u32[]{:S(2)}, u32[]{:S(2)}) collective-permute-start(f16[15,16,128]{2,1,0:T(8,128)(2,1)S(1)} %fusion.17), channel_id=1, source_target_pairs={{0,4},{1,5},{2,6},{3,7},{4,0},{5,1},{6,2},{7,3},{8,12},{9,13},{10,... | collective-permute-start | bytes 184328 | tf_op jit(solution)/shard_map/ppermute | solution.py:382
  64.6 6.1 %collective-permute-start.23 = (f16[2,2,14,16,128]{4,3,2,0,1:T(8,128)(2,1)S(1)}, f16[2,2,14,16,128]{4,3,2,0,1:T(8,128)(2,1)S(1)}, u32[]{:S(2)}, u32[]{:S(2)}) collective-permute-start(f16[2,2,14,16,128]{4,3,2,0,1:T(8,128)(2,1)S(1)} %fusion.7), channel_id=1, source_target_pairs={{0,1},{1,0},{2,3},{3,2},{4,5},{5,4},{6,7},{7,6},{8,9},{9,8},{10,11... | collective-permute-start | bytes 688136 | tf_op jit(solution)/shard_map/ppermute | solution.py:382
  71.1 4.9 %collective-permute-start.24 = (f16[2,14,16,128]{3,2,1,0:T(8,128)(2,1)S(1)}, f16[2,14,16,128]{3,2,1,0:T(8,128)(2,1)S(1)}, u32[]{:S(2)}, u32[]{:S(2)}) collective-permute-start(f16[2,14,16,128]{3,2,1,0:T(8,128)(2,1)S(1)} %fusion.14), channel_id=1, source_target_pairs={{0,2},{1,3},{2,0},{3,1},{4,6},{5,7},{6,4},{7,5},{8,10},{9,11},{10,... | collective-permute-start | bytes 344072 | tf_op jit(solution)/shard_map/ppermute | solution.py:382
  72.8 11.8 %collective-permute-start.14 = (f16[2,2,2,19,16,128]{5,4,3,1,0,2:T(8,128)(2,1)S(1)}, f16[2,2,2,19,16,128]{5,4,3,1,0,2:T(8,128)(2,1)S(1)}, u32[]{:S(2)}, u32[]{:S(2)}) collective-permute-start(f16[2,2,2,19,16,128]{5,4,3,1,0,2:T(8,128)(2,1)S(1)} %fusion), channel_id=1, source_target_pairs={{0,1},{1,0},{2,3},{3,2},{4,5},{5,4},{6,7},{7,6},{8,9},{9,8},{10,11... | collective-permute-start | bytes 1867784 | tf_op jit(solution)/shard_map/ppermute | solution.py:382
  76.1 41.3 %collective-permute-start.10 = (f32[14,16,128]{2,1,0:T(8,128)S(1)}, f32[14,16,128]{2,1,0:T(8,128)S(1)}, u32[]{:S(2)}, u32[]{:S(2)}) collective-permute-start(f32[14,16,128]{2,1,0:T(8,128)S(1)} %get-tuple-element.53.refs_0_), channel_id=1, source_target_pairs={{0,8},{8,0},{16,24},{24,16},{1,9},{9,1},{17,25},{25,17},{2,10},{10... | collective-permute-start | bytes 344072 | tf_op jit(solution)/shard_map/ppermute | solution.py:382
  76.2 37.2 %collective-permute-start.11 = (f32[14,16,128]{2,1,0:T(8,128)S(1)}, f32[14,16,128]{2,1,0:T(8,128)S(1)}, u32[]{:S(2)}, u32[]{:S(2)}) collective-permute-start(f32[14,16,128]{2,1,0:T(8,128)S(1)} %get-tuple-element.53.refs_0_), channel_id=1, source_target_pairs={{0,16},{8,24},{16,0},{24,8},{1,17},{9,25},{17,1},{25,9},{2,18},{10... | collective-permute-start | bytes 344072 | tf_op jit(solution)/shard_map/ppermute | solution.py:382
  85.4 7.6 %collective-permute-start.15 = (f16[2,2,19,16,128]{4,3,2,1,0:T(8,128)(2,1)S(1)}, f16[2,2,19,16,128]{4,3,2,1,0:T(8,128)(2,1)S(1)}, u32[]{:S(2)}, u32[]{:S(2)}) collective-permute-start(f16[2,2,19,16,128]{4,3,2,1,0:T(8,128)(2,1)S(1)} %fusion.3), channel_id=1, source_target_pairs={{0,2},{1,3},{2,0},{3,1},{4,6},{5,7},{6,4},{7,5},{8,10},{9,11},{10,... | collective-permute-start | bytes 933896 | tf_op jit(solution)/shard_map/ppermute | solution.py:382
  92.9 5.9 %collective-permute-start.25 = (f16[14,16,128]{2,1,0:T(8,128)(2,1)S(1)}, f16[14,16,128]{2,1,0:T(8,128)(2,1)S(1)}, u32[]{:S(2)}, u32[]{:S(2)}) collective-permute-start(f16[14,16,128]{2,1,0:T(8,128)(2,1)S(1)} %fusion.19), channel_id=1, source_target_pairs={{0,4},{1,5},{2,6},{3,7},{4,0},{5,1},{6,2},{7,3},{8,12},{9,13},{10,... | collective-permute-start | bytes 172040 | tf_op jit(solution)/shard_map/ppermute | solution.py:382
  98.9 6.4 %collective-permute-start.16 = (f16[2,19,16,128]{3,2,1,0:T(8,128)(2,1)S(1)}, f16[2,19,16,128]{3,2,1,0:T(8,128)(2,1)S(1)}, u32[]{:S(2)}, u32[]{:S(2)}) collective-permute-start(f16[2,19,16,128]{3,2,1,0:T(8,128)(2,1)S(1)} %fusion.9), channel_id=1, source_target_pairs={{0,16},{8,24},{16,0},{24,8},{1,17},{9,25},{17,1},{25,9},{2,18},{10... | collective-permute-start | bytes 466952 | tf_op jit(solution)/shard_map/ppermute | solution.py:382
  105.6 5.4 %collective-permute-start.17 = (f16[19,16,128]{2,1,0:T(8,128)(2,1)S(1)}, f16[19,16,128]{2,1,0:T(8,128)(2,1)S(1)}, u32[]{:S(2)}, u32[]{:S(2)}) collective-permute-start(f16[19,16,128]{2,1,0:T(8,128)(2,1)S(1)} %fusion.16), channel_id=1, source_target_pairs={{0,4},{1,5},{2,6},{3,7},{4,0},{5,1},{6,2},{7,3},{8,12},{9,13},{10,... | collective-permute-start | bytes 233480 | tf_op jit(solution)/shard_map/ppermute | solution.py:382
  111.1 6.9 %collective-permute-start.19 = (f32[18,16,128]{2,1,0:T(8,128)S(1)}, f32[18,16,128]{2,1,0:T(8,128)S(1)}, u32[]{:S(2)}, u32[]{:S(2)}) collective-permute-start(f32[18,16,128]{2,1,0:T(8,128)S(1)} %add_select_fusion.10.refs_0_), channel_id=1, source_target_pairs={{0,16},{8,24},{16,0},{24,8},{1,17},{9,25},{17,1},{25,9},{2,18},{10... | collective-permute-start | bytes 442376 | tf_op jit(solution)/shard_map/ppermute | solution.py:382
  111.8 5.7 %collective-permute-start.27 = (f32[13,16,128]{2,1,0:T(8,128)S(1)}, f32[13,16,128]{2,1,0:T(8,128)S(1)}, u32[]{:S(2)}, u32[]{:S(2)}) collective-permute-start(f32[13,16,128]{2,1,0:T(8,128)S(1)} %add_select_fusion.12.refs_0_), channel_id=1, source_target_pairs={{0,16},{8,24},{16,0},{24,8},{1,17},{9,25},{17,1},{25,9},{2,18},{10... | collective-permute-start | bytes 319496 | tf_op jit(solution)/shard_map/ppermute | solution.py:382
  113.4 6.7 %collective-permute-start.26 = (f32[13,16,128]{2,1,0:T(8,128)S(1)}, f32[13,16,128]{2,1,0:T(8,128)S(1)}, u32[]{:S(2)}, u32[]{:S(2)}) collective-permute-start(f32[13,16,128]{2,1,0:T(8,128)S(1)} %add_select_fusion.12.refs_0_), channel_id=1, source_target_pairs={{0,8},{8,0},{16,24},{24,16},{1,9},{9,1},{17,25},{25,17},{2,10},{10... | collective-permute-start | bytes 319496 | tf_op jit(solution)/shard_map/ppermute | solution.py:382
  113.4 5.4 %collective-permute-start.12 = (f32[14,16,128]{2,1,0:T(8,128)S(1)}, f32[14,16,128]{2,1,0:T(8,128)S(1)}, u32[]{:S(2)}, u32[]{:S(2)}) collective-permute-start(f32[14,16,128]{2,1,0:T(8,128)S(1)} %collective-permute-done.11.refs_2_), channel_id=1, source_target_pairs={{0,8},{8,0},{16,24},{24,16},{1,9},{9,1},{17,25},{25,17},{2,10},{10... | collective-permute-start | bytes 344072 | tf_op jit(solution)/shard_map/ppermute | solution.py:382
  117.5 2.6 %collective-permute-start.28 = (f32[13,16,128]{2,1,0:T(8,128)S(1)}, f32[13,16,128]{2,1,0:T(8,128)S(1)}, u32[]{:S(2)}, u32[]{:S(2)}) collective-permute-start(f32[13,16,128]{2,1,0:T(8,128)S(1)} %collective-permute-done.27.refs_2_), channel_id=1, source_target_pairs={{0,8},{8,0},{16,24},{24,16},{1,9},{9,1},{17,25},{25,17},{2,10},{10... | collective-permute-start | bytes 319496 | tf_op jit(solution)/shard_map/ppermute | solution.py:382
  117.5 4.0 %collective-permute-start.18 = (f32[18,16,128]{2,1,0:T(8,128)S(1)}, f32[18,16,128]{2,1,0:T(8,128)S(1)}, u32[]{:S(2)}, u32[]{:S(2)}) collective-permute-start(f32[18,16,128]{2,1,0:T(8,128)S(1)} %add_select_fusion.10.refs_0_), channel_id=1, source_target_pairs={{0,8},{8,0},{16,24},{24,16},{1,9},{9,1},{17,25},{25,17},{2,10},{10... | collective-permute-start | bytes 442376 | tf_op jit(solution)/shard_map/ppermute | solution.py:382
  118.0 3.5 %collective-permute-start.20 = (f32[18,16,128]{2,1,0:T(8,128)S(1)}, f32[18,16,128]{2,1,0:T(8,128)S(1)}, u32[]{:S(2)}, u32[]{:S(2)}) collective-permute-start(f32[18,16,128]{2,1,0:T(8,128)S(1)} %collective-permute-done.19.refs_2_), channel_id=1, source_target_pairs={{0,8},{8,0},{16,24},{24,16},{1,9},{9,1},{17,25},{25,17},{2,10},{10... | collective-permute-start | bytes 442376 | tf_op jit(solution)/shard_map/ppermute | solution.py:382
  (2 other events, 11.7 us)

commit v3 on v2

--- a/solution.py
+++ b/solution.py
@@ -348,17 +348,21 @@
     return body
 
 
-def make_output(tiles, size):
+def make_output(layouts, size):
+    count = len(layouts)
+
     def body(me, *refs):
-        parts, out, flat = refs[:size], refs[size], refs[size + 1]
-        for mask in range(size):
-            flat[slot_of(me[0] ^ mask, size)] = parts[mask][...] * (1.0 / size)
-        for tile in range(tiles.count):
-            i, j = tile // tiles.across, tile % tiles.across
-            r0, r1 = i * ROWS, min((i + 1) * ROWS, tiles.rows)
-            out[r0:r1, j * LANES : (j + 1) * LANES] = flat[
-                tile // tiles.each, tile % tiles.each, : r1 - r0
-            ]
+        outs, flats = refs[size * count : size * count + count], refs[size * count + count :]
+        for k, tiles in enumerate(layouts):
+            parts, out, flat = refs[size * k : size * (k + 1)], outs[k], flats[k]
+            for mask in range(size):
+                flat[slot_of(me[0] ^ mask, size)] = parts[mask][: tiles.each] * (1.0 / size)
+            for tile in range(tiles.count):
+                i, j = tile // tiles.across, tile % tiles.across
+                r0, r1 = i * ROWS, min((i + 1) * ROWS, tiles.rows)
+                out[r0:r1, j * LANES : (j + 1) * LANES] = flat[
+                    tile // tiles.each, tile % tiles.each, : r1 - r0
+                ]
 
     return body
 
@@ -462,19 +466,11 @@
             value = combine(jnp.where(high, high_half, low_half), decode(got, rows))
         return value
 
-    def spread(tiles, value):
-        parts = {0: value[: tiles.each]}
+    def spread(value):
+        parts = {0: value}
         for bit in reversed(range(bits)):
             parts.update({m | (1 << bit): swap(v, bit) for m, v in list(parts.items())})
-        return call(
-            make_output(tiles, size),
-            shape((tiles.rows, tiles.cols), F32),
-            50_000_000,
-            4,
-            me,
-            *[parts[m] for m in range(size)],
-            scratch=(pltpu.VMEM((size, tiles.each, ROWS, LANES), F32),),
-        )
+        return [parts[m] for m in range(size)]
 
     keep_two, send_two = call(
         make_second(channels, t_two),
@@ -545,10 +541,20 @@
         scratch=(t_zero.scratch(),),
     )
     zero = halving(zero, marks[bits:], over_graph[1::-1] + over_graph[2:])
-    grad_one = spread(t_one, one)
-    grad_two = spread(t_two, two)
-    grad_zero = spread(t_zero, zero)
-    return (grad_nodes, grad_zero, grad_one, grad_two)
+    layouts = (t_zero, t_one, t_two)
+    parts = spread(zero) + spread(one) + spread(two)
+    grads = call(
+        make_output(layouts, size),
+        tuple(shape((tiles.rows, tiles.cols), F32) for tiles in layouts),
+        50_000_000,
+        8,
+        me,
+        *parts,
+        scratch=tuple(
+            pltpu.VMEM((size, tiles.each, ROWS, LANES), F32) for tiles in layouts
+        ),
+    )
+    return (grad_nodes, *grads)
 
 
 def solution(mesh):

time: 123 us -> 117 us (0.951)
  waiting for transfers between devices: 52.3 us -> 47.2 us
  Pallas kernels: 21.9 us -> 19.6 us
    ppermute x25, waiting for transfers between devices: 51.1 us -> 46 us  [swap(): return lax.ppermute(value, axis, [(i, i ^ 1 << bit) for i in range(size)])]
    pallas_call x8 -> x6, Pallas kernels: 21.9 us -> 19.6 us  [call(): pl.pallas_call(body, out_shape=outs, in_specs=[smem] * scalars + [vmem] *...]
    ppermute x25, starting transfers between devices: 24.1 us -> 25.4 us  [swap(): return lax.ppermute(value, axis, [(i, i ^ 1 << bit) for i in range(size)])]
    select_n x12 -> x13, other arithmetic: 2.81 us -> 2.9 us  [combine(): jnp.where(is_level(first), jnp.maximum(first, second), first + second)]
  transfers between devices with their start and end apart: 29 -> 29, of which waited for: 14 -> 16; matrix products, arithmetic and copies ran while one was open for 7% -> 8% of each run, Pallas kernels for 8% -> 6%
where the time goes in v3:
time: 117 us; the launch traced here: 116 us
  waiting for transfers between devices  47.2 us (40%)
  starting transfers between devices  38.3 us (33%)
  Pallas kernels  19.6 us (17%)
  other arithmetic  7.52 us (6%)
  local copies, waits for them, and re-layouts  2.5 us (2%)
  between operations  1.18 us (1%)
    ppermute x25, waiting for transfers between devices, swap(): return lax.ppermute(value, axis, [(i, i ^ 1 << bit) for i in range(size)])  46 us
    ppermute x25, starting transfers between devices, swap(): return lax.ppermute(value, axis, [(i, i ^ 1 << bit) for i in range(size)])  25.4 us
    pallas_call x6, Pallas kernels, call(): pl.pallas_call(body, out_shape=outs, in_specs=[smem] * scalars + [vmem] *...  19.6 us
    ppermute x1, starting transfers between devices, shards(): lax.ppermute(jnp.stack([feats[atom_count - reach:], cots[atom_count - rea...  5.53 us
    ppermute x1, starting transfers between devices, shards(): from_prev = lax.ppermute(nodes[atom_count + reach:], 'graph', up)  4.78 us
    select_n x13, other arithmetic, combine(): jnp.where(is_level(first), jnp.maximum(first, second), first + second)  2.9 us
  transfers between devices with their start and end apart: 29, of which 16 were waited for; matrix products, arithmetic and copies ran while one was open for 8% of the time, Pallas kernels for 6%

profile of v3, /device:TPU:0, one launch (start us, length us, event | category | flops | bytes accessed | tf_op | source)
XLA Modules:
  0.0 116.3 jit_solution(3798011420730613493)
XLA Ops:
  1.6 1.3 %collective-permute-start.1 = (bf16[2,8,3712]{2,1,0:T(8,128)(2,1)S(1)}, bf16[2,8,3712]{2,1,0:T(8,128)(2,1)S(1)}, u32[]{:S(2)}, u32[]{:S(2)}) collective-permute-start(bf16[2,8,3712]{2,1,0:T(8,128)(2,1)S(1)} %pad_maximum_fusion.2), channel_id=1, source_target_pairs={{1,0},{2,1},{3,2},{4,3},{5,4},{6,5},{7,6},{9,8},{10,9},{11,10},{12... | collective-permute-start | bytes 356360 | tf_op jit(solution)/shard_map/ppermute | solution.py:410
  3.0 5.5 %collective-permute-start = (bf16[2,8,3712]{2,1,0:T(8,128)(2,1)S(1)}, bf16[2,8,3712]{2,1,0:T(8,128)(2,1)S(1)}, u32[]{:S(2)}, u32[]{:S(2)}) collective-permute-start(bf16[2,8,3712]{2,1,0:T(8,128)(2,1)S(1)} %pad_maximum_fusion.1), channel_id=1, source_target_pairs={{0,1},{1,2},{2,3},{3,4},{4,5},{5,6},{6,7},{8,9},{9,10},{10,11},{11... | collective-permute-start | bytes 356360 | tf_op jit(solution)/shard_map/ppermute | solution.py:407
  12.6 6.0 %shard_map.111 = (bf16[640,768]{1,0:T(8,128)(2,1)S(1)}, bf16[320,1536]{1,0:T(8,128)(2,1)S(1)}, bf16[640,640]{1,0:T(8,128)(2,1)S(1)}, bf16[320,1280]{1,0:T(8,128)...) custom-call(s32[2]{0:T(128)S(1)} %pad_add_fusion.me, ...), custom_call_target="tpu_custom_call" | custom-call | flops 3000000000 | bytes 4194304 | tf_op jit(solution)/shard_map/pallas_call | solution.py:373
  18.6 4.6 %shard_map.112.sums.refs_0_ = bf16[4,32,896]{2,1,0:T(8,128)(2,1)S(1)} custom-call(bf16[32,896]{1,0:T(8,128)(2,1)S(1)} %get-tuple-element.23.feat, f32[320,8]{1,0:T(8,128)S(1)} %copy.14.cols, f32[8,320]{1,0:T(8,128)S(1)} %stack.39.rows, bf16[640,768]{1,0:T(8,128)(2,1)S(1)} %get-tuple-element.24.x1, bf16[640,640]{1,0:T(8,128)(2,1)S(1)} %get-tuple-element.25.x2, ...), custom_call_target="tpu_custom_call" | custom-call | flops 4000000000 | bytes 4194304 | tf_op jit(solution)/shard_map/pallas_call | solution.py:373
  23.2 1.6 %collective-permute-start.5 = (bf16[4,32,896]{2,1,0:T(8,128)(2,1)S(1)}, bf16[4,32,896]{2,1,0:T(8,128)(2,1)S(1)}, u32[]{:S(2)}, u32[]{:S(2)}) collective-permute-start(bf16[4,32,896]{2,1,0:T(8,128)(2,1)S(1)} %shard_map.112.sums.refs_0_), channel_id=1, source_target_pairs={{0,16},{8,24},{16,0},{24,8},{1,17},{9,25},{17,1},{25,9},{2,18},{10... | collective-permute-start | bytes 688136 | tf_op jit(solution)/shard_map/ppermute | solution.py:386
  24.8 6.0 %collective-permute-done.5.refs_2_ = bf16[4,32,896]{2,1,0:T(8,128)(2,1)S(1)} collective-permute-done((bf16[4,32,896]{2,1,0:T(8,128)(2,1)S(1)}, bf16[4,32,896]{2,1,0:T(8,128)(2,1)S(1)}, u32[]{:S(2)}, u32[]{:S(2)}) %collective-permute-start.5) | collective-permute-done | bytes 229408 | tf_op jit(solution)/shard_map/ppermute | solution.py:386
  32.3 2.4 %shard_map.114 = f32[8,15,16,128]{3,2,1,0:T(8,128)S(1)} custom-call(s32[2]{0:T(128)S(1)} %pad_add_fusion.me, bf16[4,32,896]{2,1,0:T(8,128)(2,1)S(1)} %shard_map.112.sums.refs_0_, bf16[4,32,896]{2,1,0:T(8,128)(2,1)S(1)} %collective-permute-done.4.refs_1_, bf16[4,32,896]{2,1,0:T(8,128)(2,1)S(1)} %collective-permute-done.5.refs_2_, ...), custom_call_target="tpu_custom_call" | custom-call | flops 1000000000 | bytes 4194304 | tf_op jit(solution)/shard_map/pallas_call | solution.py:373
  34.9 1.8 %collective-permute-start.7 = (f16[2,2,15,16,128]{4,3,2,1,0:T(8,128)(2,1)S(1)}, f16[2,2,15,16,128]{4,3,2,1,0:T(8,128)(2,1)S(1)}, u32[]{:S(2)}, u32[]{:S(2)}) collective-permute-start(f16[2,2,15,16,128]{4,3,2,1,0:T(8,128)(2,1)S(1)} %fusion.5), channel_id=1, source_target_pairs={{0,2},{1,3},{2,0},{3,1},{4,6},{5,7},{6,4},{7,5},{8,10},{9,11},{10,... | collective-permute-start | bytes 737288 | tf_op jit(solution)/shard_map/ppermute | solution.py:386
  36.7 2.6 %shard_map.115 = (f32[2,8,14,16,128]{4,3,2,1,0:T(8,128)S(1)}, f32[2,8,14,16,128]{4,3,2,1,0:T(8,128)S(1)}) custom-call(s32[2]{0:T(128)S(1)} %pad_add_fusion.me, bf16[640,640]{1,0:T(8,128)(2,1)S(1)} %get-tuple-element.25.x2, bf16[320,1280]{1,0:T(8,128)(2,1)S(1)} %get-tuple-element.29.d2, f32[8,128]{1,0:T(8,128)S(1)} %get-tuple-element.36.level_in), custom_call_target="tpu_custom_call" | custom-call | flops 1200000000 | bytes 4194304 | tf_op jit(solution)/shard_map/pallas_call | solution.py:373
  39.4 3.6 %collective-permute-done.7 = f16[2,2,15,16,128]{4,3,2,1,0:T(8,128)(2,1)S(1)} collective-permute-done((f16[2,2,15,16,128]{4,3,2,1,0:T(8,128)(2,1)S(1)}, f16[2,2,15,16,128]{4,3,2,1,0:T(8,128)(2,1)S(1)}, u32[]{:S(2)}, u32[]{:S(2)}) %collective-permute-start.7) | collective-permute-done | bytes 245792 | tf_op jit(solution)/shard_map/ppermute | solution.py:386
  43.4 2.5 %collective-permute-start.8 = (f16[2,15,16,128]{3,2,1,0:T(8,128)(2,1)S(1)}, f16[2,15,16,128]{3,2,1,0:T(8,128)(2,1)S(1)}, u32[]{:S(2)}, u32[]{:S(2)}) collective-permute-start(f16[2,15,16,128]{3,2,1,0:T(8,128)(2,1)S(1)} %fusion.11), channel_id=1, source_target_pairs={{0,1},{1,0},{2,3},{3,2},{4,5},{5,4},{6,7},{7,6},{8,9},{9,8},{10,11... | collective-permute-start | bytes 368648 | tf_op jit(solution)/shard_map/ppermute | solution.py:386
  45.9 2.2 %shard_map.113 = f32[32,3712]{1,0:T(8,128)S(1)} custom-call(bf16[4,32,896]{2,1,0:T(8,128)(2,1)S(1)} %shard_map.112.sums.refs_0_, f32[8,320]{1,0:T(8,128)S(1)} %stack.39.rows, bf16[320,1536]{1,0:T(8,128)(2,1)S(1)} %get-tuple-element.28.d1, bf16[320,1280]{1,0:T(8,128)(2,1)S(1)} %get-tuple-element.29.d2, bf16[896,896]{1,0:T(8,128)(2,1)S(1)} %copy-done.1, ...), custom_call_target="tpu_custom_call" | custom-call | flops 2000000000 | bytes 4194304 | tf_op jit(solution)/shard_map/pallas_call | solution.py:373
  49.0 2.6 %collective-permute-start.9 = (f16[15,16,128]{2,1,0:T(8,128)(2,1)S(1)}, f16[15,16,128]{2,1,0:T(8,128)(2,1)S(1)}, u32[]{:S(2)}, u32[]{:S(2)}) collective-permute-start(f16[15,16,128]{2,1,0:T(8,128)(2,1)S(1)} %fusion.18), channel_id=1, source_target_pairs={{0,4},{1,5},{2,6},{3,7},{4,0},{5,1},{6,2},{7,3},{8,12},{9,13},{10,... | collective-permute-start | bytes 184328 | tf_op jit(solution)/shard_map/ppermute | solution.py:386
  52.6 1.6 %collective-permute-start.22 = (f16[2,2,2,14,16,128]{5,4,3,0,1,2:T(8,128)(2,1)S(1)}, f16[2,2,2,14,16,128]{5,4,3,0,1,2:T(8,128)(2,1)S(1)}, u32[]{:S(2)}, u32[]{:S(2)}) collective-permute-start(f16[2,2,2,14,16,128]{5,4,3,0,1,2:T(8,128)(2,1)S(1)} %fusion.2), channel_id=1, source_target_pairs={{0,16},{8,24},{16,0},{24,8},{1,17},{9,25},{17,1},{25,9},{2,18},{10... | collective-permute-start | bytes 1376264 | tf_op jit(solution)/shard_map/ppermute | solution.py:386
  55.4 4.8 %collective-permute-start.2 = (f32[8,3712]{1,0:T(8,128)S(1)}, f32[8,3712]{1,0:T(8,128)S(1)}, u32[]{:S(2)}, u32[]{:S(2)}) collective-permute-start(f32[8,3712]{1,0:T(8,128)S(1)} %get-tuple-element.46), channel_id=1, source_target_pairs={{0,1},{1,2},{2,3},{3,4},{4,5},{5,6},{6,7},{8,9},{9,10},{10,11},{11... | collective-permute-start | bytes 356360 | tf_op jit(solution)/shard_map/ppermute | solution.py:526
  60.2 2.9 %collective-permute-done.22 = f16[2,2,2,14,16,128]{5,4,3,0,1,2:T(8,128)(2,1)S(1)} collective-permute-done((f16[2,2,2,14,16,128]{5,4,3,0,1,2:T(8,128)(2,1)S(1)}, f16[2,2,2,14,16,128]{5,4,3,0,1,2:T(8,128)(2,1)S(1)}, u32[]{:S(2)}, u32[]{:S(2)}) %collective-permute-start.22) | collective-permute-done | bytes 458784 | tf_op jit(solution)/shard_map/ppermute | solution.py:386
  63.7 1.8 %collective-permute-start.23 = (f16[2,2,14,16,128]{4,3,2,0,1:T(8,128)(2,1)S(1)}, f16[2,2,14,16,128]{4,3,2,0,1:T(8,128)(2,1)S(1)}, u32[]{:S(2)}, u32[]{:S(2)}) collective-permute-start(f16[2,2,14,16,128]{4,3,2,0,1:T(8,128)(2,1)S(1)} %fusion.7), channel_id=1, source_target_pairs={{0,1},{1,0},{2,3},{3,2},{4,5},{5,4},{6,7},{7,6},{8,9},{9,8},{10,11... | collective-permute-start | bytes 688136 | tf_op jit(solution)/shard_map/ppermute | solution.py:386
  67.0 5.2 %collective-permute-done.23 = f16[2,2,14,16,128]{4,3,2,0,1:T(8,128)(2,1)S(1)} collective-permute-done((f16[2,2,14,16,128]{4,3,2,0,1:T(8,128)(2,1)S(1)}, f16[2,2,14,16,128]{4,3,2,0,1:T(8,128)(2,1)S(1)}, u32[]{:S(2)}, u32[]{:S(2)}) %collective-permute-start.23) | collective-permute-done | bytes 229408 | tf_op jit(solution)/shard_map/ppermute | solution.py:386
  73.8 3.6 %collective-permute-done.24 = f16[2,14,16,128]{3,2,1,0:T(8,128)(2,1)S(1)} collective-permute-done((f16[2,14,16,128]{3,2,1,0:T(8,128)(2,1)S(1)}, f16[2,14,16,128]{3,2,1,0:T(8,128)(2,1)S(1)}, u32[]{:S(2)}, u32[]{:S(2)}) %collective-permute-start.24) | collective-permute-done | bytes 114720 | tf_op jit(solution)/shard_map/ppermute | solution.py:386
  77.4 1.5 %collective-permute-start.11 = (f32[15,16,128]{2,1,0:T(8,128)S(1)}, f32[15,16,128]{2,1,0:T(8,128)S(1)}, u32[]{:S(2)}, u32[]{:S(2)}) collective-permute-start(f32[15,16,128]{2,1,0:T(8,128)S(1)} %add_select_fusion.11.refs_0_), channel_id=1, source_target_pairs={{0,16},{8,24},{16,0},{24,8},{1,17},{9,25},{17,1},{25,9},{2,18},{10... | collective-permute-start | bytes 368648 | tf_op jit(solution)/shard_map/ppermute | solution.py:386
  79.0 2.8 %collective-permute-done.14 = f16[2,2,2,19,16,128]{5,4,3,1,0,2:T(8,128)(2,1)S(1)} collective-permute-done((f16[2,2,2,19,16,128]{5,4,3,1,0,2:T(8,128)(2,1)S(1)}, f16[2,2,2,19,16,128]{5,4,3,1,0,2:T(8,128)(2,1)S(1)}, u32[]{:S(2)}, u32[]{:S(2)}) %collective-permute-start.14) | collective-permute-done | bytes 622624 | tf_op jit(solution)/shard_map/ppermute | solution.py:386
  82.6 2.1 %collective-permute-start.15 = (f16[2,2,19,16,128]{4,3,2,1,0:T(8,128)(2,1)S(1)}, f16[2,2,19,16,128]{4,3,2,1,0:T(8,128)(2,1)S(1)}, u32[]{:S(2)}, u32[]{:S(2)}) collective-permute-start(f16[2,2,19,16,128]{4,3,2,1,0:T(8,128)(2,1)S(1)} %fusion.3), channel_id=1, source_target_pairs={{0,2},{1,3},{2,0},{3,1},{4,6},{5,7},{6,4},{7,5},{8,10},{9,11},{10,... | collective-permute-start | bytes 933896 | tf_op jit(solution)/shard_map/ppermute | solution.py:386
  84.7 4.9 %collective-permute-done.15 = f16[2,2,19,16,128]{4,3,2,1,0:T(8,128)(2,1)S(1)} collective-permute-done((f16[2,2,19,16,128]{4,3,2,1,0:T(8,128)(2,1)S(1)}, f16[2,2,19,16,128]{4,3,2,1,0:T(8,128)(2,1)S(1)}, u32[]{:S(2)}, u32[]{:S(2)}) %collective-permute-start.15) | collective-permute-done | bytes 311328 | tf_op jit(solution)/shard_map/ppermute | solution.py:386
  90.0 1.6 %collective-permute-start.16 = (f16[2,19,16,128]{3,2,1,0:T(8,128)(2,1)S(1)}, f16[2,19,16,128]{3,2,1,0:T(8,128)(2,1)S(1)}, u32[]{:S(2)}, u32[]{:S(2)}) collective-permute-start(f16[2,19,16,128]{3,2,1,0:T(8,128)(2,1)S(1)} %fusion.9), channel_id=1, source_target_pairs={{0,16},{8,24},{16,0},{24,8},{1,17},{9,25},{17,1},{25,9},{2,18},{10... | collective-permute-start | bytes 466952 | tf_op jit(solution)/shard_map/ppermute | solution.py:386
  91.7 3.6 %collective-permute-done.16 = f16[2,19,16,128]{3,2,1,0:T(8,128)(2,1)S(1)} collective-permute-done((f16[2,19,16,128]{3,2,1,0:T(8,128)(2,1)S(1)}, f16[2,19,16,128]{3,2,1,0:T(8,128)(2,1)S(1)}, u32[]{:S(2)}, u32[]{:S(2)}) %collective-permute-start.16) | collective-permute-done | bytes 155680 | tf_op jit(solution)/shard_map/ppermute | solution.py:386
  95.3 1.7 %collective-permute-start.25 = (f16[14,16,128]{2,1,0:T(8,128)(2,1)S(1)}, f16[14,16,128]{2,1,0:T(8,128)(2,1)S(1)}, u32[]{:S(2)}, u32[]{:S(2)}) collective-permute-start(f16[14,16,128]{2,1,0:T(8,128)(2,1)S(1)} %fusion.21), channel_id=1, source_target_pairs={{0,4},{1,5},{2,6},{3,7},{4,0},{5,1},{6,2},{7,3},{8,12},{9,13},{10,... | collective-permute-start | bytes 172040 | tf_op jit(solution)/shard_map/ppermute | solution.py:386
  97.3 3.4 %collective-permute-done.25 = f16[14,16,128]{2,1,0:T(8,128)(2,1)S(1)} collective-permute-done((f16[14,16,128]{2,1,0:T(8,128)(2,1)S(1)}, f16[14,16,128]{2,1,0:T(8,128)(2,1)S(1)}, u32[]{:S(2)}, u32[]{:S(2)}) %collective-permute-start.25) | collective-permute-done | bytes 57376 | tf_op jit(solution)/shard_map/ppermute | solution.py:386
  100.7 1.5 %collective-permute-start.17 = (f16[19,16,128]{2,1,0:T(8,128)(2,1)S(1)}, f16[19,16,128]{2,1,0:T(8,128)(2,1)S(1)}, u32[]{:S(2)}, u32[]{:S(2)}) collective-permute-start(f16[19,16,128]{2,1,0:T(8,128)(2,1)S(1)} %fusion.16), channel_id=1, source_target_pairs={{0,4},{1,5},{2,6},{3,7},{4,0},{5,1},{6,2},{7,3},{8,12},{9,13},{10,... | collective-permute-start | bytes 233480 | tf_op jit(solution)/shard_map/ppermute | solution.py:386
  102.2 3.8 %collective-permute-done.17 = f16[19,16,128]{2,1,0:T(8,128)(2,1)S(1)} collective-permute-done((f16[19,16,128]{2,1,0:T(8,128)(2,1)S(1)}, f16[19,16,128]{2,1,0:T(8,128)(2,1)S(1)}, u32[]{:S(2)}, u32[]{:S(2)}) %collective-permute-start.17) | collective-permute-done | bytes 77856 | tf_op jit(solution)/shard_map/ppermute | solution.py:386
  106.1 1.6 %collective-permute-start.19 = (f32[19,16,128]{2,1,0:T(8,128)S(1)}, f32[19,16,128]{2,1,0:T(8,128)S(1)}, u32[]{:S(2)}, u32[]{:S(2)}) collective-permute-start(f32[19,16,128]{2,1,0:T(8,128)S(1)} %add_select_fusion.10.refs_4_), channel_id=1, source_target_pairs={{0,16},{8,24},{16,0},{24,8},{1,17},{9,25},{17,1},{25,9},{2,18},{10... | collective-permute-start | bytes 466952 | tf_op jit(solution)/shard_map/ppermute | solution.py:386
  108.9 3.7 %collective-permute-done.27.refs_10_ = f32[14,16,128]{2,1,0:T(8,128)S(1)} collective-permute-done((f32[14,16,128]{2,1,0:T(8,128)S(1)}, f32[14,16,128]{2,1,0:T(8,128)S(1)}, u32[]{:S(2)}, u32[]{:S(2)}) %collective-permute-start.27) | collective-permute-done | bytes 114720 | tf_op jit(solution)/shard_map/ppermute | solution.py:386
  114.6 1.7 %shard_map.116 = (f32[112,896]{1,0:T(8,128)}, f32[96,1536]{1,0:T(8,128)}, f32[80,1280]{1,0:T(8,128)}) custom-call(s32[2]{0:T(128)S(1)} %pad_add_fusion.me, f32[15,16,128]{2,1,0:T(8,128)S(1)} %add_select_fusion.11.refs_0_, f32[15,16,128]{2,1,0:T(8,128)S(1)} %collective-permute-done.10.refs_1_, f32[15,16,128]{2,1,0:T(8,128)S(1)} %collective-permute-done.11.refs_2_, ...), custom_call_target="tpu_custom_call" | custom-call | flops 50000000 | bytes 4194304 | tf_op jit(solution)/shard_map/pallas_call | solution.py:373
  (120 shorter events, 18.5 us)
Async XLA Ops:
  0.6 11.8 %copy-start.3 = (bf16[1,16,3712]{2,1,0:T(8,128)(2,1)S(1)}, bf16[1,16,3712]{2,1,0:T(8,128)(2,1)}, u32[]{:S(2)}) copy-start(bf16[1,16,3712]{2,1,0:T(8,128)(2,1)} %param.8) | copy-start | bytes 356356
  0.6 11.8 %copy-start.4 = (bf16[1,16,3712]{2,1,0:T(8,128)(2,1)S(1)}, bf16[1,16,3712]{2,1,0:T(8,128)(2,1)}, u32[]{:S(2)}) copy-start(bf16[1,16,3712]{2,1,0:T(8,128)(2,1)} %param.9) | copy-start | bytes 356356
  1.6 9.6 %collective-permute-start.1 = (bf16[2,8,3712]{2,1,0:T(8,128)(2,1)S(1)}, bf16[2,8,3712]{2,1,0:T(8,128)(2,1)S(1)}, u32[]{:S(2)}, u32[]{:S(2)}) collective-permute-start(bf16[2,8,3712]{2,1,0:T(8,128)(2,1)S(1)} %pad_maximum_fusion.2), channel_id=1, source_target_pairs={{1,0},{2,1},{3,2},{4,3},{5,4},{6,5},{7,6},{9,8},{10,9},{11,10},{12... | collective-permute-start | bytes 356360 | tf_op jit(solution)/shard_map/ppermute | solution.py:410
  3.0 9.5 %collective-permute-start = (bf16[2,8,3712]{2,1,0:T(8,128)(2,1)S(1)}, bf16[2,8,3712]{2,1,0:T(8,128)(2,1)S(1)}, u32[]{:S(2)}, u32[]{:S(2)}) collective-permute-start(bf16[2,8,3712]{2,1,0:T(8,128)(2,1)S(1)} %pad_maximum_fusion.1), channel_id=1, source_target_pairs={{0,1},{1,2},{2,3},{3,4},{4,5},{5,6},{6,7},{8,9},{9,10},{10,11},{11... | collective-permute-start | bytes 356360 | tf_op jit(solution)/shard_map/ppermute | solution.py:407
  12.5 6.1 %copy-start = (bf16[768,1536]{1,0:T(8,128)(2,1)S(1)}, bf16[768,1536]{1,0:T(8,128)(2,1)}, u32[]{:S(2)}) copy-start(bf16[768,1536]{1,0:T(8,128)(2,1)} %wo.3) | copy-start | bytes 7077892
  23.2 7.6 %collective-permute-start.5 = (bf16[4,32,896]{2,1,0:T(8,128)(2,1)S(1)}, bf16[4,32,896]{2,1,0:T(8,128)(2,1)S(1)}, u32[]{:S(2)}, u32[]{:S(2)}) collective-permute-start(bf16[4,32,896]{2,1,0:T(8,128)(2,1)S(1)} %shard_map.112.sums.refs_0_), channel_id=1, source_target_pairs={{0,16},{8,24},{16,0},{24,8},{1,17},{9,25},{17,1},{25,9},{2,18},{10... | collective-permute-start | bytes 688136 | tf_op jit(solution)/shard_map/ppermute | solution.py:386
  24.8 6.6 %collective-permute-start.4 = (bf16[4,32,896]{2,1,0:T(8,128)(2,1)S(1)}, bf16[4,32,896]{2,1,0:T(8,128)(2,1)S(1)}, u32[]{:S(2)}, u32[]{:S(2)}) collective-permute-start(bf16[4,32,896]{2,1,0:T(8,128)(2,1)S(1)} %shard_map.112.sums.refs_0_), channel_id=1, source_target_pairs={{0,8},{8,0},{16,24},{24,16},{1,9},{9,1},{17,25},{25,17},{2,10},{10... | collective-permute-start | bytes 688136 | tf_op jit(solution)/shard_map/ppermute | solution.py:386
  30.8 1.5 %collective-permute-start.6 = (bf16[4,32,896]{2,1,0:T(8,128)(2,1)S(1)}, bf16[4,32,896]{2,1,0:T(8,128)(2,1)S(1)}, u32[]{:S(2)}, u32[]{:S(2)}) collective-permute-start(bf16[4,32,896]{2,1,0:T(8,128)(2,1)S(1)} %collective-permute-done.5.refs_2_), channel_id=1, source_target_pairs={{0,8},{8,0},{16,24},{24,16},{1,9},{9,1},{17,25},{25,17},{2,10},{10... | collective-permute-start | bytes 688136 | tf_op jit(solution)/shard_map/ppermute | solution.py:386
  30.8 34.6 %collective-permute-start.13 = (f32[2,8,19,16,128]{4,3,2,1,0:T(8,128)S(1)}, f32[2,8,19,16,128]{4,3,2,1,0:T(8,128)S(1)}, u32[]{:S(2)}, u32[]{:S(2)}) collective-permute-start(f32[2,8,19,16,128]{4,3,2,1,0:T(8,128)S(1)} %get-tuple-element.35), channel_id=1, source_target_pairs={{0,8},{8,0},{16,24},{24,16},{1,9},{9,1},{17,25},{25,17},{2,10},{10... | collective-permute-start | bytes 7471112 | tf_op jit(solution)/shard_map/ppermute | solution.py:386
  34.9 8.1 %collective-permute-start.7 = (f16[2,2,15,16,128]{4,3,2,1,0:T(8,128)(2,1)S(1)}, f16[2,2,15,16,128]{4,3,2,1,0:T(8,128)(2,1)S(1)}, u32[]{:S(2)}, u32[]{:S(2)}) collective-permute-start(f16[2,2,15,16,128]{4,3,2,1,0:T(8,128)(2,1)S(1)} %fusion.5), channel_id=1, source_target_pairs={{0,2},{1,3},{2,0},{3,1},{4,6},{5,7},{6,4},{7,5},{8,10},{9,11},{10,... | collective-permute-start | bytes 737288 | tf_op jit(solution)/shard_map/ppermute | solution.py:386
  39.3 12.3 %collective-permute-start.21 = (f32[2,8,14,16,128]{4,3,2,1,0:T(8,128)S(1)}, f32[2,8,14,16,128]{4,3,2,1,0:T(8,128)S(1)}, u32[]{:S(2)}, u32[]{:S(2)}) collective-permute-start(f32[2,8,14,16,128]{4,3,2,1,0:T(8,128)S(1)} %get-tuple-element.38), channel_id=1, source_target_pairs={{0,8},{8,0},{16,24},{24,16},{1,9},{9,1},{17,25},{25,17},{2,10},{10... | collective-permute-start | bytes 5505032 | tf_op jit(solution)/shard_map/ppermute | solution.py:386
  43.4 5.4 %collective-permute-start.8 = (f16[2,15,16,128]{3,2,1,0:T(8,128)(2,1)S(1)}, f16[2,15,16,128]{3,2,1,0:T(8,128)(2,1)S(1)}, u32[]{:S(2)}, u32[]{:S(2)}) collective-permute-start(f16[2,15,16,128]{3,2,1,0:T(8,128)(2,1)S(1)} %fusion.11), channel_id=1, source_target_pairs={{0,1},{1,0},{2,3},{3,2},{4,5},{5,4},{6,7},{7,6},{8,9},{9,8},{10,11... | collective-permute-start | bytes 368648 | tf_op jit(solution)/shard_map/ppermute | solution.py:386
  49.0 11.2 %collective-permute-start.9 = (f16[15,16,128]{2,1,0:T(8,128)(2,1)S(1)}, f16[15,16,128]{2,1,0:T(8,128)(2,1)S(1)}, u32[]{:S(2)}, u32[]{:S(2)}) collective-permute-start(f16[15,16,128]{2,1,0:T(8,128)(2,1)S(1)} %fusion.18), channel_id=1, source_target_pairs={{0,4},{1,5},{2,6},{3,7},{4,0},{5,1},{6,2},{7,3},{8,12},{9,13},{10,... | collective-permute-start | bytes 184328 | tf_op jit(solution)/shard_map/ppermute | solution.py:386
  52.6 10.6 %collective-permute-start.22 = (f16[2,2,2,14,16,128]{5,4,3,0,1,2:T(8,128)(2,1)S(1)}, f16[2,2,2,14,16,128]{5,4,3,0,1,2:T(8,128)(2,1)S(1)}, u32[]{:S(2)}, u32[]{:S(2)}) collective-permute-start(f16[2,2,2,14,16,128]{5,4,3,0,1,2:T(8,128)(2,1)S(1)} %fusion.2), channel_id=1, source_target_pairs={{0,16},{8,24},{16,0},{24,8},{1,17},{9,25},{17,1},{25,9},{2,18},{10... | collective-permute-start | bytes 1376264 | tf_op jit(solution)/shard_map/ppermute | solution.py:386
  54.1 53.7 %collective-permute-start.3 = (f32[8,3712]{1,0:T(8,128)S(1)}, f32[8,3712]{1,0:T(8,128)S(1)}, u32[]{:S(2)}, u32[]{:S(2)}) collective-permute-start(f32[8,3712]{1,0:T(8,128)S(1)} %get-tuple-element.47), channel_id=1, source_target_pairs={{1,0},{2,1},{3,2},{4,3},{5,4},{6,5},{7,6},{9,8},{10,9},{11,10},{12... | collective-permute-start | bytes 356360 | tf_op jit(solution)/shard_map/ppermute | solution.py:525
  55.4 53.0 %collective-permute-start.2 = (f32[8,3712]{1,0:T(8,128)S(1)}, f32[8,3712]{1,0:T(8,128)S(1)}, u32[]{:S(2)}, u32[]{:S(2)}) collective-permute-start(f32[8,3712]{1,0:T(8,128)S(1)} %get-tuple-element.46), channel_id=1, source_target_pairs={{0,1},{1,2},{2,3},{3,4},{4,5},{5,6},{6,7},{8,9},{9,10},{10,11},{11... | collective-permute-start | bytes 356360 | tf_op jit(solution)/shard_map/ppermute | solution.py:526
  63.7 8.5 %collective-permute-start.23 = (f16[2,2,14,16,128]{4,3,2,0,1:T(8,128)(2,1)S(1)}, f16[2,2,14,16,128]{4,3,2,0,1:T(8,128)(2,1)S(1)}, u32[]{:S(2)}, u32[]{:S(2)}) collective-permute-start(f16[2,2,14,16,128]{4,3,2,0,1:T(8,128)(2,1)S(1)} %fusion.7), channel_id=1, source_target_pairs={{0,1},{1,0},{2,3},{3,2},{4,5},{5,4},{6,7},{7,6},{8,9},{9,8},{10,11... | collective-permute-start | bytes 688136 | tf_op jit(solution)/shard_map/ppermute | solution.py:386
  66.7 15.2 %collective-permute-start.14 = (f16[2,2,2,19,16,128]{5,4,3,1,0,2:T(8,128)(2,1)S(1)}, f16[2,2,2,19,16,128]{5,4,3,1,0,2:T(8,128)(2,1)S(1)}, u32[]{:S(2)}, u32[]{:S(2)}) collective-permute-start(f16[2,2,2,19,16,128]{5,4,3,1,0,2:T(8,128)(2,1)S(1)} %fusion), channel_id=1, source_target_pairs={{0,1},{1,0},{2,3},{3,2},{4,5},{5,4},{6,7},{7,6},{8,9},{9,8},{10,11... | collective-permute-start | bytes 1867784 | tf_op jit(solution)/shard_map/ppermute | solution.py:386
  72.6 4.9 %collective-permute-start.24 = (f16[2,14,16,128]{3,2,1,0:T(8,128)(2,1)S(1)}, f16[2,14,16,128]{3,2,1,0:T(8,128)(2,1)S(1)}, u32[]{:S(2)}, u32[]{:S(2)}) collective-permute-start(f16[2,14,16,128]{3,2,1,0:T(8,128)(2,1)S(1)} %fusion.14), channel_id=1, source_target_pairs={{0,2},{1,3},{2,0},{3,1},{4,6},{5,7},{6,4},{7,5},{8,10},{9,11},{10,... | collective-permute-start | bytes 344072 | tf_op jit(solution)/shard_map/ppermute | solution.py:386
  73.7 38.9 %collective-permute-start.10 = (f32[15,16,128]{2,1,0:T(8,128)S(1)}, f32[15,16,128]{2,1,0:T(8,128)S(1)}, u32[]{:S(2)}, u32[]{:S(2)}) collective-permute-start(f32[15,16,128]{2,1,0:T(8,128)S(1)} %add_select_fusion.11.refs_0_), channel_id=1, source_target_pairs={{0,8},{8,0},{16,24},{24,16},{1,9},{9,1},{17,25},{25,17},{2,10},{10... | collective-permute-start | bytes 368648 | tf_op jit(solution)/shard_map/ppermute | solution.py:386
  77.4 31.0 %collective-permute-start.11 = (f32[15,16,128]{2,1,0:T(8,128)S(1)}, f32[15,16,128]{2,1,0:T(8,128)S(1)}, u32[]{:S(2)}, u32[]{:S(2)}) collective-permute-start(f32[15,16,128]{2,1,0:T(8,128)S(1)} %add_select_fusion.11.refs_0_), channel_id=1, source_target_pairs={{0,16},{8,24},{16,0},{24,8},{1,17},{9,25},{17,1},{25,9},{2,18},{10... | collective-permute-start | bytes 368648 | tf_op jit(solution)/shard_map/ppermute | solution.py:386
  82.6 7.0 %collective-permute-start.15 = (f16[2,2,19,16,128]{4,3,2,1,0:T(8,128)(2,1)S(1)}, f16[2,2,19,16,128]{4,3,2,1,0:T(8,128)(2,1)S(1)}, u32[]{:S(2)}, u32[]{:S(2)}) collective-permute-start(f16[2,2,19,16,128]{4,3,2,1,0:T(8,128)(2,1)S(1)} %fusion.3), channel_id=1, source_target_pairs={{0,2},{1,3},{2,0},{3,1},{4,6},{5,7},{6,4},{7,5},{8,10},{9,11},{10,... | collective-permute-start | bytes 933896 | tf_op jit(solution)/shard_map/ppermute | solution.py:386
  90.0 5.3 %collective-permute-start.16 = (f16[2,19,16,128]{3,2,1,0:T(8,128)(2,1)S(1)}, f16[2,19,16,128]{3,2,1,0:T(8,128)(2,1)S(1)}, u32[]{:S(2)}, u32[]{:S(2)}) collective-permute-start(f16[2,19,16,128]{3,2,1,0:T(8,128)(2,1)S(1)} %fusion.9), channel_id=1, source_target_pairs={{0,16},{8,24},{16,0},{24,8},{1,17},{9,25},{17,1},{25,9},{2,18},{10... | collective-permute-start | bytes 466952 | tf_op jit(solution)/shard_map/ppermute | solution.py:386
  95.3 5.4 %collective-permute-start.25 = (f16[14,16,128]{2,1,0:T(8,128)(2,1)S(1)}, f16[14,16,128]{2,1,0:T(8,128)(2,1)S(1)}, u32[]{:S(2)}, u32[]{:S(2)}) collective-permute-start(f16[14,16,128]{2,1,0:T(8,128)(2,1)S(1)} %fusion.21), channel_id=1, source_target_pairs={{0,4},{1,5},{2,6},{3,7},{4,0},{5,1},{6,2},{7,3},{8,12},{9,13},{10,... | collective-permute-start | bytes 172040 | tf_op jit(solution)/shard_map/ppermute | solution.py:386
  100.7 5.3 %collective-permute-start.17 = (f16[19,16,128]{2,1,0:T(8,128)(2,1)S(1)}, f16[19,16,128]{2,1,0:T(8,128)(2,1)S(1)}, u32[]{:S(2)}, u32[]{:S(2)}) collective-permute-start(f16[19,16,128]{2,1,0:T(8,128)(2,1)S(1)} %fusion.16), channel_id=1, source_target_pairs={{0,4},{1,5},{2,6},{3,7},{4,0},{5,1},{6,2},{7,3},{8,12},{9,13},{10,... | collective-permute-start | bytes 233480 | tf_op jit(solution)/shard_map/ppermute | solution.py:386
  106.1 7.0 %collective-permute-start.19 = (f32[19,16,128]{2,1,0:T(8,128)S(1)}, f32[19,16,128]{2,1,0:T(8,128)S(1)}, u32[]{:S(2)}, u32[]{:S(2)}) collective-permute-start(f32[19,16,128]{2,1,0:T(8,128)S(1)} %add_select_fusion.10.refs_4_), channel_id=1, source_target_pairs={{0,16},{8,24},{16,0},{24,8},{1,17},{9,25},{17,1},{25,9},{2,18},{10... | collective-permute-start | bytes 466952 | tf_op jit(solution)/shard_map/ppermute | solution.py:386
  107.8 4.9 %collective-permute-start.27 = (f32[14,16,128]{2,1,0:T(8,128)S(1)}, f32[14,16,128]{2,1,0:T(8,128)S(1)}, u32[]{:S(2)}, u32[]{:S(2)}) collective-permute-start(f32[14,16,128]{2,1,0:T(8,128)S(1)} %add_select_fusion.12.refs_8_), channel_id=1, source_target_pairs={{0,16},{8,24},{16,0},{24,8},{1,17},{9,25},{17,1},{25,9},{2,18},{10... | collective-permute-start | bytes 344072 | tf_op jit(solution)/shard_map/ppermute | solution.py:386
  108.4 5.5 %collective-permute-start.12 = (f32[15,16,128]{2,1,0:T(8,128)S(1)}, f32[15,16,128]{2,1,0:T(8,128)S(1)}, u32[]{:S(2)}, u32[]{:S(2)}) collective-permute-start(f32[15,16,128]{2,1,0:T(8,128)S(1)} %collective-permute-done.11.refs_2_), channel_id=1, source_target_pairs={{0,8},{8,0},{16,24},{24,16},{1,9},{9,1},{17,25},{25,17},{2,10},{10... | collective-permute-start | bytes 368648 | tf_op jit(solution)/shard_map/ppermute | solution.py:386
  108.4 5.5 %collective-permute-start.26 = (f32[14,16,128]{2,1,0:T(8,128)S(1)}, f32[14,16,128]{2,1,0:T(8,128)S(1)}, u32[]{:S(2)}, u32[]{:S(2)}) collective-permute-start(f32[14,16,128]{2,1,0:T(8,128)S(1)} %add_select_fusion.12.refs_8_), channel_id=1, source_target_pairs={{0,8},{8,0},{16,24},{24,16},{1,9},{9,1},{17,25},{25,17},{2,10},{10... | collective-permute-start | bytes 344072 | tf_op jit(solution)/shard_map/ppermute | solution.py:386
  112.7 1.3 %collective-permute-start.28 = (f32[14,16,128]{2,1,0:T(8,128)S(1)}, f32[14,16,128]{2,1,0:T(8,128)S(1)}, u32[]{:S(2)}, u32[]{:S(2)}) collective-permute-start(f32[14,16,128]{2,1,0:T(8,128)S(1)} %collective-permute-done.27.refs_10_), channel_id=1, source_target_pairs={{0,8},{8,0},{16,24},{24,16},{1,9},{9,1},{17,25},{25,17},{2,10},{10... | collective-permute-start | bytes 344072 | tf_op jit(solution)/shard_map/ppermute | solution.py:386
  112.7 1.5 %collective-permute-start.18 = (f32[19,16,128]{2,1,0:T(8,128)S(1)}, f32[19,16,128]{2,1,0:T(8,128)S(1)}, u32[]{:S(2)}, u32[]{:S(2)}) collective-permute-start(f32[19,16,128]{2,1,0:T(8,128)S(1)} %add_select_fusion.10.refs_4_), channel_id=1, source_target_pairs={{0,8},{8,0},{16,24},{24,16},{1,9},{9,1},{17,25},{25,17},{2,10},{10... | collective-permute-start | bytes 466952 | tf_op jit(solution)/shard_map/ppermute | solution.py:386
  113.2 1.4 %collective-permute-start.20 = (f32[19,16,128]{2,1,0:T(8,128)S(1)}, f32[19,16,128]{2,1,0:T(8,128)S(1)}, u32[]{:S(2)}, u32[]{:S(2)}) collective-permute-start(f32[19,16,128]{2,1,0:T(8,128)S(1)} %collective-permute-done.19.refs_6_), channel_id=1, source_target_pairs={{0,8},{8,0},{16,24},{24,16},{1,9},{9,1},{17,25},{25,17},{2,10},{10... | collective-permute-start | bytes 466952 | tf_op jit(solution)/shard_map/ppermute | solution.py:386
  (2 other events, 12.1 us)

commit v4 on v3

--- a/solution.py
+++ b/solution.py
@@ -466,11 +466,11 @@
             value = combine(jnp.where(high, high_half, low_half), decode(got, rows))
         return value
 
-    def spread(value):
-        parts = {0: value}
+    def spread(value, rows=ROWS):
+        parts = {0: encode(value, rows)}
         for bit in reversed(range(bits)):
             parts.update({m | (1 << bit): swap(v, bit) for m, v in list(parts.items())})
-        return [parts[m] for m in range(size)]
+        return [decode(parts[m], rows) for m in range(size)]
 
     keep_two, send_two = call(
         make_second(channels, t_two),
@@ -542,7 +542,7 @@
     )
     zero = halving(zero, marks[bits:], over_graph[1::-1] + over_graph[2:])
     layouts = (t_zero, t_one, t_two)
-    parts = spread(zero) + spread(one) + spread(two)
+    parts = spread(zero) + spread(one) + spread(two, rows=1)
     grads = call(
         make_output(layouts, size),
         tuple(shape((tiles.rows, tiles.cols), F32) for tiles in layouts),

time: 117 us -> 133 us (1.14)
  waiting for transfers between devices: 47.2 us -> 64.9 us
  starting transfers between devices: 38.3 us -> 36.4 us
    ppermute x25, waiting for transfers between devices: 46 us -> 63.7 us  [swap(): return lax.ppermute(value, axis, [(i, i ^ 1 << bit) for i in range(size)])]
    ppermute x25, starting transfers between devices: 25.4 us -> 23.1 us  [swap(): return lax.ppermute(value, axis, [(i, i ^ 1 << bit) for i in range(size)])]
  transfers between devices with their start and end apart: 29 -> 29, of which waited for: 16 -> 17; matrix products, arithmetic and copies ran while one was open for 8% -> 7% of each run, Pallas kernels for 6% -> 5%
where the time goes in v4:
time: 133 us
  waiting for transfers between devices  64.9 us (49%)
  starting transfers between devices  36.4 us (27%)
  Pallas kernels  19.4 us (15%)
  other arithmetic  8.29 us (6%)
  local copies, waits for them, and re-layouts  2.59 us (2%)
    ppermute x25, waiting for transfers between devices, swap(): return lax.ppermute(value, axis, [(i, i ^ 1 << bit) for i in range(size)])  63.7 us
    ppermute x25, starting transfers between devices, swap(): return lax.ppermute(value, axis, [(i, i ^ 1 << bit) for i in range(size)])  23.1 us
    pallas_call x6, Pallas kernels, call(): pl.pallas_call(body, out_shape=outs, in_specs=[smem] * scalars + [vmem] *...  19.4 us
    ppermute x1, starting transfers between devices, shards(): lax.ppermute(jnp.stack([feats[atom_count - reach:], cots[atom_count - rea...  5.53 us
    ppermute x1, starting transfers between devices, shards(): from_prev = lax.ppermute(nodes[atom_count + reach:], 'graph', up)  5.21 us
    select_n x13, other arithmetic, combine(): jnp.where(is_level(first), jnp.maximum(first, second), first + second)  2.94 us
  transfers between devices with their start and end apart: 29, of which 17 were waited for; matrix products, arithmetic and copies ran while one was open for 7% of the time, Pallas kernels for 5%

profile of v4, /device:TPU:0, one launch (start us, length us, event | category | flops | bytes accessed | tf_op | source)
XLA Modules:
  0.0 132.9 jit_solution(14273214511268648476)
XLA Ops:
  1.6 1.3 collective-permute-start.1
  3.0 5.5 %collective-permute-start = (bf16[2,8,3712]{2,1,0:T(8,128)(2,1)S(1)}, bf16[2,8,3712]{2,1,0:T(8,128)(2,1)S(1)}, u32[]{:S(2)}, u32[]{:S(2)}) collective-permute-start(bf16[2,8,3712]{2,1,0:T(8,128)(2,1)S(1)} %pad_maximum_fusion.1), channel_id=1, source_target_pairs={{0,1},{1,2},{2,3},{3,4},{4,5},{5,6},{6,7},{8,9},{9,10},{10,11},{11... | collective-permute-start | bytes 356360 | tf_op jit(solution)/shard_map/ppermute | solution.py:407
  12.6 5.8 %shard_map.111 = (bf16[640,768]{1,0:T(8,128)(2,1)S(1)}, bf16[320,1536]{1,0:T(8,128)(2,1)S(1)}, bf16[640,640]{1,0:T(8,128)(2,1)S(1)}, bf16[320,1280]{1,0:T(8,128)...) custom-call(s32[2]{0:T(128)S(1)} %pad_add_fusion.me, ...), custom_call_target="tpu_custom_call" | custom-call | flops 3000000000 | bytes 4194304 | tf_op jit(solution)/shard_map/pallas_call | solution.py:373
  18.4 4.6 %shard_map.112.sums.refs_0_ = bf16[4,32,896]{2,1,0:T(8,128)(2,1)S(1)} custom-call(bf16[32,896]{1,0:T(8,128)(2,1)S(1)} %get-tuple-element.23.feat, f32[320,8]{1,0:T(8,128)S(1)} %copy.14.cols, f32[8,320]{1,0:T(8,128)S(1)} %stack.39.rows, bf16[640,768]{1,0:T(8,128)(2,1)S(1)} %get-tuple-element.24.x1, bf16[640,640]{1,0:T(8,128)(2,1)S(1)} %get-tuple-element.25.x2, ...), custom_call_target="tpu_custom_call" | custom-call | flops 4000000000 | bytes 4194304 | tf_op jit(solution)/shard_map/pallas_call | solution.py:373
  23.2 1.6 %collective-permute-start.5 = (bf16[4,32,896]{2,1,0:T(8,128)(2,1)S(1)}, bf16[4,32,896]{2,1,0:T(8,128)(2,1)S(1)}, u32[]{:S(2)}, u32[]{:S(2)}) collective-permute-start(bf16[4,32,896]{2,1,0:T(8,128)(2,1)S(1)} %shard_map.112.sums.refs_0_), channel_id=1, source_target_pairs={{0,16},{8,24},{16,0},{24,8},{1,17},{9,25},{17,1},{25,9},{2,18},{10... | collective-permute-start | bytes 688136 | tf_op jit(solution)/shard_map/ppermute | solution.py:386
  24.7 2.2 %shard_map.113 = f32[32,3712]{1,0:T(8,128)S(1)} custom-call(bf16[4,32,896]{2,1,0:T(8,128)(2,1)S(1)} %shard_map.112.sums.refs_0_, f32[8,320]{1,0:T(8,128)S(1)} %stack.39.rows, bf16[320,1536]{1,0:T(8,128)(2,1)S(1)} %get-tuple-element.28.d1, bf16[320,1280]{1,0:T(8,128)(2,1)S(1)} %get-tuple-element.29.d2, bf16[896,896]{1,0:T(8,128)(2,1)S(1)} %copy-done.1, ...), custom_call_target="tpu_custom_call" | custom-call | flops 2000000000 | bytes 4194304 | tf_op jit(solution)/shard_map/pallas_call | solution.py:373
  27.0 1.3 collective-permute-start.3
  28.3 5.2 %collective-permute-start.2 = (f32[8,3712]{1,0:T(8,128)S(1)}, f32[8,3712]{1,0:T(8,128)S(1)}, u32[]{:S(2)}, u32[]{:S(2)}) collective-permute-start(f32[8,3712]{1,0:T(8,128)S(1)} %get-tuple-element.48), channel_id=1, source_target_pairs={{0,1},{1,2},{2,3},{3,4},{4,5},{5,6},{6,7},{8,9},{9,10},{10,11},{11... | collective-permute-start | bytes 356360 | tf_op jit(solution)/shard_map/ppermute | solution.py:526
  35.1 2.4 %shard_map.114 = f32[8,15,16,128]{3,2,1,0:T(8,128)S(1)} custom-call(s32[2]{0:T(128)S(1)} %pad_add_fusion.me, bf16[4,32,896]{2,1,0:T(8,128)(2,1)S(1)} %shard_map.112.sums.refs_0_, bf16[4,32,896]{2,1,0:T(8,128)(2,1)S(1)} %collective-permute-done.4.refs_1_, bf16[4,32,896]{2,1,0:T(8,128)(2,1)S(1)} %collective-permute-done.5.refs_2_, ...), custom_call_target="tpu_custom_call" | custom-call | flops 1000000000 | bytes 4194304 | tf_op jit(solution)/shard_map/pallas_call | solution.py:373
  37.7 2.8 %collective-permute-start.7 = (f16[2,2,15,16,128]{4,3,2,0,1:T(8,128)(2,1)S(1)}, f16[2,2,15,16,128]{4,3,2,0,1:T(8,128)(2,1)S(1)}, u32[]{:S(2)}, u32[]{:S(2)}) collective-permute-start(f16[2,2,15,16,128]{4,3,2,0,1:T(8,128)(2,1)S(1)} %fusion.5), channel_id=1, source_target_pairs={{0,2},{1,3},{2,0},{3,1},{4,6},{5,7},{6,4},{7,5},{8,10},{9,11},{10,... | collective-permute-start | bytes 737288 | tf_op jit(solution)/shard_map/ppermute | solution.py:386
  40.5 2.6 %shard_map.115 = (f32[2,8,14,16,128]{4,3,2,1,0:T(8,128)S(1)}, f32[2,8,14,16,128]{4,3,2,1,0:T(8,128)S(1)}) custom-call(s32[2]{0:T(128)S(1)} %pad_add_fusion.me, bf16[640,640]{1,0:T(8,128)(2,1)S(1)} %get-tuple-element.25.x2, bf16[320,1280]{1,0:T(8,128)(2,1)S(1)} %get-tuple-element.29.d2, f32[8,128]{1,0:T(8,128)S(1)} %get-tuple-element.36.level_in), custom_call_target="tpu_custom_call" | custom-call | flops 1200000000 | bytes 4194304 | tf_op jit(solution)/shard_map/pallas_call | solution.py:373
  43.2 3.5 %collective-permute-done.7 = f16[2,2,15,16,128]{4,3,2,0,1:T(8,128)(2,1)S(1)} collective-permute-done((f16[2,2,15,16,128]{4,3,2,0,1:T(8,128)(2,1)S(1)}, f16[2,2,15,16,128]{4,3,2,0,1:T(8,128)(2,1)S(1)}, u32[]{:S(2)}, u32[]{:S(2)}) %collective-permute-start.7) | collective-permute-done | bytes 245792 | tf_op jit(solution)/shard_map/ppermute | solution.py:386
  47.2 2.0 %collective-permute-start.8 = (f16[2,15,16,128]{3,2,1,0:T(8,128)(2,1)S(1)}, f16[2,15,16,128]{3,2,1,0:T(8,128)(2,1)S(1)}, u32[]{:S(2)}, u32[]{:S(2)}) collective-permute-start(f16[2,15,16,128]{3,2,1,0:T(8,128)(2,1)S(1)} %fusion.11), channel_id=1, source_target_pairs={{0,1},{1,0},{2,3},{3,2},{4,5},{5,4},{6,7},{7,6},{8,9},{9,8},{10,11... | collective-permute-start | bytes 368648 | tf_op jit(solution)/shard_map/ppermute | solution.py:386
  49.1 3.0 %collective-permute-done.8 = f16[2,15,16,128]{3,2,1,0:T(8,128)(2,1)S(1)} collective-permute-done((f16[2,15,16,128]{3,2,1,0:T(8,128)(2,1)S(1)}, f16[2,15,16,128]{3,2,1,0:T(8,128)(2,1)S(1)}, u32[]{:S(2)}, u32[]{:S(2)}) %collective-permute-start.8) | collective-permute-done | bytes 122912 | tf_op jit(solution)/shard_map/ppermute | solution.py:386
  52.4 2.8 %collective-permute-start.9 = (f16[15,16,128]{2,1,0:T(8,128)(2,1)S(1)}, f16[15,16,128]{2,1,0:T(8,128)(2,1)S(1)}, u32[]{:S(2)}, u32[]{:S(2)}) collective-permute-start(f16[15,16,128]{2,1,0:T(8,128)(2,1)S(1)} %fusion.19), channel_id=1, source_target_pairs={{0,4},{1,5},{2,6},{3,7},{4,0},{5,1},{6,2},{7,3},{8,12},{9,13},{10,... | collective-permute-start | bytes 184328 | tf_op jit(solution)/shard_map/ppermute | solution.py:386
  55.9 1.7 %collective-permute-done.9 = f16[15,16,128]{2,1,0:T(8,128)(2,1)S(1)} collective-permute-done((f16[15,16,128]{2,1,0:T(8,128)(2,1)S(1)}, f16[15,16,128]{2,1,0:T(8,128)(2,1)S(1)}, u32[]{:S(2)}, u32[]{:S(2)}) %collective-permute-start.9) | collective-permute-done | bytes 61472 | tf_op jit(solution)/shard_map/ppermute | solution.py:386
  58.4 3.7 %collective-permute-done.11 = f16[15,16,128]{2,1,0:T(8,128)(2,1)S(1)} collective-permute-done((f16[15,16,128]{2,1,0:T(8,128)(2,1)S(1)}, f16[15,16,128]{2,1,0:T(8,128)(2,1)S(1)}, u32[]{:S(2)}, u32[]{:S(2)}) %collective-permute-start.11) | collective-permute-done | bytes 61472 | tf_op jit(solution)/shard_map/ppermute | solution.py:386
  63.7 12.3 %collective-permute-done.22 = f16[2,2,2,14,16,128]{5,4,3,0,1,2:T(8,128)(2,1)S(1)} collective-permute-done((f16[2,2,2,14,16,128]{5,4,3,0,1,2:T(8,128)(2,1)S(1)}, f16[2,2,2,14,16,128]{5,4,3,0,1,2:T(8,128)(2,1)S(1)}, u32[]{:S(2)}, u32[]{:S(2)}) %collective-permute-start.22) | collective-permute-done | bytes 458784 | tf_op jit(solution)/shard_map/ppermute | solution.py:386
  76.5 2.0 %collective-permute-start.23 = (f16[2,2,14,16,128]{4,3,2,0,1:T(8,128)(2,1)S(1)}, f16[2,2,14,16,128]{4,3,2,0,1:T(8,128)(2,1)S(1)}, u32[]{:S(2)}, u32[]{:S(2)}) collective-permute-start(f16[2,2,14,16,128]{4,3,2,0,1:T(8,128)(2,1)S(1)} %fusion.7), channel_id=1, source_target_pairs={{0,1},{1,0},{2,3},{3,2},{4,5},{5,4},{6,7},{7,6},{8,9},{9,8},{10,11... | collective-permute-start | bytes 688136 | tf_op jit(solution)/shard_map/ppermute | solution.py:386
  79.4 4.5 %collective-permute-done.23 = f16[2,2,14,16,128]{4,3,2,0,1:T(8,128)(2,1)S(1)} collective-permute-done((f16[2,2,14,16,128]{4,3,2,0,1:T(8,128)(2,1)S(1)}, f16[2,2,14,16,128]{4,3,2,0,1:T(8,128)(2,1)S(1)}, u32[]{:S(2)}, u32[]{:S(2)}) %collective-permute-start.23) | collective-permute-done | bytes 229408 | tf_op jit(solution)/shard_map/ppermute | solution.py:386
  84.3 1.6 %collective-permute-start.24 = (f16[2,14,16,128]{3,2,1,0:T(8,128)(2,1)S(1)}, f16[2,14,16,128]{3,2,1,0:T(8,128)(2,1)S(1)}, u32[]{:S(2)}, u32[]{:S(2)}) collective-permute-start(f16[2,14,16,128]{3,2,1,0:T(8,128)(2,1)S(1)} %fusion.14), channel_id=1, source_target_pairs={{0,2},{1,3},{2,0},{3,1},{4,6},{5,7},{6,4},{7,5},{8,10},{9,11},{10,... | collective-permute-start | bytes 344072 | tf_op jit(solution)/shard_map/ppermute | solution.py:386
  85.9 3.2 %collective-permute-done.24 = f16[2,14,16,128]{3,2,1,0:T(8,128)(2,1)S(1)} collective-permute-done((f16[2,14,16,128]{3,2,1,0:T(8,128)(2,1)S(1)}, f16[2,14,16,128]{3,2,1,0:T(8,128)(2,1)S(1)}, u32[]{:S(2)}, u32[]{:S(2)}) %collective-permute-start.24) | collective-permute-done | bytes 114720 | tf_op jit(solution)/shard_map/ppermute | solution.py:386
  89.4 2.7 %collective-permute-start.25 = (f16[14,16,128]{2,1,0:T(8,128)(2,1)S(1)}, f16[14,16,128]{2,1,0:T(8,128)(2,1)S(1)}, u32[]{:S(2)}, u32[]{:S(2)}) collective-permute-start(f16[14,16,128]{2,1,0:T(8,128)(2,1)S(1)} %fusion.23), channel_id=1, source_target_pairs={{0,4},{1,5},{2,6},{3,7},{4,0},{5,1},{6,2},{7,3},{8,12},{9,13},{10,... | collective-permute-start | bytes 172040 | tf_op jit(solution)/shard_map/ppermute | solution.py:386
  92.3 1.7 %collective-permute-start.14 = (f16[2,2,2,19,16,128]{5,4,3,0,1,2:T(8,128)(2,1)S(1)}, f16[2,2,2,19,16,128]{5,4,3,0,1,2:T(8,128)(2,1)S(1)}, u32[]{:S(2)}, u32[]{:S(2)}) collective-permute-start(f16[2,2,2,19,16,128]{5,4,3,0,1,2:T(8,128)(2,1)S(1)} %fusion), channel_id=1, source_target_pairs={{0,1},{1,0},{2,3},{3,2},{4,5},{5,4},{6,7},{7,6},{8,9},{9,8},{10,11... | collective-permute-start | bytes 1867784 | tf_op jit(solution)/shard_map/ppermute | solution.py:386
  95.3 3.6 %collective-permute-done.27 = f16[14,16,128]{2,1,0:T(8,128)(2,1)S(1)} collective-permute-done((f16[14,16,128]{2,1,0:T(8,128)(2,1)S(1)}, f16[14,16,128]{2,1,0:T(8,128)(2,1)S(1)}, u32[]{:S(2)}, u32[]{:S(2)}) %collective-permute-start.27) | collective-permute-done | bytes 57376 | tf_op jit(solution)/shard_map/ppermute | solution.py:386
  99.0 7.0 %collective-permute-done.14 = f16[2,2,2,19,16,128]{5,4,3,0,1,2:T(8,128)(2,1)S(1)} collective-permute-done((f16[2,2,2,19,16,128]{5,4,3,0,1,2:T(8,128)(2,1)S(1)}, f16[2,2,2,19,16,128]{5,4,3,0,1,2:T(8,128)(2,1)S(1)}, u32[]{:S(2)}, u32[]{:S(2)}) %collective-permute-start.14) | collective-permute-done | bytes 622624 | tf_op jit(solution)/shard_map/ppermute | solution.py:386
  106.7 1.8 %collective-permute-start.15 = (f16[2,2,19,16,128]{4,3,2,0,1:T(8,128)(2,1)S(1)}, f16[2,2,19,16,128]{4,3,2,0,1:T(8,128)(2,1)S(1)}, u32[]{:S(2)}, u32[]{:S(2)}) collective-permute-start(f16[2,2,19,16,128]{4,3,2,0,1:T(8,128)(2,1)S(1)} %fusion.3), channel_id=1, source_target_pairs={{0,2},{1,3},{2,0},{3,1},{4,6},{5,7},{6,4},{7,5},{8,10},{9,11},{10,... | collective-permute-start | bytes 933896 | tf_op jit(solution)/shard_map/ppermute | solution.py:386
  108.5 5.1 %collective-permute-done.15 = f16[2,2,19,16,128]{4,3,2,0,1:T(8,128)(2,1)S(1)} collective-permute-done((f16[2,2,19,16,128]{4,3,2,0,1:T(8,128)(2,1)S(1)}, f16[2,2,19,16,128]{4,3,2,0,1:T(8,128)(2,1)S(1)}, u32[]{:S(2)}, u32[]{:S(2)}) %collective-permute-start.15) | collective-permute-done | bytes 311328 | tf_op jit(solution)/shard_map/ppermute | solution.py:386
  114.7 4.7 %collective-permute-done.16 = f16[2,19,16,128]{3,2,1,0:T(8,128)(2,1)S(1)} collective-permute-done((f16[2,19,16,128]{3,2,1,0:T(8,128)(2,1)S(1)}, f16[2,19,16,128]{3,2,1,0:T(8,128)(2,1)S(1)}, u32[]{:S(2)}, u32[]{:S(2)}) %collective-permute-start.16) | collective-permute-done | bytes 155680 | tf_op jit(solution)/shard_map/ppermute | solution.py:386
  120.2 4.9 %collective-permute-done.17 = f16[19,16,128]{2,1,0:T(8,128)(2,1)S(1)} collective-permute-done((f16[19,16,128]{2,1,0:T(8,128)(2,1)S(1)}, f16[19,16,128]{2,1,0:T(8,128)(2,1)S(1)}, u32[]{:S(2)}, u32[]{:S(2)}) %collective-permute-start.17) | collective-permute-done | bytes 77856 | tf_op jit(solution)/shard_map/ppermute | solution.py:386
  125.9 3.9 %collective-permute-done.19 = f16[19,16,128]{2,1,0:T(8,128)(2,1)S(1)} collective-permute-done((f16[19,16,128]{2,1,0:T(8,128)(2,1)S(1)}, f16[19,16,128]{2,1,0:T(8,128)(2,1)S(1)}, u32[]{:S(2)}, u32[]{:S(2)}) %collective-permute-start.19) | collective-permute-done | bytes 77856 | tf_op jit(solution)/shard_map/ppermute | solution.py:386
  131.2 1.7 %shard_map.116 = (f32[112,896]{1,0:T(8,128)}, f32[96,1536]{1,0:T(8,128)}, f32[80,1280]{1,0:T(8,128)}) custom-call(s32[2]{0:T(128)S(1)} %pad_add_fusion.me, f32[15,16,128]{2,1,0:T(8,128)S(1)} %get-tuple-element.67.refs_0_, f32[15,16,128]{2,1,0:T(8,128)S(1)} %get-tuple-element.68.refs_1_, f32[15,16,128]{2,1,0:T(8,128)S(1)} %get-tuple-element.69.refs_2_, ...), custom_call_target="tpu_custom_call" | custom-call | flops 50000000 | bytes 4194304 | tf_op jit(solution)/shard_map/pallas_call | solution.py:373
  (142 shorter events, 18.8 us)
Async XLA Ops:
  0.6 11.8 %copy-start.3 = (bf16[1,16,3712]{2,1,0:T(8,128)(2,1)S(1)}, bf16[1,16,3712]{2,1,0:T(8,128)(2,1)}, u32[]{:S(2)}) copy-start(bf16[1,16,3712]{2,1,0:T(8,128)(2,1)} %param.8) | copy-start | bytes 356356
  0.6 11.8 %copy-start.4 = (bf16[1,16,3712]{2,1,0:T(8,128)(2,1)S(1)}, bf16[1,16,3712]{2,1,0:T(8,128)(2,1)}, u32[]{:S(2)}) copy-start(bf16[1,16,3712]{2,1,0:T(8,128)(2,1)} %param.9) | copy-start | bytes 356356
  1.6 9.6 %collective-permute-start.1 = (bf16[2,8,3712]{2,1,0:T(8,128)(2,1)S(1)}, bf16[2,8,3712]{2,1,0:T(8,128)(2,1)S(1)}, u32[]{:S(2)}, u32[]{:S(2)}) collective-permute-start(bf16[2,8,3712]{2,1,0:T(8,128)(2,1)S(1)} %pad_maximum_fusion.2), channel_id=1, source_target_pairs={{1,0},{2,1},{3,2},{4,3},{5,4},{6,5},{7,6},{9,8},{10,9},{11,10},{12... | collective-permute-start | bytes 356360 | tf_op jit(solution)/shard_map/ppermute | solution.py:410
  3.0 9.5 %collective-permute-start = (bf16[2,8,3712]{2,1,0:T(8,128)(2,1)S(1)}, bf16[2,8,3712]{2,1,0:T(8,128)(2,1)S(1)}, u32[]{:S(2)}, u32[]{:S(2)}) collective-permute-start(bf16[2,8,3712]{2,1,0:T(8,128)(2,1)S(1)} %pad_maximum_fusion.1), channel_id=1, source_target_pairs={{0,1},{1,2},{2,3},{3,4},{4,5},{5,6},{6,7},{8,9},{9,10},{10,11},{11... | collective-permute-start | bytes 356360 | tf_op jit(solution)/shard_map/ppermute | solution.py:407
  12.5 5.9 %copy-start = (bf16[768,1536]{1,0:T(8,128)(2,1)S(1)}, bf16[768,1536]{1,0:T(8,128)(2,1)}, u32[]{:S(2)}) copy-start(bf16[768,1536]{1,0:T(8,128)(2,1)} %wo.3) | copy-start | bytes 7077892
  23.1 11.0 %collective-permute-start.4 = (bf16[4,32,896]{2,1,0:T(8,128)(2,1)S(1)}, bf16[4,32,896]{2,1,0:T(8,128)(2,1)S(1)}, u32[]{:S(2)}, u32[]{:S(2)}) collective-permute-start(bf16[4,32,896]{2,1,0:T(8,128)(2,1)S(1)} %shard_map.112.sums.refs_0_), channel_id=1, source_target_pairs={{0,8},{8,0},{16,24},{24,16},{1,9},{9,1},{17,25},{25,17},{2,10},{10... | collective-permute-start | bytes 688136 | tf_op jit(solution)/shard_map/ppermute | solution.py:386
  23.2 10.3 %collective-permute-start.5 = (bf16[4,32,896]{2,1,0:T(8,128)(2,1)S(1)}, bf16[4,32,896]{2,1,0:T(8,128)(2,1)S(1)}, u32[]{:S(2)}, u32[]{:S(2)}) collective-permute-start(bf16[4,32,896]{2,1,0:T(8,128)(2,1)S(1)} %shard_map.112.sums.refs_0_), channel_id=1, source_target_pairs={{0,16},{8,24},{16,0},{24,8},{1,17},{9,25},{17,1},{25,9},{2,18},{10... | collective-permute-start | bytes 688136 | tf_op jit(solution)/shard_map/ppermute | solution.py:386
  27.0 28.2 %collective-permute-start.3 = (f32[8,3712]{1,0:T(8,128)S(1)}, f32[8,3712]{1,0:T(8,128)S(1)}, u32[]{:S(2)}, u32[]{:S(2)}) collective-permute-start(f32[8,3712]{1,0:T(8,128)S(1)} %get-tuple-element.49), channel_id=1, source_target_pairs={{1,0},{2,1},{3,2},{4,3},{5,4},{6,5},{7,6},{9,8},{10,9},{11,10},{12... | collective-permute-start | bytes 356360 | tf_op jit(solution)/shard_map/ppermute | solution.py:525
  28.3 26.9 %collective-permute-start.2 = (f32[8,3712]{1,0:T(8,128)S(1)}, f32[8,3712]{1,0:T(8,128)S(1)}, u32[]{:S(2)}, u32[]{:S(2)}) collective-permute-start(f32[8,3712]{1,0:T(8,128)S(1)} %get-tuple-element.48), channel_id=1, source_target_pairs={{0,1},{1,2},{2,3},{3,4},{4,5},{5,6},{6,7},{8,9},{9,10},{10,11},{11... | collective-permute-start | bytes 356360 | tf_op jit(solution)/shard_map/ppermute | solution.py:526
  33.5 1.6 %collective-permute-start.6 = (bf16[4,32,896]{2,1,0:T(8,128)(2,1)S(1)}, bf16[4,32,896]{2,1,0:T(8,128)(2,1)S(1)}, u32[]{:S(2)}, u32[]{:S(2)}) collective-permute-start(bf16[4,32,896]{2,1,0:T(8,128)(2,1)S(1)} %collective-permute-done.5.refs_2_), channel_id=1, source_target_pairs={{0,8},{8,0},{16,24},{24,16},{1,9},{9,1},{17,25},{25,17},{2,10},{10... | collective-permute-start | bytes 688136 | tf_op jit(solution)/shard_map/ppermute | solution.py:386
  33.6 44.9 %collective-permute-start.13 = (f32[2,8,19,16,128]{4,3,2,1,0:T(8,128)S(1)}, f32[2,8,19,16,128]{4,3,2,1,0:T(8,128)S(1)}, u32[]{:S(2)}, u32[]{:S(2)}) collective-permute-start(f32[2,8,19,16,128]{4,3,2,1,0:T(8,128)S(1)} %get-tuple-element.35), channel_id=1, source_target_pairs={{0,8},{8,0},{16,24},{24,16},{1,9},{9,1},{17,25},{25,17},{2,10},{10... | collective-permute-start | bytes 7471112 | tf_op jit(solution)/shard_map/ppermute | solution.py:386
  37.7 9.1 %collective-permute-start.7 = (f16[2,2,15,16,128]{4,3,2,0,1:T(8,128)(2,1)S(1)}, f16[2,2,15,16,128]{4,3,2,0,1:T(8,128)(2,1)S(1)}, u32[]{:S(2)}, u32[]{:S(2)}) collective-permute-start(f16[2,2,15,16,128]{4,3,2,0,1:T(8,128)(2,1)S(1)} %fusion.5), channel_id=1, source_target_pairs={{0,2},{1,3},{2,0},{3,1},{4,6},{5,7},{6,4},{7,5},{8,10},{9,11},{10,... | collective-permute-start | bytes 737288 | tf_op jit(solution)/shard_map/ppermute | solution.py:386
  43.2 18.9 %collective-permute-start.21 = (f32[2,8,14,16,128]{4,3,2,1,0:T(8,128)S(1)}, f32[2,8,14,16,128]{4,3,2,1,0:T(8,128)S(1)}, u32[]{:S(2)}, u32[]{:S(2)}) collective-permute-start(f32[2,8,14,16,128]{4,3,2,1,0:T(8,128)S(1)} %get-tuple-element.38), channel_id=1, source_target_pairs={{0,8},{8,0},{16,24},{24,16},{1,9},{9,1},{17,25},{25,17},{2,10},{10... | collective-permute-start | bytes 5505032 | tf_op jit(solution)/shard_map/ppermute | solution.py:386
  47.2 4.9 %collective-permute-start.8 = (f16[2,15,16,128]{3,2,1,0:T(8,128)(2,1)S(1)}, f16[2,15,16,128]{3,2,1,0:T(8,128)(2,1)S(1)}, u32[]{:S(2)}, u32[]{:S(2)}) collective-permute-start(f16[2,15,16,128]{3,2,1,0:T(8,128)(2,1)S(1)} %fusion.11), channel_id=1, source_target_pairs={{0,1},{1,0},{2,3},{3,2},{4,5},{5,4},{6,7},{7,6},{8,9},{9,8},{10,11... | collective-permute-start | bytes 368648 | tf_op jit(solution)/shard_map/ppermute | solution.py:386
  52.4 5.2 %collective-permute-start.9 = (f16[15,16,128]{2,1,0:T(8,128)(2,1)S(1)}, f16[15,16,128]{2,1,0:T(8,128)(2,1)S(1)}, u32[]{:S(2)}, u32[]{:S(2)}) collective-permute-start(f16[15,16,128]{2,1,0:T(8,128)(2,1)S(1)} %fusion.19), channel_id=1, source_target_pairs={{0,4},{1,5},{2,6},{3,7},{4,0},{5,1},{6,2},{7,3},{8,12},{9,13},{10,... | collective-permute-start | bytes 184328 | tf_op jit(solution)/shard_map/ppermute | solution.py:386
  57.8 4.3 %collective-permute-start.11 = (f16[15,16,128]{2,1,0:T(8,128)(2,1)S(1)}, f16[15,16,128]{2,1,0:T(8,128)(2,1)S(1)}, u32[]{:S(2)}, u32[]{:S(2)}) collective-permute-start(f16[15,16,128]{2,1,0:T(8,128)(2,1)S(1)} %fusion.20), channel_id=1, source_target_pairs={{0,16},{8,24},{16,0},{24,8},{1,17},{9,25},{17,1},{25,9},{2,18},{10... | collective-permute-start | bytes 184328 | tf_op jit(solution)/shard_map/ppermute | solution.py:386
  58.4 3.7 %collective-permute-start.10 = (f16[15,16,128]{2,1,0:T(8,128)(2,1)S(1)}, f16[15,16,128]{2,1,0:T(8,128)(2,1)S(1)}, u32[]{:S(2)}, u32[]{:S(2)}) collective-permute-start(f16[15,16,128]{2,1,0:T(8,128)(2,1)S(1)} %fusion.20), channel_id=1, source_target_pairs={{0,8},{8,0},{16,24},{24,16},{1,9},{9,1},{17,25},{25,17},{2,10},{10... | collective-permute-start | bytes 184328 | tf_op jit(solution)/shard_map/ppermute | solution.py:386
  62.1 1.6 %collective-permute-start.12 = (f16[15,16,128]{2,1,0:T(8,128)(2,1)S(1)}, f16[15,16,128]{2,1,0:T(8,128)(2,1)S(1)}, u32[]{:S(2)}, u32[]{:S(2)}) collective-permute-start(f16[15,16,128]{2,1,0:T(8,128)(2,1)S(1)} %collective-permute-done.11), channel_id=1, source_target_pairs={{0,8},{8,0},{16,24},{24,16},{1,9},{9,1},{17,25},{25,17},{2,10},{10... | collective-permute-start | bytes 184328 | tf_op jit(solution)/shard_map/ppermute | solution.py:386
  63.0 13.0 %collective-permute-start.22 = (f16[2,2,2,14,16,128]{5,4,3,0,1,2:T(8,128)(2,1)S(1)}, f16[2,2,2,14,16,128]{5,4,3,0,1,2:T(8,128)(2,1)S(1)}, u32[]{:S(2)}, u32[]{:S(2)}) collective-permute-start(f16[2,2,2,14,16,128]{5,4,3,0,1,2:T(8,128)(2,1)S(1)} %fusion.2), channel_id=1, source_target_pairs={{0,16},{8,24},{16,0},{24,8},{1,17},{9,25},{17,1},{25,9},{2,18},{10... | collective-permute-start | bytes 1376264 | tf_op jit(solution)/shard_map/ppermute | solution.py:386
  76.5 7.4 %collective-permute-start.23 = (f16[2,2,14,16,128]{4,3,2,0,1:T(8,128)(2,1)S(1)}, f16[2,2,14,16,128]{4,3,2,0,1:T(8,128)(2,1)S(1)}, u32[]{:S(2)}, u32[]{:S(2)}) collective-permute-start(f16[2,2,14,16,128]{4,3,2,0,1:T(8,128)(2,1)S(1)} %fusion.7), channel_id=1, source_target_pairs={{0,1},{1,0},{2,3},{3,2},{4,5},{5,4},{6,7},{7,6},{8,9},{9,8},{10,11... | collective-permute-start | bytes 688136 | tf_op jit(solution)/shard_map/ppermute | solution.py:386
  84.3 4.9 %collective-permute-start.24 = (f16[2,14,16,128]{3,2,1,0:T(8,128)(2,1)S(1)}, f16[2,14,16,128]{3,2,1,0:T(8,128)(2,1)S(1)}, u32[]{:S(2)}, u32[]{:S(2)}) collective-permute-start(f16[2,14,16,128]{3,2,1,0:T(8,128)(2,1)S(1)} %fusion.14), channel_id=1, source_target_pairs={{0,2},{1,3},{2,0},{3,1},{4,6},{5,7},{6,4},{7,5},{8,10},{9,11},{10,... | collective-permute-start | bytes 344072 | tf_op jit(solution)/shard_map/ppermute | solution.py:386
  89.4 5.1 %collective-permute-start.25 = (f16[14,16,128]{2,1,0:T(8,128)(2,1)S(1)}, f16[14,16,128]{2,1,0:T(8,128)(2,1)S(1)}, u32[]{:S(2)}, u32[]{:S(2)}) collective-permute-start(f16[14,16,128]{2,1,0:T(8,128)(2,1)S(1)} %fusion.23), channel_id=1, source_target_pairs={{0,4},{1,5},{2,6},{3,7},{4,0},{5,1},{6,2},{7,3},{8,12},{9,13},{10,... | collective-permute-start | bytes 172040 | tf_op jit(solution)/shard_map/ppermute | solution.py:386
  92.3 13.6 %collective-permute-start.14 = (f16[2,2,2,19,16,128]{5,4,3,0,1,2:T(8,128)(2,1)S(1)}, f16[2,2,2,19,16,128]{5,4,3,0,1,2:T(8,128)(2,1)S(1)}, u32[]{:S(2)}, u32[]{:S(2)}) collective-permute-start(f16[2,2,2,19,16,128]{5,4,3,0,1,2:T(8,128)(2,1)S(1)} %fusion), channel_id=1, source_target_pairs={{0,1},{1,0},{2,3},{3,2},{4,5},{5,4},{6,7},{7,6},{8,9},{9,8},{10,11... | collective-permute-start | bytes 1867784 | tf_op jit(solution)/shard_map/ppermute | solution.py:386
  94.7 4.2 %collective-permute-start.27 = (f16[14,16,128]{2,1,0:T(8,128)(2,1)S(1)}, f16[14,16,128]{2,1,0:T(8,128)(2,1)S(1)}, u32[]{:S(2)}, u32[]{:S(2)}) collective-permute-start(f16[14,16,128]{2,1,0:T(8,128)(2,1)S(1)} %fusion.24), channel_id=1, source_target_pairs={{0,16},{8,24},{16,0},{24,8},{1,17},{9,25},{17,1},{25,9},{2,18},{10... | collective-permute-start | bytes 172040 | tf_op jit(solution)/shard_map/ppermute | solution.py:386
  95.3 13.2 %collective-permute-start.26 = (f16[14,16,128]{2,1,0:T(8,128)(2,1)S(1)}, f16[14,16,128]{2,1,0:T(8,128)(2,1)S(1)}, u32[]{:S(2)}, u32[]{:S(2)}) collective-permute-start(f16[14,16,128]{2,1,0:T(8,128)(2,1)S(1)} %fusion.24), channel_id=1, source_target_pairs={{0,8},{8,0},{16,24},{24,16},{1,9},{9,1},{17,25},{25,17},{2,10},{10... | collective-permute-start | bytes 172040 | tf_op jit(solution)/shard_map/ppermute | solution.py:386
  99.0 15.7 %collective-permute-start.28 = (f16[14,16,128]{2,1,0:T(8,128)(2,1)S(1)}, f16[14,16,128]{2,1,0:T(8,128)(2,1)S(1)}, u32[]{:S(2)}, u32[]{:S(2)}) collective-permute-start(f16[14,16,128]{2,1,0:T(8,128)(2,1)S(1)} %collective-permute-done.27), channel_id=1, source_target_pairs={{0,8},{8,0},{16,24},{24,16},{1,9},{9,1},{17,25},{25,17},{2,10},{10... | collective-permute-start | bytes 172040 | tf_op jit(solution)/shard_map/ppermute | solution.py:386
  106.7 7.0 %collective-permute-start.15 = (f16[2,2,19,16,128]{4,3,2,0,1:T(8,128)(2,1)S(1)}, f16[2,2,19,16,128]{4,3,2,0,1:T(8,128)(2,1)S(1)}, u32[]{:S(2)}, u32[]{:S(2)}) collective-permute-start(f16[2,2,19,16,128]{4,3,2,0,1:T(8,128)(2,1)S(1)} %fusion.3), channel_id=1, source_target_pairs={{0,2},{1,3},{2,0},{3,1},{4,6},{5,7},{6,4},{7,5},{8,10},{9,11},{10,... | collective-permute-start | bytes 933896 | tf_op jit(solution)/shard_map/ppermute | solution.py:386
  114.1 5.3 %collective-permute-start.16 = (f16[2,19,16,128]{3,2,1,0:T(8,128)(2,1)S(1)}, f16[2,19,16,128]{3,2,1,0:T(8,128)(2,1)S(1)}, u32[]{:S(2)}, u32[]{:S(2)}) collective-permute-start(f16[2,19,16,128]{3,2,1,0:T(8,128)(2,1)S(1)} %fusion.9), channel_id=1, source_target_pairs={{0,16},{8,24},{16,0},{24,8},{1,17},{9,25},{17,1},{25,9},{2,18},{10... | collective-permute-start | bytes 466952 | tf_op jit(solution)/shard_map/ppermute | solution.py:386
  119.7 5.4 %collective-permute-start.17 = (f16[19,16,128]{2,1,0:T(8,128)(2,1)S(1)}, f16[19,16,128]{2,1,0:T(8,128)(2,1)S(1)}, u32[]{:S(2)}, u32[]{:S(2)}) collective-permute-start(f16[19,16,128]{2,1,0:T(8,128)(2,1)S(1)} %fusion.16), channel_id=1, source_target_pairs={{0,4},{1,5},{2,6},{3,7},{4,0},{5,1},{6,2},{7,3},{8,12},{9,13},{10,... | collective-permute-start | bytes 233480 | tf_op jit(solution)/shard_map/ppermute | solution.py:386
  125.3 4.5 %collective-permute-start.19 = (f16[19,16,128]{2,1,0:T(8,128)(2,1)S(1)}, f16[19,16,128]{2,1,0:T(8,128)(2,1)S(1)}, u32[]{:S(2)}, u32[]{:S(2)}) collective-permute-start(f16[19,16,128]{2,1,0:T(8,128)(2,1)S(1)} %fusion.17), channel_id=1, source_target_pairs={{0,16},{8,24},{16,0},{24,8},{1,17},{9,25},{17,1},{25,9},{2,18},{10... | collective-permute-start | bytes 233480 | tf_op jit(solution)/shard_map/ppermute | solution.py:386
  125.9 3.9 %collective-permute-start.18 = (f16[19,16,128]{2,1,0:T(8,128)(2,1)S(1)}, f16[19,16,128]{2,1,0:T(8,128)(2,1)S(1)}, u32[]{:S(2)}, u32[]{:S(2)}) collective-permute-start(f16[19,16,128]{2,1,0:T(8,128)(2,1)S(1)} %fusion.17), channel_id=1, source_target_pairs={{0,8},{8,0},{16,24},{24,16},{1,9},{9,1},{17,25},{25,17},{2,10},{10... | collective-permute-start | bytes 233480 | tf_op jit(solution)/shard_map/ppermute | solution.py:386
  129.7 1.3 collective-permute-start.20
  (2 other events, 11.7 us)
